TPU v7x, 128 devices: a whole 4x4x4 slice. The times are simulated.
128 devices in a mesh: dp: 8 (over x, core), seq: 16 (over y, z).
Axes of the slice: x: 4, y: 4, z: 4, core: 2. Of those that a mesh axis runs over, the one named last changes fastest.
Arguments:
- hidden: bfloat16 [32768, 1536], P(('dp', 'seq')), may hold values from -6 to 6
- database: bfloat16 [8, 192, 128, 896], P('dp', 'seq'), may hold values from -8 to 8
- block_home: int32 [192], replicated, may hold values from 0 to 191, as said below
- neighbours: int32 [512, 2], P(('dp', 'seq')), may hold values from 0 to 191, as said below
- neighbour_counts: int32 [512], P(('dp', 'seq')), may hold values from 1 to 2
- encoder_gain: float32 [896], replicated, may hold values from 0.25 to 1.75
- encoder_projection: bfloat16 [896, 2688], replicated, may hold values from -2 to 2
- encoder_output: bfloat16 [896, 896], replicated, may hold values from -0.1875 to 0.1875
- cross_gain: float32 [1536], replicated, may hold values from 0.25 to 1.75
- cross_query: bfloat16 [1536, 1536], replicated, may hold values from -2 to 2
- cross_keyvalue: bfloat16 [3072, 896], replicated, may hold values from -2 to 2
- cross_output: bfloat16 [1536, 1536], replicated, may hold values from -0.15625 to 0.15625
- cotangent: bfloat16 [32768, 1536], P(('dp', 'seq')), may hold values from -6 to 6
Outputs:
- output: bfloat16 [32768, 1536], P(('dp', 'seq'))
- keyvalue_grad: float32 [3072, 896], P('seq')
Inputs may be any that keep to these rules, and one draw needn't show every extreme that they name: A permutation: block b lies at position block_home[b] of the second dimension of database. `neighbours`: the 8 ids of one device's spans name at most 2 blocks whose positions lie on the same device of seq, and exactly 2 on some device, on every device. Ids may repeat.
All inputs are finite; a program needn't handle non-finite values.
Results may differ from a plain program's by a relative error of at most 0.02.
Values may be sent and summed in bfloat16 or wider, within the bound.
No kernel may reach another device: no remote copies, remote signals or barrier semaphores. Data moves between devices by JAX's collectives and lax.ppermute only.
A program may use at most 128 MiB of HBM per device.

v0:
```python
import jax
import jax.numpy as jnp
from jax import lax
from jax.sharding import PartitionSpec as P

HEAD = 128
K = 2
SPAN = 64


EPSILON = 1e-06


def shifted(block, axis, distance):
    devices = range(lax.axis_size(axis))
    route = [(i - distance, i) for i in devices if i - distance in devices]
    return lax.ppermute(block, axis, route)


def sent_to_all(shard, axis):
    copies = jnp.broadcast_to(shard, (lax.axis_size(axis), *shard.shape))
    return lax.all_to_all(copies, axis, split_axis=0, concat_axis=0, tiled=True)


def over_copies(shard, axis):
    return sent_to_all(shard, axis).astype(jnp.float32).sum(axis=0)


def rms_norm(values, norm_gain):
    widened = values.astype(jnp.float32)
    return (
        widened
        * lax.rsqrt(jnp.mean(widened * widened, axis=-1, keepdims=True) + EPSILON)
        * norm_gain
    )


def encode(blocks, encoder_gain, encoder_projection, encoder_output):
    count, length, width = blocks.shape
    head_count = width // HEAD
    normed = rms_norm(blocks, encoder_gain).astype(jnp.bfloat16)
    projected = jnp.dot(
        normed.reshape(count * length, width),
        encoder_projection,
        preferred_element_type=jnp.float32,
    )
    projected = projected.astype(jnp.bfloat16).reshape(count, length, 3, head_count, HEAD)
    scores = jnp.einsum(
        "bqhd,bkhd->bhqk",
        projected[:, :, 0],
        projected[:, :, 1],
        preferred_element_type=jnp.float32,
    ) * HEAD ** (-0.5)
    weights = jax.nn.softmax(scores, axis=-1).astype(jnp.bfloat16)
    attended = jnp.einsum(
        "bhqk,bkhd->bqhd", weights, projected[:, :, 2], preferred_element_type=jnp.float32
    ).astype(jnp.bfloat16)
    mixed = jnp.dot(
        attended.reshape(count * length, width), encoder_output, preferred_element_type=jnp.float32
    )
    return (blocks.astype(jnp.float32) + mixed.reshape(count, length, width)).astype(jnp.bfloat16)


def attend(queries, keyvalue, key_mask, row_flag, grad_attended):
    groups, rows, width = queries.shape
    key_total = keyvalue.shape[1]
    head_count = width // HEAD
    score_scale = HEAD ** (-0.5)
    query_heads = queries.reshape(groups, rows, head_count, HEAD)
    key_heads = keyvalue[:, :, :width].reshape(groups, key_total, head_count, HEAD)
    value_heads = keyvalue[:, :, width:].reshape(groups, key_total, head_count, HEAD)
    grad_heads = grad_attended.reshape(groups, rows, head_count, HEAD)
    scores = (
        jnp.einsum("gqhd,gkhd->ghqk", query_heads, key_heads, preferred_element_type=jnp.float32)
        * score_scale
    )
    scores = jnp.where(key_mask[:, None, None, :], scores, -1e30)
    chances = jax.nn.softmax(scores, axis=-1) * row_flag[:, None, :, None]
    chances_low = chances.astype(jnp.bfloat16)
    attended = jnp.einsum(
        "ghqk,gkhd->gqhd", chances_low, value_heads, preferred_element_type=jnp.float32
    ).astype(jnp.bfloat16)
    grad_chances = jnp.einsum(
        "gqhd,gkhd->ghqk", grad_heads, value_heads, preferred_element_type=jnp.float32
    )
    grad_scores = (
        chances * (grad_chances - jnp.sum(chances * grad_chances, axis=-1, keepdims=True))
    ).astype(jnp.bfloat16)
    grad_keys = (
        jnp.einsum("ghqk,gqhd->gkhd", grad_scores, query_heads, preferred_element_type=jnp.float32)
        * score_scale
    )
    grad_values = jnp.einsum(
        "ghqk,gqhd->gkhd", chances_low, grad_heads, preferred_element_type=jnp.float32
    )
    grad_keyvalue = jnp.concatenate(
        [
            grad_keys.reshape(groups, key_total, width),
            grad_values.reshape(groups, key_total, width),
        ],
        axis=-1,
    ).astype(jnp.bfloat16)
    return (attended.reshape(groups, rows, width), grad_keyvalue)


def locate(block_ids, block_home):
    hits = block_ids[..., None] == jnp.arange(block_home.shape[0], dtype=jnp.int32)
    return jnp.sum(jnp.where(hits, block_home, 0), axis=-1)


def project_keys(key_rows, cross_keyvalue):
    return lax.dot_general(
        key_rows, cross_keyvalue, (((1,), (1,)), ((), ())), preferred_element_type=jnp.float32
    ).astype(jnp.bfloat16)


def local(
    hidden,
    database,
    block_home,
    neighbours,
    neighbour_counts,
    encoder_gain,
    encoder_projection,
    encoder_output,
    cross_gain,
    cross_query,
    cross_keyvalue,
    cross_output,
    cotangent,
):
    token_count, width = hidden.shape
    shard_blocks, block_length, feature = (database.shape[1], database.shape[2], database.shape[3])
    span_count = token_count // SPAN
    requests = span_count * K
    key_total = K * block_length
    seq_devices = lax.axis_size("seq")
    reader_index = lax.axis_index("seq")
    capacity = max(2, -(-requests // seq_devices))
    local_base = database[0]
    asked = lax.all_gather(neighbours, "seq", axis=0, tiled=True)
    asked_where = locate(asked, block_home).reshape(seq_devices, requests)
    asked_owner = asked_where // shard_blocks
    asked_slot = asked_where % shard_blocks
    matched = asked_owner == reader_index
    matched_rank = jnp.cumsum(matched.astype(jnp.int32), axis=1) - 1
    picked = matched[:, None, :] & (
        matched_rank[:, None, :] == jnp.arange(capacity, dtype=jnp.int32)[None, :, None]
    )
    local_index = jnp.sum(jnp.where(picked, asked_slot[:, None, :], 0), axis=-1)
    occupied = jnp.any(picked, axis=-1)
    outgoing = jnp.take(local_base, local_index.reshape(-1), axis=0).reshape(
        seq_devices, capacity, block_length, feature
    )
    outgoing = jnp.where(occupied[:, :, None, None], outgoing, jnp.zeros_like(outgoing))
    incoming = lax.all_to_all(outgoing, "seq", split_axis=0, concat_axis=0, tiled=True)
    mine_where = locate(neighbours.reshape(-1), block_home)
    mine_owner = mine_where // shard_blocks
    same_owner = mine_owner[:, None] == mine_owner[None, :]
    earlier = jnp.arange(requests)[:, None] > jnp.arange(requests)[None, :]
    mine_rank = jnp.sum((same_owner & earlier).astype(jnp.int32), axis=1)
    fetched = jnp.take(
        incoming.reshape(seq_devices * capacity, block_length, feature),
        mine_owner * capacity + mine_rank,
        axis=0,
    )
    encoded = encode(fetched, encoder_gain, encoder_projection, encoder_output)
    normed = rms_norm(hidden, cross_gain).astype(jnp.bfloat16)
    queries = jnp.dot(normed, cross_query, preferred_element_type=jnp.float32).astype(jnp.bfloat16)
    grad_attended = lax.dot_general(
        cotangent, cross_output, (((1,), (1,)), ((), ())), preferred_element_type=jnp.float32
    ).astype(jnp.bfloat16)
    local_rows = encoded.reshape(requests * block_length, feature)
    local_keyvalue = project_keys(local_rows, cross_keyvalue).reshape(
        span_count, key_total, 2 * width
    )
    local_flags = jnp.arange(K, dtype=jnp.int32)[None, :] < neighbour_counts[:, None]
    local_mask = jnp.repeat(local_flags, block_length, axis=1)
    late_queries, late_grads = shifted((queries[: SPAN - 1], grad_attended[: SPAN - 1]), "seq", -1)
    query_rows = jnp.concatenate([queries[SPAN - 1 :], late_queries], axis=0)
    grad_rows = jnp.concatenate([grad_attended[SPAN - 1 :], late_grads], axis=0)
    row_flag = jnp.ones((span_count, SPAN), jnp.float32)
    attended_groups, grad_keyvalue = attend(
        query_rows.reshape(span_count, SPAN, width),
        local_keyvalue,
        local_mask,
        row_flag,
        grad_rows.reshape(span_count, SPAN, width),
    )
    attended_rows = attended_groups.reshape(token_count, width)
    returned = shifted(attended_rows[token_count - SPAN + 1 :], "seq", 1)
    attended = jnp.concatenate([returned, attended_rows[: token_count - SPAN + 1]], axis=0)
    cross = jnp.dot(attended, cross_output, preferred_element_type=jnp.float32)
    output = (hidden.astype(jnp.float32) + cross).astype(jnp.bfloat16)
    grad_rows_all = grad_keyvalue.reshape(-1, 2 * width)
    partial_grad = lax.psum_scatter(
        lax.dot_general(
            grad_rows_all, local_rows, (((0,), (0,)), ((), ())), preferred_element_type=jnp.float32
        ).astype(jnp.bfloat16),
        "seq",
        scatter_dimension=0,
        tiled=True,
    )
    keyvalue_grad = over_copies(partial_grad, "dp").astype(jnp.float32)
    return (output, keyvalue_grad)


def solution(mesh):
    placed = (
        P(("dp", "seq"), None),
        P("dp", "seq", None, None),
        P(),
        P(("dp", "seq"), None),
        P(("dp", "seq")),
        P(),
        P(),
        P(),
        P(),
        P(),
        P(),
        P(),
        P(("dp", "seq"), None),
    )
    return jax.shard_map(
        local,
        mesh=mesh,
        in_specs=placed,
        out_specs=(P(("dp", "seq"), None), P("seq", None)),
        check_vma=False,
    )
```

profile of v0, /device:TPU:1, one launch (start us, length us, event | category | flops | bytes accessed | tf_op | source)
XLA Modules:
  0.0 384.4 jit_solution(16597211294415155366)
XLA Ops:
  7.2 20.7 %all-gather = s32[16,4,2]{1,2,0:T(2,128)S(1)} all-gather(s32[1,4,2]{1,2,0:T(2,128)} %bitcast.101), channel_id=1, replica_groups=mesh['dp'=8,'seq'=16] {'seq'}, dimensions={0}, use_global_device_ids=true | all-gather | bytes 544 | tf_op jit(solution)/shard_map/all_gather | solution.py:141
  28.0 0.9 select_reduce_fusion
  30.3 4.3 %gather_fusion = bf16[32,128,896]{2,1,0:T(8,128)(2,1)} fusion(bf16[12,128,896]{2,1,0:T(8,128)(2,1)S(1)} %bitcast.88, s32[1024]{0:T(1024)S(1)} %pad_clamp_fusion.1), kind=kCustom, calls=%fused_computation | custom fusion | bytes 14680192 | tf_op jit(solution)/shard_map/jit(_take)/gather | solution.py:152
  34.6 7.2 %select_select_fusion = bf16[16,2,128,896]{3,2,1,0:T(8,128)(2,1)} fusion(bf16[16,2,128,896]{3,2,1,0:T(8,128)(2,1)} %bitcast.89, pred[16,2]{1,0:T(8,128)(4,1)S(1)} %copy.78, pred[16,2]{1,0:T(8,128)(4,1)S(1)} %copy.76), kind=kLoop, calls=%fused_computation.4 | loop fusion | flops 7340032 | bytes 14680128 | tf_op jit(solution)/shard_map/jit(_where)/select_n | solution.py:155
  41.7 4.8 %all-to-all-start = ((bf16[16,2,128,896]{3,2,1,0:T(8,128)(2,1)}), bf16[16,2,128,896]{3,2,1,0:T(8,128)(2,1)}, u32[]{:S(2)}, u32[]{:S(2)}) async-start(bf16[16,2,128,896]{3,2,1,0:T(8,128)(2,1)} %select_select_fusion), calls=%async_computation | async-start | bytes 14680064 | tf_op jit(solution)/shard_map/all_to_all | solution.py:156
  46.9 3.9 %convolution_convert_fusion.3 = bf16[256,1536]{1,0:T(8,128)(2,1)S(1)} fusion(bf16[1536,1536]{1,0:T(8,128)(2,1)} %param.22, bf16[256,1536]{1,0:T(8,128)(2,1)S(1)} %copy-done.6, f32[1536]{0:T(1024)S(1)} %copy-done.12, f32[256]{0:T(256)S(1)} %add_rsqrt_fusion), kind=kOutput, calls=%fused_computation.32 | convolution fusion | flops 1209925632 | bytes 6298624 | tf_op jit(solution)/shard_map/dot_general | solution.py:169
  50.8 0.7 slice.53
  51.5 1.4 collective-permute-start
  53.0 1.4 convolution_convert_fusion.2
  54.4 1.3 collective-permute-start.2
  56.8 46.9 %collective-permute-done = bf16[63,1536]{1,0:T(8,128)(2,1)S(1)} collective-permute-done((bf16[63,1536]{1,0:T(8,128)(2,1)}, bf16[63,1536]{1,0:T(8,128)(2,1)S(1)}, u32[]{:S(2)}, u32[]{:S(2)}) %collective-permute-start) | collective-permute-done | bytes 193568 | tf_op jit(solution)/shard_map/ppermute | solution.py:17
  103.8 1.6 reshape_reshape.9
  105.3 25.5 %collective-permute-done.2 = bf16[63,1536]{1,0:T(8,128)(2,1)S(1)} collective-permute-done((bf16[63,1536]{1,0:T(8,128)(2,1)S(1)}, bf16[63,1536]{1,0:T(8,128)(2,1)S(1)}, u32[]{:S(2)}, u32[]{:S(2)}) %collective-permute-start.2) | collective-permute-done | bytes 193568 | tf_op jit(solution)/shard_map/ppermute | solution.py:17
  130.9 1.5 reshape_reshape.11
  132.4 3.9 %gather_fusion.1 = bf16[8,128,896]{2,1,0:T(8,128)(2,1)S(1)} fusion(bf16[32,128,896]{2,1,0:T(8,128)(2,1)} %bitcast.4, s32[1024]{0:T(1024)S(1)} %pad_clamp_fusion), kind=kCustom, calls=%fused_computation.1 | custom fusion | bytes 3670048 | tf_op jit(solution)/shard_map/jit(_take)/gather | solution.py:162
  137.4 10.8 %convolution_convert_fusion = bf16[1024,2688]{1,0:T(8,128)(2,1)} fusion(bf16[896,2688]{1,0:T(8,128)(2,1)} %param.19, bf16[1024,896]{1,0:T(8,128)(2,1)S(1)} %bitcast_select_fusion, f32[896]{0:T(1024)S(1)} %copy-done.13, f32[1024]{0:T(1024)S(1)} %rsqrt_bitcast_fusion), kind=kOutput, calls=%fused_computation.10 | convolution fusion | flops 4938924032 | bytes 12164608 | tf_op jit(solution)/shard_map/dot_general | solution.py:42
  148.2 11.7 %reshape.275 = bf16[8,128,3,7,128]{4,3,2,1,0:T(8,128)(2,1)} reshape(bf16[1024,2688]{1,0:T(8,128)(2,1)} %convolution_convert_fusion) | data formatting | bytes 11010048 | tf_op jit(solution)/shard_map/reshape | solution.py:47
  159.9 5.6 %fusion.66 = (bf16[8,128,1,7,128]{4,3,2,1,0:T(8,128)(2,1)}, bf16[8,128,1,7,128]{4,3,2,1,0:T(8,128)(2,1)}, bf16[8,128,1,7,128]{4,3,2,1,0:T(8,128)(2,1)}) fusion(bf16[8,128,3,7,128]{4,3,2,1,0:T(8,128)(2,1)} %reshape.275), kind=kLoop, calls=%fused_computation.122 | loop fusion | bytes 11010048 | tf_op jit(solution)/shard_map/slice | solution.py:56
  165.6 4.0 %copy.107 = bf16[8,128,1,7,128]{1,4,3,0,2:T(8,128)(2,1)} copy(bf16[8,128,1,7,128]{4,3,2,1,0:T(8,128)(2,1)} %get-tuple-element.8) | data formatting | bytes 3670016
  169.5 3.6 fusion.18
  173.2 3.5 fusion.67
  177.4 0.7 copy-done.10
  178.1 2.4 fusion.10
  180.5 7.2 %convolution_convert_fusion.1 = bf16[1024,3072]{1,0:T(8,128)(2,1)S(1)} fusion(bf16[1024,896]{1,0:T(8,128)(2,1)S(1)} %bitcast.108, bf16[3072,896]{1,0:T(8,128)(2,1)S(1)} %bitcast.103), kind=kOutput, calls=%fused_computation.11 | convolution fusion | flops 5640290304 | bytes 13631488 | tf_op jit(solution)/shard_map/dot_general | solution.py:112
  187.7 3.3 fusion.65
  191.0 4.8 %copy.111 = bf16[4,256,1536]{1,2,0:T(8,128)(2,1)} copy(bf16[4,256,1536]{2,1,0:T(8,128)(2,1)} %get-tuple-element.6) | data formatting | bytes 6291456
  195.7 2.5 fusion.48
  198.2 1.4 fusion.68
  199.7 1.6 copy-done.17
  201.3 1.7 convert_bitcast_fusion
  203.0 2.4 copy.97
  205.4 2.4 copy.114
  207.9 4.7 %copy.110 = bf16[4,256,1536]{1,2,0:T(8,128)(2,1)} copy(bf16[4,256,1536]{2,1,0:T(8,128)(2,1)} %get-tuple-element.7) | data formatting | bytes 6291456
  212.6 4.3 %multiply_reduce_fusion.1 = (f32[4,12,64]{2,1,0:T(8,128)S(1)}, f32[4,12,64,256]{3,2,1,0:T(8,128)S(1)}) fusion(f32[4,12,64,256]{3,2,1,0:T(8,128)} %copy-done.17, f32[4,12,64]{2,1,0:T(8,128)S(1)} %get-tuple-element.15, bf16[4,256,12,128]{1,3,2,0:T(8,128)(2,1)} %bitcast.97, bf16[4,64,12,128]{3,2,1,0:T(8,128)(2,1)S(1)} %copy-done.5), kind=kOutput, calls=%fused_computation.26 | convolution fusion | flops 203682816 | bytes 10248192 | tf_op jit(solution)/shard_map/gqhd,gkhd->ghqk/dot_general | solution.py:83
  216.9 1.9 fusion.12
  218.9 2.4 copy.95
  221.3 0.8 copy.113
  222.1 1.1 copy-done.3
  223.8 11.0 %fusion.6 = bf16[3072,896]{1,0:T(8,128)(2,1)} fusion(bf16[1024,896]{1,0:T(8,128)(2,1)S(1)} %bitcast.109, bf16[1024,1536]{0,1:T(8,128)(2,1)S(1)} %bitcast.99, bf16[1024,1536]{0,1:T(8,128)(2,1)S(1)} %bitcast.100), kind=kOutput, calls=%fused_computation.13 | convolution fusion | flops 5652480000 | bytes 13631488 | tf_op jit(solution)/shard_map/dot_general | solution.py:197
  234.8 96.1 %reduce-scatter.2.cloned.1.call-done = bf16[192,896]{1,0:T(8,128)(2,1)} async-done(((bf16[3072,896]{1,0:T(8,128)(2,1)}), bf16[192,896]{1,0:T(8,128)(2,1)}) %reduce-scatter.2.cloned.1.call-update) | async-done | bytes 344080 | tf_op jit(solution)/shard_map/reduce_scatter | solution.py:196
  331.0 2.8 broadcast_in_dim.130
  333.8 6.9 %all-to-all-start.1 = ((bf16[8,192,896]{2,1,0:T(8,128)(2,1)}), bf16[8,192,896]{2,1,0:T(8,128)(2,1)}, u32[]{:S(2)}, u32[]{:S(2)}) async-start(bf16[8,192,896]{2,1,0:T(8,128)(2,1)} %broadcast_in_dim.130), calls=%async_computation.2 | async-start | bytes 5505024 | tf_op jit(solution)/shard_map/all_to_all | solution.py:22
  340.7 4.2 %fusion.35 = bf16[4,64,12,128]{3,1,2,0:T(8,128)(2,1)S(1)} fusion(bf16[4,256,12,128]{1,3,2,0:T(8,128)(2,1)} %bitcast.98, f32[4,12,64,256]{3,2,1,0:T(8,128)} %copy-done.17, f32[4,12,64]{2,1,0:T(8,128)S(1)} %get-tuple-element.15), kind=kOutput, calls=%fused_computation.58 | convolution fusion | flops 203292672 | bytes 7090176 | tf_op jit(solution)/shard_map/ghqk,gkhd->gqhd/dot_general | solution.py:80
  345.7 2.8 collective-permute-start.1
  348.6 4.0 %collective-permute-done.1 = bf16[63,1536]{1,0:T(8,128)(2,1)S(1)} collective-permute-done((bf16[63,1536]{1,0:T(8,128)(2,1)S(1)}, bf16[63,1536]{1,0:T(8,128)(2,1)S(1)}, u32[]{:S(2)}, u32[]{:S(2)}) %collective-permute-start.1) | collective-permute-done | bytes 193568 | tf_op jit(solution)/shard_map/ppermute | solution.py:17
  352.7 2.3 fusion.15
  354.9 19.1 %all-to-all-done.1 = bf16[8,192,896]{2,1,0:T(8,128)(2,1)} async-done(((bf16[8,192,896]{2,1,0:T(8,128)(2,1)}), bf16[8,192,896]{2,1,0:T(8,128)(2,1)}, u32[]{:S(2)}, u32[]{:S(2)}) %all-to-all-start.1) | async-done | bytes 2752544 | tf_op jit(solution)/shard_map/all_to_all | solution.py:22
  374.0 3.1 convert_reduce_fusion
  (105 shorter events, 6.2 us)
Async XLA Ops:
  7.2 23.1 %copy-start = (bf16[1,12,128,896]{3,2,1,0:T(8,128)(2,1)S(1)}, bf16[1,12,128,896]{3,2,1,0:T(8,128)(2,1)}, u32[]{:S(2)}) copy-start(bf16[1,12,128,896]{3,2,1,0:T(8,128)(2,1)} %param.14) | copy-start | bytes 8257540
  41.7 4.9 %copy-start.6 = (bf16[256,1536]{1,0:T(8,128)(2,1)S(1)}, bf16[256,1536]{1,0:T(8,128)(2,1)}, u32[]{:S(2)}) copy-start(bf16[256,1536]{1,0:T(8,128)(2,1)} %param.13) | copy-start | bytes 2359300
  41.7 5.1 %copy-start.12 = (f32[1536]{0:T(1024)S(1)}, f32[1536]{0:T(1024)}, u32[]{:S(2)}) copy-start(f32[1536]{0:T(1024)} %param.21) | copy-start | bytes 18436
  41.7 90.6 %all-to-all-start = ((bf16[16,2,128,896]{3,2,1,0:T(8,128)(2,1)}), bf16[16,2,128,896]{3,2,1,0:T(8,128)(2,1)}, u32[]{:S(2)}, u32[]{:S(2)}) async-start(bf16[16,2,128,896]{3,2,1,0:T(8,128)(2,1)} %select_select_fusion), calls=%async_computation | async-start | bytes 14680064 | tf_op jit(solution)/shard_map/all_to_all | solution.py:156
  46.6 284.4 %reduce-scatter.2.cloned.1.call-start = ((), (), s32[]{:S(2)}) async-start(), calls=%async_computation.3 | async-start | bytes 5849088 | tf_op jit(solution)/shard_map/reduce_scatter | solution.py:196
  46.6 6.3 %slice-start.2 = ((s8[4718592]{0:T(1024)(128)(4,1)}), s8[4194304]{0:T(1024)(128)(4,1)S(1)}, s32[]{:S(2)}) async-start(s8[4718592]{0:T(1024)(128)(4,1)} %bitcast.104), calls=%async_computation.6 | async-start | bytes 8388608
  46.9 6.1 %slice-start.3 = ((s8[4718592]{0:T(1024)(128)(4,1)}), s8[524288]{0:T(1024)(128)(4,1)S(1)}, s32[]{:S(2)}) async-start(s8[4718592]{0:T(1024)(128)(4,1)} %bitcast.104), calls=%async_computation.7 | async-start | bytes 1048576
  46.9 6.1 %copy-start.11 = (bf16[256,1536]{1,0:T(8,128)(2,1)S(1)}, bf16[256,1536]{1,0:T(8,128)(2,1)}, u32[]{:S(2)}) copy-start(bf16[256,1536]{1,0:T(8,128)(2,1)} %param.25) | copy-start | bytes 2359300
  51.5 4.2 %copy-start.8 = (s32[4,2]{0,1:T(2,128)S(1)}, s32[4,2]{0,1:T(2,128)}, u32[]{:S(2)}) copy-start(s32[4,2]{0,1:T(2,128)} %param.16) | copy-start | bytes 100
  51.5 4.7 %copy-start.9 = (s32[192]{0:T(256)S(1)}, s32[192]{0:T(256)}, u32[]{:S(2)}) copy-start(s32[192]{0:T(256)} %param.15) | copy-start | bytes 2308
  51.5 5.1 %copy-start.14 = (s32[4]{0:T(128)S(1)}, s32[4]{0:T(128)}, u32[]{:S(2)}) copy-start(s32[4]{0:T(128)} %param.17) | copy-start | bytes 52
  51.5 52.2 %collective-permute-start = (bf16[63,1536]{1,0:T(8,128)(2,1)}, bf16[63,1536]{1,0:T(8,128)(2,1)S(1)}, u32[]{:S(2)}, u32[]{:S(2)}) collective-permute-start(bf16[63,1536]{1,0:T(8,128)(2,1)} %slice.53), channel_id=1, source_target_pairs={{1,0},{2,1},{3,2},{4,3},{5,4},{6,5},{7,6},{8,7},{9,8},{10,9},{11,1... | collective-permute-start | bytes 580616 | tf_op jit(solution)/shard_map/ppermute | solution.py:17
  54.4 76.4 %collective-permute-start.2 = (bf16[63,1536]{1,0:T(8,128)(2,1)S(1)}, bf16[63,1536]{1,0:T(8,128)(2,1)S(1)}, u32[]{:S(2)}, u32[]{:S(2)}) collective-permute-start(bf16[63,1536]{1,0:T(8,128)(2,1)S(1)} %slice.58), channel_id=1, source_target_pairs={{1,0},{2,1},{3,2},{4,3},{5,4},{6,5},{7,6},{8,7},{9,8},{10,9},{11,1... | collective-permute-start | bytes 580616 | tf_op jit(solution)/shard_map/ppermute | solution.py:17
  136.3 1.1 copy-start.13
  173.1 3.5 copy-start.4
  173.2 7.4 %slice-start = ((s8[5505024]{0:T(1024)(128)(4,1)}), s8[4194304]{0:T(1024)(128)(4,1)S(1)}, s32[]{:S(2)}) async-start(s8[5505024]{0:T(1024)(128)(4,1)} %bitcast.102), calls=%async_computation.4 | async-start | bytes 8388608
  176.7 1.4 copy-start.10
  176.7 3.8 slice-start.1
  180.5 7.2 %copy-start.15 = (bf16[8,128,896]{2,1,0:T(8,128)(2,1)}, bf16[8,128,896]{2,1,0:T(8,128)(2,1)S(1)}, u32[]{:S(2)}) copy-start(bf16[8,128,896]{2,1,0:T(8,128)(2,1)S(1)} %fusion.10) | copy-start | bytes 5505028
  191.0 4.8 %copy-start.2 = (bf16[4,64,12,128]{3,2,1,0:T(8,128)(2,1)S(1)}, bf16[4,64,12,128]{3,2,1,0:T(8,128)(2,1)}, u32[]{:S(2)}) copy-start(bf16[4,64,12,128]{3,2,1,0:T(8,128)(2,1)} %reshape_reshape.9) | copy-start | bytes 2359300
  198.2 3.1 copy-start.5
  199.7 1.6 copy-start.17
  212.6 4.3 %copy-start.18 = (f32[4,12,64,256]{3,2,1,0:T(8,128)S(1)}, f32[4,12,64,256]{3,2,1,0:T(8,128)}, u32[]{:S(2)}) copy-start(f32[4,12,64,256]{3,2,1,0:T(8,128)} %copy-done.17) | copy-start | bytes 9437188
  221.3 1.9 copy-start.3
  221.3 2.4 copy-start.16
  333.8 18.8 %slice-start.4 = ((s8[4718592]{0:T(1024)(128)(4,1)}), s8[524288]{0:T(1024)(128)(4,1)S(1)}, s32[]{:S(2)}) async-start(s8[4718592]{0:T(1024)(128)(4,1)} %bitcast.106), calls=%async_computation.8 | async-start | bytes 1048576
  333.8 40.2 %all-to-all-start.1 = ((bf16[8,192,896]{2,1,0:T(8,128)(2,1)}), bf16[8,192,896]{2,1,0:T(8,128)(2,1)}, u32[]{:S(2)}, u32[]{:S(2)}) async-start(bf16[8,192,896]{2,1,0:T(8,128)(2,1)} %broadcast_in_dim.130), calls=%async_computation.2 | async-start | bytes 5505024 | tf_op jit(solution)/shard_map/all_to_all | solution.py:22
  340.7 12.0 %slice-start.5 = ((s8[4718592]{0:T(1024)(128)(4,1)}), s8[4194304]{0:T(1024)(128)(4,1)S(1)}, s32[]{:S(2)}) async-start(s8[4718592]{0:T(1024)(128)(4,1)} %bitcast.106), calls=%async_computation.9 | async-start | bytes 8388608
  344.9 7.7 %copy-start.7 = (bf16[256,1536]{1,0:T(8,128)(2,1)S(1)}, bf16[256,1536]{1,0:T(8,128)(2,1)}, u32[]{:S(2)}) copy-start(bf16[256,1536]{1,0:T(8,128)(2,1)} %param.13) | copy-start | bytes 2359300
  345.7 6.9 %collective-permute-start.1 = (bf16[63,1536]{1,0:T(8,128)(2,1)S(1)}, bf16[63,1536]{1,0:T(8,128)(2,1)S(1)}, u32[]{:S(2)}, u32[]{:S(2)}) collective-permute-start(bf16[63,1536]{1,0:T(8,128)(2,1)S(1)} %slice.55), channel_id=1, source_target_pairs={{0,1},{1,2},{2,3},{3,4},{4,5},{5,6},{6,7},{7,8},{8,9},{9,10},{10,1... | collective-permute-start | bytes 580616 | tf_op jit(solution)/shard_map/ppermute | solution.py:17
  352.6 24.4 %copy-start.1 = (bf16[1,12,128,896]{3,2,1,0:T(8,128)(2,1)S(1)}, bf16[1,12,128,896]{3,2,1,0:T(8,128)(2,1)}, u32[]{:S(2)}) copy-start(bf16[1,12,128,896]{3,2,1,0:T(8,128)(2,1)} %param.14) | copy-start | bytes 8257540
Sparse Core Ops, SparseCore 0:
  235.0 95.9 reduce-scatter.1
where the time goes:
time: 392 us; the launch traced here: 384 us
  waiting for transfers between devices  192 us (49%)
  local copies, waits for them, and re-layouts  63.8 us (16%)
  matrix products  57.9 us (15%)
  blocking collectives  20.7 us (5%)
  other arithmetic  18.1 us (5%)
  starting transfers between devices  17.2 us (4%)
  between operations  15 us (4%)
    reduce_scatter x1, waiting for transfers between devices, local(): lax.psum_scatter(lax.dot_general(grad_rows_all, local_rows, (((0,), (0,))...  96.1 us
    ppermute x3, waiting for transfers between devices, shifted(): return lax.ppermute(block, axis, route)  76.4 us
    unnamed x58, local copies, waits for them, and re-layouts  21.2 us
    all_gather x1, blocking collectives, local(): asked = lax.all_gather(neighbours, 'seq', axis=0, tiled=True)  20.7 us
    all_to_all x1, waiting for transfers between devices, sent_to_all(): return lax.all_to_all(copies, axis, split_axis=0, concat_axis=0, tiled=True)  19.1 us
    reshape x1, local copies, waits for them, and re-layouts, encode(): projected.astype(jnp.bfloat16).reshape(count, length, 3, head_count, HEAD)  11.7 us
    dot_general x1, matrix products, local(): lax.dot_general(grad_rows_all, local_rows, (((0,), (0,)), ((), ())), pref...  11 us
    dot_general x1, matrix products, encode(): jnp.dot(normed.reshape(count * length, width), encoder_projection, prefer...  10.8 us
  transfers between devices with their start and end apart: 6, of which 5 were waited for; matrix products, arithmetic and copies ran while one was open for 5% of the time, Pallas kernels for 0%

commit v1 on v0

v1 whole, which is shorter than its diff:
```python
import functools

import jax
import jax.numpy as jnp
from jax import lax
from jax.experimental import pallas as pl
from jax.experimental.pallas import tpu as pltpu
from jax.sharding import PartitionSpec as P


HEAD = 128
K = 2
SPAN = 64
EPSILON = 1e-06
BF16 = jnp.bfloat16
F32 = jnp.float32
VMEM = pltpu.VMEM
NN = (((1,), (0,)), ((), ()))
NT = (((1,), (1,)), ((), ()))
TN = (((0,), (0,)), ((), ()))


def dot(a, b, dims):
    return lax.dot_general(a, b, dims, preferred_element_type=F32)


def rms_norm(values, norm_gain):
    widened = values.astype(F32)
    return (
        widened
        * lax.rsqrt(jnp.mean(widened * widened, axis=-1, keepdims=True) + EPSILON)
        * norm_gain
    )


def spread_kernel(blocks_ref, notes_ref, hidden_ref, cotangent_ref, slices_ref, tails_ref):
    blocks, _, feature = blocks_ref.shape
    devices, units, rows, _ = slices_ref.shape
    tiles = feature // HEAD
    for d in range(devices):
        for b in range(blocks):
            for k in range(tiles):
                slices_ref[d, b * tiles + k] = blocks_ref[
                    b, d * rows : (d + 1) * rows, k * HEAD : (k + 1) * HEAD
                ]
        slices_ref[d, units - 1] = notes_ref[...]

    @pl.when(pl.program_id(0) == 0)
    def _():
        tails_ref[0] = hidden_ref[...]
        tails_ref[1] = cotangent_ref[...]


def spread(database, notes, hidden, cotangent, devices):
    blocks, length, feature = database.shape
    width = hidden.shape[1]
    units = blocks * (feature // HEAD) + 1
    rows = length // devices
    step = 4
    return pl.pallas_call(
        spread_kernel,
        grid=(devices // step,),
        out_shape=(
            jax.ShapeDtypeStruct((devices, units, rows, HEAD), BF16),
            jax.ShapeDtypeStruct((2, SPAN, width), BF16),
        ),
        in_specs=[
            pl.BlockSpec((blocks, step * rows, feature), lambda i: (0, i, 0)),
            pl.BlockSpec((rows, HEAD), lambda i: (0, 0)),
            pl.BlockSpec((SPAN, width), lambda i: (0, 0)),
            pl.BlockSpec((SPAN, width), lambda i: (0, 0)),
        ],
        out_specs=(
            pl.BlockSpec((step, units, rows, HEAD), lambda i: (i, 0, 0, 0)),
            pl.BlockSpec((2, SPAN, width), lambda i: (0, 0, 0)),
        ),
        cost_estimate=pl.CostEstimate(flops=1 << 20, bytes_accessed=6 << 20, transcendentals=0),
        compiler_params=pltpu.CompilerParams(vmem_limit_bytes=60 << 20),
        name="spread",
    )(database, notes, hidden, cotangent)


def pick_kernel(tiles, where_ref, table_ref, *outs):
    blocks = table_ref.shape[1] // tiles

    @pl.loop(0, outs[0].shape[0])
    def _(r):
        first = 0
        for out in outs:
            for i in range(out.shape[1] // tiles):
                where = where_ref[r, first + i]
                start = (where % blocks) * tiles
                out[r, i * tiles : (i + 1) * tiles] = table_ref[
                    where // blocks, pl.ds(start, tiles)
                ]
            first += out.shape[1] // tiles


def pick(where, table, tiles, chunks):
    readers, requests = where.shape
    rows, width = table.shape[2:]
    shape = jax.ShapeDtypeStruct((readers, requests // chunks * tiles, rows, width), BF16)
    whole = pl.BlockSpec(memory_space=VMEM)
    return pl.pallas_call(
        functools.partial(pick_kernel, tiles),
        out_shape=(shape,) * chunks,
        in_specs=[pl.BlockSpec(memory_space=pltpu.SMEM), whole],
        out_specs=(whole,) * chunks,
        compiler_params=pltpu.CompilerParams(vmem_limit_bytes=60 << 20),
        name="pick",
    )(where, table)


def span_kernel(
    first_span,
    counts_ref,
    pieces_ref,
    gain_ref,
    projection_hbm,
    output_hbm,
    keyvalue_hbm,
    queries_ref,
    grads_ref,
    encoded_ref,
    grad_ref,
    attended_ref,
    projection_ref,
    output_ref,
    keyvalue_ref,
    plain_ref,
    normed_ref,
    qkv_ref,
    mixed_ref,
    kv_ref,
    encoder_scores_ref,
    encoder_weights_ref,
    scores_ref,
    changes_ref,
    chances_ref,
    grad_scores_ref,
    sems,
):
    slices, _, rows, _ = pieces_ref.shape
    length = slices * rows
    total, feature = encoded_ref.shape
    width = queries_ref.shape[1]
    blocks = total // length
    tiles = feature // HEAD
    heads = width // HEAD
    spans = blocks // K
    keys = K * length
    scale = HEAD ** (-0.5)
    chunk = 2 * width // (slices * 8)
    tile = 512
    steps = (3 * feature) // tile
    rest = pl.ds(steps * tile, 3 * feature - steps * tile)
    wide_steps = 2 * width // tile

    def load(columns, index):
        return pltpu.make_async_copy(
            projection_hbm.at[:, columns], projection_ref.at[:, columns], sems.at[index]
        )

    def wide_load(columns, index):
        return pltpu.make_async_copy(
            keyvalue_hbm.at[columns], keyvalue_ref.at[columns], sems.at[steps + 2 + index]
        )

    output_load = pltpu.make_async_copy(output_hbm, output_ref, sems.at[steps + 1])
    for j in range(steps):
        load(pl.ds(j * tile, tile), j).start()
    load(rest, steps).start()
    output_load.start()
    for j in range(wide_steps):
        wide_load(pl.ds(j * tile, tile), j).start()

    gain = gain_ref[...].reshape(1, feature)
    for b in range(blocks):
        block_rows = slice(b * length, (b + 1) * length)
        for k in range(tiles):
            plain_ref[block_rows, k * HEAD : (k + 1) * HEAD] = (
                pieces_ref[:, b * tiles + k].astype(F32).reshape(length, HEAD)
            )
        normed_ref[block_rows] = rms_norm(plain_ref[block_rows], gain).astype(BF16)

    @pl.loop(0, steps)
    def _(j):
        columns = pl.ds(pl.multiple_of(j * tile, tile), tile)
        load(columns, j).wait()
        qkv_ref[:, columns] = dot(normed_ref[...], projection_ref[:, columns], NN).astype(BF16)

    load(rest, steps).wait()
    qkv_ref[:, rest] = dot(normed_ref[...], projection_ref[:, rest], NN).astype(BF16)

    together = 2
    ones = jnp.ones((length, HEAD), BF16)

    @pl.loop(0, blocks // together)
    def _(step):
        pairs = [(b, h) for b in range(together) for h in range(tiles)]

        def part(which, b, h):
            start = pl.multiple_of((step * together + b) * length, length)
            return qkv_ref[pl.ds(start, length), pl.ds(which * feature + h * HEAD, HEAD)]

        for i, (b, h) in enumerate(pairs):
            encoder_scores_ref[i] = dot(part(0, b, h), part(1, b, h), NT) * scale
        tops = [jnp.max(encoder_scores_ref[i], axis=-1, keepdims=True) for i in range(len(pairs))]
        for i, top in enumerate(tops):
            encoder_weights_ref[i] = jnp.exp(encoder_scores_ref[i] - top).astype(BF16)
        for i, (b, h) in enumerate(pairs):
            value = jnp.concatenate([part(2, b, h), ones], axis=-1)
            summed_up = dot(encoder_weights_ref[i], value, NN)
            start = pl.multiple_of((step * together + b) * length, length)
            mixed_ref[pl.ds(start, length), h * HEAD : (h + 1) * HEAD] = (
                summed_up[:, :HEAD] / summed_up[:, HEAD:]
            ).astype(BF16)

    output_load.wait()
    for start in range(0, feature, 256):
        columns = slice(start, min(start + 256, feature))
        encoded_ref[:, columns] = (
            plain_ref[:, columns] + dot(mixed_ref[...], output_ref[:, columns], NN)
        ).astype(BF16)

    @pl.loop(0, wide_steps)
    def _(j):
        columns = pl.ds(pl.multiple_of(j * tile, tile), tile)
        wide_load(columns, j).wait()
        kv_ref[:, columns] = dot(encoded_ref[...], keyvalue_ref[columns, :], NT).astype(BF16)

    key_block = lax.broadcasted_iota(jnp.int32, (1, keys), 1) // length

    @pl.loop(0, spans)
    def _(u):
        valid = key_block < counts_ref[first_span + u]
        query_rows = pl.ds(pl.multiple_of(u * SPAN, SPAN), SPAN)
        key_rows = pl.ds(pl.multiple_of(u * keys, keys), keys)

        def columns(h):
            return slice(h * HEAD, (h + 1) * HEAD)

        for h in range(heads):
            key = kv_ref[key_rows, columns(h)]
            value = kv_ref[key_rows, columns(heads + h)]
            scores = dot(queries_ref[query_rows, columns(h)], key, NT) * scale
            scores_ref[h] = jnp.where(valid, scores, -1e30)
            changes_ref[h] = dot(grads_ref[query_rows, columns(h)], value, NT)
        tops = [jnp.max(scores_ref[h], axis=-1, keepdims=True) for h in range(heads)]
        for h in range(heads):
            scores_ref[h] = jnp.exp(scores_ref[h] - tops[h])
        sums = [jnp.sum(scores_ref[h], axis=-1, keepdims=True) for h in range(heads)]
        for h in range(heads):
            chances = scores_ref[h] * (1.0 / sums[h])
            scores_ref[h] = chances
            chances_ref[h] = chances.astype(BF16)
        inners = [
            jnp.sum(scores_ref[h] * changes_ref[h], axis=-1, keepdims=True) for h in range(heads)
        ]
        for h in range(heads):
            grad_scores_ref[h] = (scores_ref[h] * (changes_ref[h] - inners[h])).astype(BF16)
        for h in range(heads):
            value = kv_ref[key_rows, columns(heads + h)]
            query = queries_ref[query_rows, columns(h)]
            grad = grads_ref[query_rows, columns(h)]
            attended_ref[query_rows, columns(h)] = dot(chances_ref[h], value, NN).astype(BF16)
            for part, piece in enumerate(
                (
                    dot(query, grad_scores_ref[h], TN) * scale,
                    dot(grad, chances_ref[h], TN),
                )
            ):
                for j in range(HEAD // 8):
                    row = part * width + h * HEAD + j * 8
                    seq, inside = divmod(row, 8 * chunk)
                    dp, offset = divmod(inside, chunk)
                    base = ((dp // 2) * slices + seq) * chunk + offset
                    grad_ref[dp % 2, base : base + 8, key_rows] = piece[j * 8 : j * 8 + 8].astype(
                        BF16
                    )


def span_step(part, counts, pieces, gain, projection, output, keyvalue, queries, grads):
    width = queries.shape[1]
    feature = keyvalue.shape[1]
    slices, units, rows, _ = pieces.shape
    tiles = feature // HEAD
    length = slices * rows
    blocks = units // tiles
    total = blocks * length
    spans = blocks // K
    keys = K * length
    heads = width // HEAD
    whole = pl.BlockSpec(memory_space=VMEM)
    hbm = pl.BlockSpec(memory_space=pltpu.HBM)
    own = pl.BlockSpec((spans * SPAN, width), lambda i: (part, 0))
    return pl.pallas_call(
        functools.partial(span_kernel, part * spans),
        grid=(1,),
        out_shape=(
            jax.ShapeDtypeStruct((total, feature), BF16),
            jax.ShapeDtypeStruct((2, width, total), BF16),
            jax.ShapeDtypeStruct((spans * SPAN, width), BF16),
        ),
        in_specs=[
            pl.BlockSpec(memory_space=pltpu.SMEM),
            whole,
            whole,
            hbm,
            hbm,
            hbm,
            own,
            own,
        ],
        out_specs=(whole, whole, whole),
        scratch_shapes=[
            VMEM(projection.shape, BF16),
            VMEM(output.shape, BF16),
            VMEM(keyvalue.shape, BF16),
            VMEM((total, feature), F32),
            VMEM((total, feature), BF16),
            VMEM((total, 3 * feature), BF16),
            VMEM((total, feature), BF16),
            VMEM((total, 2 * width), BF16),
            VMEM((2 * tiles, length, length), F32),
            VMEM((2 * tiles, length, length), BF16),
            VMEM((heads, SPAN, keys), F32),
            VMEM((heads, SPAN, keys), F32),
            VMEM((heads, SPAN, keys), BF16),
            VMEM((heads, SPAN, keys), BF16),
            pltpu.SemaphoreType.DMA((3 * feature // 512 + 2 + 2 * width // 512,)),
        ],
        cost_estimate=pl.CostEstimate(
            flops=total * feature * (8 * feature + 4 * width),
            bytes_accessed=20 << 20,
            transcendentals=1 << 20,
        ),
        compiler_params=pltpu.CompilerParams(vmem_limit_bytes=60 << 20),
        name="spans",
    )(counts, pieces, gain, projection, output, keyvalue, queries, grads)


def weight_kernel(half_ref, grad_a, grad_b, encoded_a, encoded_b, out_ref):
    out_ref[...] = (
        dot(grad_a[0], encoded_a[...], NN) + dot(grad_b[0], encoded_b[...], NN)
    ).astype(BF16)


def weight_half(half, grads, encodeds):
    _, rows, keys = grads[0].shape
    feature = encodeds[0].shape[1]
    tile = 512
    grad_spec = pl.BlockSpec((1, tile, keys), lambda i, half: (half[0], i, 0))
    encoded_spec = pl.BlockSpec((keys, feature), lambda i, half: (0, 0))
    return pl.pallas_call(
        weight_kernel,
        grid_spec=pltpu.PrefetchScalarGridSpec(
            num_scalar_prefetch=1,
            grid=(rows // tile,),
            in_specs=[grad_spec, grad_spec, encoded_spec, encoded_spec],
            out_specs=pl.BlockSpec((tile, feature), lambda i, half: (i, 0)),
        ),
        out_shape=jax.ShapeDtypeStruct((rows, feature), BF16),
        cost_estimate=pl.CostEstimate(
            flops=4 * rows * feature * keys, bytes_accessed=8 << 20, transcendentals=0
        ),
        compiler_params=pltpu.CompilerParams(vmem_limit_bytes=60 << 20),
        name="weight_half",
    )(half, *grads, *encodeds)


def locate(block_ids, block_home):
    hits = block_ids[..., None] == jnp.arange(block_home.shape[0], dtype=jnp.int32)
    return jnp.sum(jnp.where(hits, block_home, 0), axis=-1)


def all_to_all(block, axis, groups=None):
    return lax.all_to_all(
        block, axis, split_axis=0, concat_axis=0, tiled=True, axis_index_groups=groups
    )


def summed(copies):
    return copies.astype(F32).sum(axis=0)


def local(
    hidden,
    database,
    block_home,
    neighbours,
    neighbour_counts,
    encoder_gain,
    encoder_projection,
    encoder_output,
    cross_gain,
    cross_query,
    cross_keyvalue,
    cross_output,
    cotangent,
):
    token_count, _ = hidden.shape
    _, length, feature = database.shape[1:]
    seq = lax.axis_size("seq")
    dp = lax.axis_size("dp")
    requests = neighbours.size
    tail = SPAN - 1

    tiles = feature // HEAD
    where = locate(neighbours.reshape(-1), block_home)
    notes = jnp.broadcast_to(jnp.pad(where, (0, HEAD - requests)), (length // seq, HEAD))
    slices, tails = spread(database[0], notes.astype(BF16), hidden, cotangent, seq)
    late = lax.ppermute(tails, "seq", [(i, i - 1) for i in range(1, seq)])
    late_hidden, late_cotangent = late[0, :tail], late[1, :tail]
    table = all_to_all(slices, "seq")
    readers_where = table[:, -1, 0, :requests].astype(jnp.int32)

    own_hidden = jnp.concatenate([hidden[tail:], late_hidden], axis=0)
    own_cotangent = jnp.concatenate([cotangent[tail:], late_cotangent], axis=0)
    normed = rms_norm(own_hidden, cross_gain).astype(BF16)
    queries = dot(normed, cross_query, NN).astype(BF16)
    grads = dot(own_cotangent, cross_output, NT).astype(BF16)

    chunks = 2
    encoded, grad_rows, attended = [], [], []
    picked = pick(readers_where, table, tiles, chunks)
    for part in range(chunks):
        pieces = all_to_all(picked[part], "seq")
        out = span_step(
            part,
            neighbour_counts,
            pieces,
            encoder_gain,
            encoder_projection,
            encoder_output,
            cross_keyvalue,
            queries,
            grads,
        )
        encoded.append(out[0])
        grad_rows.append(out[1])
        attended.append(out[2])

    core = lax.axis_index("dp") % 2
    theirs = weight_half((1 - core).reshape(1), grad_rows, encoded)
    received = lax.ppermute(theirs, "dp", [(i, i ^ 1) for i in range(dp)])
    mine = weight_half(core.reshape(1), grad_rows, encoded)
    pair = (mine.astype(F32) + received.astype(F32)).astype(BF16)

    half = [
        [d * seq + s for d in range(c, dp, 2) for s in range(seq)] for c in range(2)
    ]
    sent = all_to_all(pair.reshape(dp // 2 * seq, -1, feature), ("dp", "seq"), half)
    piece = summed(sent).astype(BF16)
    keyvalue_grad = all_to_all(jnp.broadcast_to(piece, (dp, *piece.shape)), "dp")
    keyvalue_grad = keyvalue_grad.reshape(-1, feature).astype(F32)

    cross = dot(jnp.concatenate(attended, axis=0), cross_output, NN)
    rows = (own_hidden.astype(F32) + cross).astype(BF16)
    forth = [(i, i + 1) for i in range(seq - 1)]
    returned = lax.ppermute(rows[token_count - tail :], "seq", forth)
    first = jnp.where(lax.axis_index("seq") == 0, hidden[:tail], returned)
    output = jnp.concatenate([first, rows[: token_count - tail]], axis=0)
    return (output, keyvalue_grad)


def solution(mesh):
    placed = (
        P(("dp", "seq"), None),
        P("dp", "seq", None, None),
        P(),
        P(("dp", "seq"), None),
        P(("dp", "seq")),
        P(),
        P(),
        P(),
        P(),
        P(),
        P(),
        P(),
        P(("dp", "seq"), None),
    )
    return jax.shard_map(
        local,
        mesh=mesh,
        in_specs=placed,
        out_specs=(P(("dp", "seq"), None), P("seq", None)),
        check_vma=False,
    )
```

time: 392 us -> 209 us (0.53); the launches traced: 384 us -> 208 us
  waiting for transfers between devices: 192 us -> 71.3 us
  Pallas kernels: 0 us -> 59.7 us
  local copies, waits for them, and re-layouts: 63.8 us -> 9.02 us
  matrix products: 57.9 us -> 13.4 us
  starting transfers between devices: 17.2 us -> 43.8 us
  blocking collectives: 20.7 us -> 0 us
  between operations: 15 us -> 0.81 us
  other arithmetic: 18.1 us -> 9.7 us
    reduce_scatter x1 -> x0, waiting for transfers between devices: 96.1 us -> none  [local(): lax.psum_scatter(lax.dot_general(grad_rows_all, local_rows, (((0,), (0,))...]
    ppermute x3, waiting for transfers between devices: 76.4 us -> 0.01 us  [the longest x1 0.01 us: local(): late = lax.ppermute(tails, 'seq', [(i, i - 1) for i in range(1, seq)])]
    pallas_call x0 -> x6, Pallas kernels: none -> 59.7 us  [the longest x2 37.7 us: span_step(): pl.pallas_call(functools.partial(span_kernel, part * spans), grid=(1,), o...]
    all_to_all x2 -> x5, waiting for transfers between devices: 19.1 us -> 71.3 us  [all_to_all(): lax.all_to_all(block, axis, split_axis=0, concat_axis=0, tiled=True, axis...]
    dot_general x14 -> x3, matrix products: 57.9 us -> 13.4 us  [dot(): return lax.dot_general(a, b, dims, preferred_element_type=F32)]
    all_to_all x2 -> x5, starting transfers between devices: 11.7 us -> 33.9 us  [all_to_all(): lax.all_to_all(block, axis, split_axis=0, concat_axis=0, tiled=True, axis...]
    all_gather x1 -> x0, blocking collectives: 20.7 us -> none  [local(): asked = lax.all_gather(neighbours, 'seq', axis=0, tiled=True)]
    unnamed x58 -> x19, local copies, waits for them, and re-layouts: 21.2 us -> 2.65 us
  transfers between devices with their start and end apart: 6 -> 8, of which waited for: 5 -> 4; matrix products, arithmetic and copies ran while one was open for 5% -> 11% of each run, Pallas kernels for 0% -> 14%
where the time goes in v1:
time: 209 us; the launch traced here: 208 us
  waiting for transfers between devices  71.3 us (34%)
  Pallas kernels  59.7 us (29%)
  starting transfers between devices  43.8 us (21%)
  matrix products  13.4 us (6%)
  other arithmetic  9.7 us (5%)
  local copies, waits for them, and re-layouts  9.02 us (4%)
    all_to_all x5, waiting for transfers between devices, all_to_all(): lax.all_to_all(block, axis, split_axis=0, concat_axis=0, tiled=True, axis...  71.3 us
    pallas_call x2, Pallas kernels, span_step(): pl.pallas_call(functools.partial(span_kernel, part * spans), grid=(1,), o...  37.7 us
    all_to_all x5, starting transfers between devices, all_to_all(): lax.all_to_all(block, axis, split_axis=0, concat_axis=0, tiled=True, axis...  33.9 us
    pallas_call x2, Pallas kernels, weight_half(): pl.pallas_call(weight_kernel, grid_spec=pltpu.PrefetchScalarGridSpec(num_...  13.6 us
    dot_general x3, matrix products, dot(): return lax.dot_general(a, b, dims, preferred_element_type=F32)  13.4 us
    ppermute x1, starting transfers between devices, local(): received = lax.ppermute(theirs, 'dp', [(i, i ^ 1) for i in range(dp)])  5.02 us
    pallas_call x1, Pallas kernels, spread(): pl.pallas_call(spread_kernel, grid=(devices // step,), out_shape=(jax.Sha...  4.34 us
  transfers between devices with their start and end apart: 8, of which 4 were waited for; matrix products, arithmetic and copies ran while one was open for 11% of the time, Pallas kernels for 14%

profile of v1, /device:TPU:1, one launch (start us, length us, event | category | flops | bytes accessed | tf_op | source)
XLA Modules:
  0.0 207.8 jit_solution(5973691855876703033)
XLA Ops:
  0.6 0.8 copy.24
  1.4 0.1 eq.21
  1.5 0.9 select_reduce_fusion
  2.4 0.6 broadcast_in_dim.19.notes_ref
  2.9 4.3 %spread.1 = (bf16[16,85,8,128]{3,2,1,0:T(8,128)(2,1)}, bf16[2,64,1536]{2,1,0:T(8,128)(2,1)}) custom-call(bf16[12,128,896]{2,1,0:T(8,128)(2,1)} %bitcast.16, bf16[8,128]{1,0:T(8,128)(2,1)} %broadcast_in_dim.19.notes_ref, bf16[256,1536]{1,0:T(8,128)(2,1)} %hidden_ref.1, bf16[256,1536]{1,0:T(8,128)(2,1)} %cotangent_ref.1), custom_call_target="tpu_custom_call" | custom-call | flops 1048576 | bytes 6291456 | tf_op jit(solution)/shard_map/spread/pallas_call | solution.py:60
  7.3 8.6 %all-to-all-start = ((bf16[16,85,8,128]{3,2,1,0:T(8,128)(2,1)}), bf16[16,85,8,128]{3,2,1,0:T(8,128)(2,1)S(1)}, u32[]{:S(2)}, u32[]{:S(2)}) async-start(bf16[16,85,8,128]{3,2,1,0:T(8,128)(2,1)} %get-tuple-element.13), calls=%async_computation | async-start | bytes 5570560 | tf_op jit(solution)/shard_map/all_to_all | solution.py:378
  15.9 1.3 collective-permute-start
  17.2 0.0 copy-start.1
  17.2 1.3 slice.25
  18.5 0.0 copy-done.1
  18.5 1.0 slice.28
  19.5 32.8 %all-to-all-done.table_ref = bf16[16,85,8,128]{3,2,1,0:T(8,128)(2,1)S(1)} async-done(((bf16[16,85,8,128]{3,2,1,0:T(8,128)(2,1)}), bf16[16,85,8,128]{3,2,1,0:T(8,128)(2,1)S(1)}, u32[]{:S(2)}, u32[]{:S(2)}) %all-to-all-start) | async-done | bytes 2785312 | tf_op jit(solution)/shard_map/all_to_all | solution.py:378
  52.4 0.7 slice_convert_fusion
  53.0 0.9 copy-done
  53.9 4.1 %pick.1 = (bf16[16,28,8,128]{3,2,1,0:T(8,128)(2,1)}, bf16[16,28,8,128]{3,2,1,0:T(8,128)(2,1)}) custom-call(s32[16,8]{1,0:T(8,128)} %bitcast.17, bf16[16,85,8,128]{3,2,1,0:T(8,128)(2,1)} %copy-done), custom_call_target="tpu_custom_call" | custom-call | tf_op jit(solution)/shard_map/pick/pallas_call | solution.py:104
  58.1 6.5 %all-to-all-start.2 = ((bf16[16,28,8,128]{3,2,1,0:T(8,128)(2,1)}), bf16[16,28,8,128]{3,2,1,0:T(8,128)(2,1)S(1)}, u32[]{:S(2)}, u32[]{:S(2)}) async-start(bf16[16,28,8,128]{3,2,1,0:T(8,128)(2,1)} %get-tuple-element.16), calls=%async_computation.2 | async-start | bytes 1835008 | tf_op jit(solution)/shard_map/all_to_all | solution.py:378
  64.6 0.0 collective-permute-done
  64.6 1.0 slice_bitcast_fusion
  65.6 0.0 copy-start.6
  65.6 0.3 fusion.1
  65.9 0.0 copy-done.3
  65.9 4.6 %convolution_convert_fusion.1.queries_ref = bf16[256,1536]{1,0:T(8,128)(2,1)} fusion(bf16[1536,1536]{1,0:T(8,128)(2,1)} %param.22, f32[1536]{0:T(1024)S(1)} %copy-done.8, f32[256]{0:T(256)S(1)} %add_rsqrt_fusion, bf16[63,1536]{1,0:T(8,128)(2,1)S(1)} %get-tuple-element.23, bf16[193,1536]{1,0:T(8,128)(2,1)S(1)} %slice.25), kind=kOutput, calls=%fused_computation.4 | convolution fusion | flops 1211105280 | bytes 6298624 | tf_op jit(solution)/shard_map/dot_general | solution.py:24
  70.6 5.4 %all-to-all-done.2.pieces_ref = bf16[16,28,8,128]{3,2,1,0:T(8,128)(2,1)S(1)} async-done(((bf16[16,28,8,128]{3,2,1,0:T(8,128)(2,1)}), bf16[16,28,8,128]{3,2,1,0:T(8,128)(2,1)S(1)}, u32[]{:S(2)}, u32[]{:S(2)}) %all-to-all-start.2) | async-done | bytes 917536 | tf_op jit(solution)/shard_map/all_to_all | solution.py:378
  75.9 4.1 %all-to-all-start.1 = ((bf16[16,28,8,128]{3,2,1,0:T(8,128)(2,1)}), bf16[16,28,8,128]{3,2,1,0:T(8,128)(2,1)S(1)}, u32[]{:S(2)}, u32[]{:S(2)}) async-start(bf16[16,28,8,128]{3,2,1,0:T(8,128)(2,1)} %get-tuple-element.14), calls=%async_computation.1 | async-start | bytes 1835008 | tf_op jit(solution)/shard_map/all_to_all | solution.py:378
  80.0 4.7 %convolution_convert_fusion.grads_ref = bf16[256,1536]{1,0:T(8,128)(2,1)} fusion(bf16[1536,1536]{1,0:T(8,128)(2,1)} %param.24, bf16[63,1536]{1,0:T(8,128)(2,1)S(1)} %get-tuple-element.22, bf16[193,1536]{1,0:T(8,128)(2,1)S(1)} %copy-done.7), kind=kOutput, calls=%fused_computation.3 | convolution fusion | flops 1209925632 | bytes 6291456 | tf_op jit(solution)/shard_map/dot_general | solution.py:24
  84.7 18.8 %spans.3 = (bf16[512,896]{1,0:T(8,128)(2,1)}, bf16[2,1536,512]{2,1,0:T(8,128)(2,1)}, bf16[128,1536]{1,0:T(8,128)(2,1)}) custom-call(s32[4]{0:T(128)} %counts_ref.3, bf16[16,28,8,128]{3,2,1,0:T(8,128)(2,1)} %copy-done.4, f32[896]{0:T(1024)} %gain_ref.3, bf16[896,2688]{1,0:T(8,128)(2,1)} %projection_hbm.3, bf16[896,896]{1,0:T(8,128)(2,1)} %output_hbm.3, ...), custom_call_target="tpu_custom_call" | custom-call | flops 6106906624 | bytes 20971520 | tf_op jit(solution)/shard_map/spans/pallas_call | solution.py:297
  103.5 0.0 all-to-all-done.1.pieces_ref
  103.5 0.9 copy-done.5
  104.5 18.8 %spans.2 = (bf16[512,896]{1,0:T(8,128)(2,1)}, bf16[2,1536,512]{2,1,0:T(8,128)(2,1)}, bf16[128,1536]{1,0:T(8,128)(2,1)}) custom-call(s32[4]{0:T(128)} %counts_ref.3, bf16[16,28,8,128]{3,2,1,0:T(8,128)(2,1)} %copy-done.5, f32[896]{0:T(1024)} %gain_ref.3, bf16[896,2688]{1,0:T(8,128)(2,1)} %projection_hbm.3, bf16[896,896]{1,0:T(8,128)(2,1)} %output_hbm.3, ...), custom_call_target="tpu_custom_call" | custom-call | flops 6106906624 | bytes 20971520 | tf_op jit(solution)/shard_map/spans/pallas_call | solution.py:297
  123.3 6.9 %weight_half.3 = bf16[1536,896]{1,0:T(8,128)(2,1)} custom-call(s32[1]{0:T(128)} %bitcast.5.half_ref, bf16[2,1536,512]{2,1,0:T(8,128)(2,1)} %get-tuple-element.18.grad_a, bf16[2,1536,512]{2,1,0:T(8,128)(2,1)} %get-tuple-element.19.grad_b, bf16[512,896]{1,0:T(8,128)(2,1)} %get-tuple-element.20.encoded_a, bf16[512,896]{1,0:T(8,128)(2,1)} %get-tuple-element.21.encoded_b), custom_call_target="tpu_custom_call" | custom-call | flops 2818572288 | bytes 8388608 | tf_op jit(solution)/shard_map/weight_half/pallas_call | solution.py:355
  130.1 5.0 %collective-permute-start.2 = (bf16[1536,896]{1,0:T(8,128)(2,1)}, bf16[1536,896]{1,0:T(8,128)(2,1)S(1)}, u32[]{:S(2)}, u32[]{:S(2)}) collective-permute-start(bf16[1536,896]{1,0:T(8,128)(2,1)} %weight_half.3), channel_id=1, source_target_pairs={{0,16},{16,0},{32,48},{48,32},{64,80},{80,64},{96,112},{112,96},{1... | collective-permute-start | bytes 8257544 | tf_op jit(solution)/shard_map/ppermute | solution.py:446
  135.2 6.7 %weight_half.2 = bf16[1536,896]{1,0:T(8,128)(2,1)} custom-call(s32[1]{0:T(128)} %bitcast.4.half_ref, bf16[2,1536,512]{2,1,0:T(8,128)(2,1)} %get-tuple-element.18.grad_a, bf16[2,1536,512]{2,1,0:T(8,128)(2,1)} %get-tuple-element.19.grad_b, bf16[512,896]{1,0:T(8,128)(2,1)} %get-tuple-element.20.encoded_a, bf16[512,896]{1,0:T(8,128)(2,1)} %get-tuple-element.21.encoded_b), custom_call_target="tpu_custom_call" | custom-call | flops 2818572288 | bytes 8388608 | tf_op jit(solution)/shard_map/weight_half/pallas_call | solution.py:355
  141.9 0.0 collective-permute-done.2
  141.9 4.0 %add_convert_fusion = bf16[1536,896]{1,0:T(8,128)(2,1)} fusion(bf16[1536,896]{1,0:T(8,128)(2,1)S(1)} %collective-permute-done.2, bf16[1536,896]{1,0:T(8,128)(2,1)} %weight_half.2), kind=kLoop, calls=%fused_computation | loop fusion | flops 5505024 | bytes 8257536 | tf_op jit(solution)/shard_map/convert_element_type | solution.py:448
  145.9 10.1 %all-to-all-start.3 = ((bf16[64,24,896]{2,1,0:T(8,128)(2,1)}), bf16[64,24,896]{2,1,0:T(8,128)(2,1)S(1)}, u32[]{:S(2)}, u32[]{:S(2)}) async-start(bf16[64,24,896]{2,1,0:T(8,128)(2,1)} %bitcast.15), calls=%async_computation.3 | async-start | bytes 5505024 | tf_op jit(solution)/shard_map/all_to_all | solution.py:378
  156.0 4.1 %fusion = bf16[256,1536]{1,0:T(8,128)(2,1)S(1)} fusion(bf16[1536,1536]{1,0:T(8,128)(2,1)} %param.24, bf16[128,1536]{1,0:T(8,128)(2,1)} %get-tuple-element.17, bf16[128,1536]{1,0:T(8,128)(2,1)} %get-tuple-element.15, bf16[63,1536]{1,0:T(8,128)(2,1)} %copy-done.6, bf16[193,1536]{1,0:T(8,128)(2,1)} %copy-done.3), kind=kOutput, calls=%fused_computation.2 | convolution fusion | flops 1211891712 | bytes 7077888 | tf_op jit(solution)/shard_map/dot_general | solution.py:24
  160.1 0.0 copy-start.2
  160.1 0.8 slice.35
  160.9 3.6 %collective-permute-start.1 = (bf16[63,1536]{1,0:T(8,128)(2,1)}, bf16[63,1536]{1,0:T(8,128)(2,1)}, u32[]{:S(2)}, u32[]{:S(2)}) collective-permute-start(bf16[63,1536]{1,0:T(8,128)(2,1)} %slice.35), channel_id=1, source_target_pairs={{0,1},{1,2},{2,3},{3,4},{4,5},{5,6},{6,7},{7,8},{8,9},{9,10},{10,1... | collective-permute-start | bytes 580616 | tf_op jit(solution)/shard_map/ppermute | solution.py:461
  164.5 27.8 %all-to-all-done.3 = bf16[64,24,896]{2,1,0:T(8,128)(2,1)S(1)} async-done(((bf16[64,24,896]{2,1,0:T(8,128)(2,1)}), bf16[64,24,896]{2,1,0:T(8,128)(2,1)S(1)}, u32[]{:S(2)}, u32[]{:S(2)}) %all-to-all-start.3) | async-done | bytes 2752544 | tf_op jit(solution)/shard_map/all_to_all | solution.py:378
  192.4 1.0 reduce_sum.32
  193.4 1.5 broadcast_in_dim.20
  194.9 4.7 %all-to-all-start.4 = ((bf16[8,24,896]{2,1,0:T(8,128)(2,1)}), bf16[8,24,896]{2,1,0:T(8,128)(2,1)S(1)}, u32[]{:S(2)}, u32[]{:S(2)}) async-start(bf16[8,24,896]{2,1,0:T(8,128)(2,1)} %broadcast_in_dim.20), calls=%async_computation.4 | async-start | bytes 688128 | tf_op jit(solution)/shard_map/all_to_all | solution.py:378
  199.7 0.0 collective-permute-done.1
  199.7 1.0 slice_select_fusion
  200.6 1.0 pad_maximum_fusion.1
  201.7 5.3 %all-to-all-done.4 = bf16[8,24,896]{2,1,0:T(8,128)(2,1)S(1)} async-done(((bf16[8,24,896]{2,1,0:T(8,128)(2,1)}), bf16[8,24,896]{2,1,0:T(8,128)(2,1)S(1)}, u32[]{:S(2)}, u32[]{:S(2)}) %all-to-all-start.4) | async-done | bytes 344096 | tf_op jit(solution)/shard_map/all_to_all | solution.py:378
  206.9 0.9 bitcast_convert_fusion
  (16 shorter events, 0.0 us)
Async XLA Ops:
  7.3 45.1 %all-to-all-start = ((bf16[16,85,8,128]{3,2,1,0:T(8,128)(2,1)}), bf16[16,85,8,128]{3,2,1,0:T(8,128)(2,1)S(1)}, u32[]{:S(2)}, u32[]{:S(2)}) async-start(bf16[16,85,8,128]{3,2,1,0:T(8,128)(2,1)} %get-tuple-element.13), calls=%async_computation | async-start | bytes 5570560 | tf_op jit(solution)/shard_map/all_to_all | solution.py:378
  15.9 48.7 %collective-permute-start = (bf16[2,64,1536]{2,1,0:T(8,128)(2,1)}, bf16[2,64,1536]{2,1,0:T(8,128)(2,1)}, u32[]{:S(2)}, u32[]{:S(2)}) collective-permute-start(bf16[2,64,1536]{2,1,0:T(8,128)(2,1)} %get-tuple-element.12), channel_id=1, source_target_pairs={{1,0},{2,1},{3,2},{4,3},{5,4},{6,5},{7,6},{8,7},{9,8},{10,9},{11,1... | collective-permute-start | bytes 1179656 | tf_op jit(solution)/shard_map/ppermute | solution.py:413
  17.2 1.3 copy-start.1
  18.5 47.4 %copy-start.3 = (bf16[193,1536]{1,0:T(8,128)(2,1)}, bf16[193,1536]{1,0:T(8,128)(2,1)S(1)}, u32[]{:S(2)}) copy-start(bf16[193,1536]{1,0:T(8,128)(2,1)S(1)} %slice.25) | copy-start | bytes 1778692
  52.4 1.6 copy-start
  58.1 7.8 %copy-start.8 = (f32[1536]{0:T(1024)S(1)}, f32[1536]{0:T(1024)}, u32[]{:S(2)}) copy-start(f32[1536]{0:T(1024)} %param.21) | copy-start | bytes 18436
  58.1 17.9 %all-to-all-start.2 = ((bf16[16,28,8,128]{3,2,1,0:T(8,128)(2,1)}), bf16[16,28,8,128]{3,2,1,0:T(8,128)(2,1)S(1)}, u32[]{:S(2)}, u32[]{:S(2)}) async-start(bf16[16,28,8,128]{3,2,1,0:T(8,128)(2,1)} %get-tuple-element.16), calls=%async_computation.2 | async-start | bytes 1835008 | tf_op jit(solution)/shard_map/all_to_all | solution.py:378
  65.6 5.0 %copy-start.6 = (bf16[63,1536]{1,0:T(8,128)(2,1)}, bf16[63,1536]{1,0:T(8,128)(2,1)S(1)}, u32[]{:S(2)}) copy-start(bf16[63,1536]{1,0:T(8,128)(2,1)S(1)} %get-tuple-element.23) | copy-start | bytes 580612
  70.6 9.4 %copy-start.7 = (bf16[193,1536]{1,0:T(8,128)(2,1)S(1)}, bf16[193,1536]{1,0:T(8,128)(2,1)}, u32[]{:S(2)}) copy-start(bf16[193,1536]{1,0:T(8,128)(2,1)} %slice.28) | copy-start | bytes 1778692
  75.9 8.7 %copy-start.4 = (bf16[16,28,8,128]{3,2,1,0:T(8,128)(2,1)}, bf16[16,28,8,128]{3,2,1,0:T(8,128)(2,1)S(1)}, u32[]{:S(2)}) copy-start(bf16[16,28,8,128]{3,2,1,0:T(8,128)(2,1)S(1)} %all-to-all-done.2.pieces_ref) | copy-start | bytes 2752516
  75.9 27.6 %all-to-all-start.1 = ((bf16[16,28,8,128]{3,2,1,0:T(8,128)(2,1)}), bf16[16,28,8,128]{3,2,1,0:T(8,128)(2,1)S(1)}, u32[]{:S(2)}, u32[]{:S(2)}) async-start(bf16[16,28,8,128]{3,2,1,0:T(8,128)(2,1)} %get-tuple-element.14), calls=%async_computation.1 | async-start | bytes 1835008 | tf_op jit(solution)/shard_map/all_to_all | solution.py:378
  103.5 0.9 copy-start.5
  130.1 11.8 %collective-permute-start.2 = (bf16[1536,896]{1,0:T(8,128)(2,1)}, bf16[1536,896]{1,0:T(8,128)(2,1)S(1)}, u32[]{:S(2)}, u32[]{:S(2)}) collective-permute-start(bf16[1536,896]{1,0:T(8,128)(2,1)} %weight_half.3), channel_id=1, source_target_pairs={{0,16},{16,0},{32,48},{48,32},{64,80},{80,64},{96,112},{112,96},{1... | collective-permute-start | bytes 8257544 | tf_op jit(solution)/shard_map/ppermute | solution.py:446
  145.9 46.5 %all-to-all-start.3 = ((bf16[64,24,896]{2,1,0:T(8,128)(2,1)}), bf16[64,24,896]{2,1,0:T(8,128)(2,1)S(1)}, u32[]{:S(2)}, u32[]{:S(2)}) async-start(bf16[64,24,896]{2,1,0:T(8,128)(2,1)} %bitcast.15), calls=%async_computation.3 | async-start | bytes 5505024 | tf_op jit(solution)/shard_map/all_to_all | solution.py:378
  160.1 33.3 %copy-start.2 = (bf16[256,1536]{1,0:T(8,128)(2,1)}, bf16[256,1536]{1,0:T(8,128)(2,1)S(1)}, u32[]{:S(2)}) copy-start(bf16[256,1536]{1,0:T(8,128)(2,1)S(1)} %fusion) | copy-start | bytes 2359300
  160.9 38.7 %collective-permute-start.1 = (bf16[63,1536]{1,0:T(8,128)(2,1)}, bf16[63,1536]{1,0:T(8,128)(2,1)}, u32[]{:S(2)}, u32[]{:S(2)}) collective-permute-start(bf16[63,1536]{1,0:T(8,128)(2,1)} %slice.35), channel_id=1, source_target_pairs={{0,1},{1,2},{2,3},{3,4},{4,5},{5,6},{6,7},{7,8},{8,9},{9,10},{10,1... | collective-permute-start | bytes 580616 | tf_op jit(solution)/shard_map/ppermute | solution.py:461
  194.9 5.7 %slice-start = ((bf16[256,1536]{1,0:T(8,128)(2,1)}), bf16[193,1536]{1,0:T(8,128)(2,1)S(1)}, s32[]{:S(2)}) async-start(bf16[256,1536]{1,0:T(8,128)(2,1)} %copy-done.2), calls=%async_computation.5 | async-start | bytes 1228800 | tf_op jit(solution)/shard_map/slice | solution.py:463
  194.9 12.0 %all-to-all-start.4 = ((bf16[8,24,896]{2,1,0:T(8,128)(2,1)}), bf16[8,24,896]{2,1,0:T(8,128)(2,1)S(1)}, u32[]{:S(2)}, u32[]{:S(2)}) async-start(bf16[8,24,896]{2,1,0:T(8,128)(2,1)} %broadcast_in_dim.20), calls=%async_computation.4 | async-start | bytes 688128 | tf_op jit(solution)/shard_map/all_to_all | solution.py:378

commit v2 on v1

--- a/solution.py
+++ b/solution.py
@@ -33,51 +33,63 @@
     )
 
 
-def spread_kernel(blocks_ref, notes_ref, hidden_ref, cotangent_ref, slices_ref, tails_ref):
-    blocks, _, feature = blocks_ref.shape
+def spread_kernel(home_ref, neighbours_ref, blocks_hbm, hidden_ref, cotangent_ref, slices_ref, tails_ref, blocks_ref, sems):
+    blocks, length, feature = blocks_ref.shape
     devices, units, rows, _ = slices_ref.shape
     tiles = feature // HEAD
+    parts = sems.shape[0]
+    size = length // parts
+
+    def load(part):
+        part_rows = pl.ds(part * size, size)
+        return pltpu.make_async_copy(
+            blocks_hbm.at[:, part_rows], blocks_ref.at[:, part_rows], sems.at[part]
+        )
+
+    for part in range(parts):
+        load(part).start()
+    lane = lax.broadcasted_iota(jnp.int32, (rows, HEAD), 1)
+    notes = jnp.zeros((rows, HEAD), jnp.int32)
+    spans, each = neighbours_ref.shape
+    for u in range(spans):
+        for n in range(each):
+            notes = jnp.where(lane == u * each + n, home_ref[neighbours_ref[u, n]], notes)
+    notes = notes.astype(F32).astype(BF16)
+    tails_ref[0] = hidden_ref[...]
+    tails_ref[1] = cotangent_ref[...]
     for d in range(devices):
+        if d % (devices // parts) == 0:
+            load(d // (devices // parts)).wait()
         for b in range(blocks):
             for k in range(tiles):
                 slices_ref[d, b * tiles + k] = blocks_ref[
                     b, d * rows : (d + 1) * rows, k * HEAD : (k + 1) * HEAD
                 ]
-        slices_ref[d, units - 1] = notes_ref[...]
-
-    @pl.when(pl.program_id(0) == 0)
-    def _():
-        tails_ref[0] = hidden_ref[...]
-        tails_ref[1] = cotangent_ref[...]
-
-
-def spread(database, notes, hidden, cotangent, devices):
+        slices_ref[d, units - 1] = notes
+
+
+def spread(block_home, neighbours, database, hidden, cotangent, devices):
     blocks, length, feature = database.shape
     width = hidden.shape[1]
     units = blocks * (feature // HEAD) + 1
     rows = length // devices
-    step = 4
+    smem = pl.BlockSpec(memory_space=pltpu.SMEM)
+    first = pl.BlockSpec((SPAN, width), lambda i: (0, 0))
+    whole = pl.BlockSpec(memory_space=VMEM)
     return pl.pallas_call(
         spread_kernel,
-        grid=(devices // step,),
+        grid=(1,),
         out_shape=(
             jax.ShapeDtypeStruct((devices, units, rows, HEAD), BF16),
             jax.ShapeDtypeStruct((2, SPAN, width), BF16),
         ),
-        in_specs=[
-            pl.BlockSpec((blocks, step * rows, feature), lambda i: (0, i, 0)),
-            pl.BlockSpec((rows, HEAD), lambda i: (0, 0)),
-            pl.BlockSpec((SPAN, width), lambda i: (0, 0)),
-            pl.BlockSpec((SPAN, width), lambda i: (0, 0)),
-        ],
-        out_specs=(
-            pl.BlockSpec((step, units, rows, HEAD), lambda i: (i, 0, 0, 0)),
-            pl.BlockSpec((2, SPAN, width), lambda i: (0, 0, 0)),
-        ),
+        in_specs=[smem, smem, pl.BlockSpec(memory_space=pltpu.HBM), first, first],
+        out_specs=(whole, whole),
+        scratch_shapes=[VMEM(database.shape, BF16), pltpu.SemaphoreType.DMA((4,))],
         cost_estimate=pl.CostEstimate(flops=1 << 20, bytes_accessed=6 << 20, transcendentals=0),
         compiler_params=pltpu.CompilerParams(vmem_limit_bytes=60 << 20),
         name="spread",
-    )(database, notes, hidden, cotangent)
+    )(block_home, neighbours, database, hidden, cotangent)
 
 
 def pick_kernel(tiles, where_ref, table_ref, *outs):
@@ -151,29 +163,24 @@
     keys = K * length
     scale = HEAD ** (-0.5)
     chunk = 2 * width // (slices * 8)
-    tile = 512
-    steps = (3 * feature) // tile
-    rest = pl.ds(steps * tile, 3 * feature - steps * tile)
-    wide_steps = 2 * width // tile
-
-    def load(columns, index):
+    tile = 1024
+    narrow = range(0, 3 * feature, tile)
+    wide = range(0, 2 * width, tile)
+
+    def load(j):
+        columns = pl.ds(narrow[j], min(tile, 3 * feature - narrow[j]))
         return pltpu.make_async_copy(
-            projection_hbm.at[:, columns], projection_ref.at[:, columns], sems.at[index]
+            projection_hbm.at[:, columns], projection_ref.at[:, columns], sems.at[j]
         )
 
-    def wide_load(columns, index):
+    def wide_load(j):
+        columns = pl.ds(wide[j], tile)
         return pltpu.make_async_copy(
-            keyvalue_hbm.at[columns], keyvalue_ref.at[columns], sems.at[steps + 2 + index]
+            keyvalue_hbm.at[columns], keyvalue_ref.at[columns], sems.at[len(narrow) + 1 + j]
         )
 
-    output_load = pltpu.make_async_copy(output_hbm, output_ref, sems.at[steps + 1])
-    for j in range(steps):
-        load(pl.ds(j * tile, tile), j).start()
-    load(rest, steps).start()
-    output_load.start()
-    for j in range(wide_steps):
-        wide_load(pl.ds(j * tile, tile), j).start()
-
+    output_load = pltpu.make_async_copy(output_hbm, output_ref, sems.at[len(narrow)])
+    load(0).start()
     gain = gain_ref[...].reshape(1, feature)
     for b in range(blocks):
         block_rows = slice(b * length, (b + 1) * length)
@@ -183,14 +190,17 @@
             )
         normed_ref[block_rows] = rms_norm(plain_ref[block_rows], gain).astype(BF16)
 
-    @pl.loop(0, steps)
-    def _(j):
-        columns = pl.ds(pl.multiple_of(j * tile, tile), tile)
-        load(columns, j).wait()
+    for j in range(1, len(narrow)):
+        load(j).start()
+    for j in range(len(narrow)):
+        load(j).wait()
+        if j == 0:
+            output_load.start()
+        if j == 1:
+            for i in range(len(wide)):
+                wide_load(i).start()
+        columns = slice(narrow[j], min(narrow[j] + tile, 3 * feature))
         qkv_ref[:, columns] = dot(normed_ref[...], projection_ref[:, columns], NN).astype(BF16)
-
-    load(rest, steps).wait()
-    qkv_ref[:, rest] = dot(normed_ref[...], projection_ref[:, rest], NN).astype(BF16)
 
     together = 2
     ones = jnp.ones((length, HEAD), BF16)
@@ -223,10 +233,9 @@
             plain_ref[:, columns] + dot(mixed_ref[...], output_ref[:, columns], NN)
         ).astype(BF16)
 
-    @pl.loop(0, wide_steps)
-    def _(j):
-        columns = pl.ds(pl.multiple_of(j * tile, tile), tile)
-        wide_load(columns, j).wait()
+    for j in range(len(wide)):
+        wide_load(j).wait()
+        columns = slice(wide[j], wide[j] + tile)
         kv_ref[:, columns] = dot(encoded_ref[...], keyvalue_ref[columns, :], NT).astype(BF16)
 
     key_block = lax.broadcasted_iota(jnp.int32, (1, keys), 1) // length
@@ -328,14 +337,14 @@
             VMEM((heads, SPAN, keys), F32),
             VMEM((heads, SPAN, keys), BF16),
             VMEM((heads, SPAN, keys), BF16),
-            pltpu.SemaphoreType.DMA((3 * feature // 512 + 2 + 2 * width // 512,)),
+            pltpu.SemaphoreType.DMA((pl.cdiv(3 * feature, 1024) + 1 + 2 * width // 1024,)),
         ],
         cost_estimate=pl.CostEstimate(
             flops=total * feature * (8 * feature + 4 * width),
             bytes_accessed=20 << 20,
             transcendentals=1 << 20,
         ),
-        compiler_params=pltpu.CompilerParams(vmem_limit_bytes=60 << 20),
+        compiler_params=pltpu.CompilerParams(vmem_limit_bytes=(60, 54)[part] << 20),
         name="spans",
     )(counts, pieces, gain, projection, output, keyvalue, queries, grads)
 
@@ -364,14 +373,9 @@
         cost_estimate=pl.CostEstimate(
             flops=4 * rows * feature * keys, bytes_accessed=8 << 20, transcendentals=0
         ),
-        compiler_params=pltpu.CompilerParams(vmem_limit_bytes=60 << 20),
+        compiler_params=pltpu.CompilerParams(vmem_limit_bytes=24 << 20),
         name="weight_half",
     )(half, *grads, *encodeds)
-
-
-def locate(block_ids, block_home):
-    hits = block_ids[..., None] == jnp.arange(block_home.shape[0], dtype=jnp.int32)
-    return jnp.sum(jnp.where(hits, block_home, 0), axis=-1)
 
 
 def all_to_all(block, axis, groups=None):
@@ -400,16 +404,14 @@
     cotangent,
 ):
     token_count, _ = hidden.shape
-    _, length, feature = database.shape[1:]
+    _, _, feature = database.shape[1:]
     seq = lax.axis_size("seq")
     dp = lax.axis_size("dp")
     requests = neighbours.size
     tail = SPAN - 1
 
     tiles = feature // HEAD
-    where = locate(neighbours.reshape(-1), block_home)
-    notes = jnp.broadcast_to(jnp.pad(where, (0, HEAD - requests)), (length // seq, HEAD))
-    slices, tails = spread(database[0], notes.astype(BF16), hidden, cotangent, seq)
+    slices, tails = spread(block_home, neighbours, database[0], hidden, cotangent, seq)
     late = lax.ppermute(tails, "seq", [(i, i - 1) for i in range(1, seq)])
     late_hidden, late_cotangent = late[0, :tail], late[1, :tail]
     table = all_to_all(slices, "seq")

time: 209 us -> 205 us (0.981)
  Pallas kernels: 59.7 us -> 53.2 us
  local copies, waits for them, and re-layouts: 9.02 us -> 12.2 us
  other arithmetic: 9.7 us -> 7.13 us
    pallas_call x2, Pallas kernels: 13.6 us -> 7.53 us  [weight_half(): pl.pallas_call(weight_kernel, grid_spec=pltpu.PrefetchScalarGridSpec(num_...]
    unnamed x19 -> x25, local copies, waits for them, and re-layouts: 2.65 us -> 6.51 us
  transfers between devices with their start and end apart: 8 -> 8, of which waited for: 4 -> 5; matrix products, arithmetic and copies ran while one was open for 11% -> 11% of each run, Pallas kernels for 14% -> 13%
where the time goes in v2:
time: 205 us; the launch traced here: 203 us
  waiting for transfers between devices  70.9 us (35%)
  Pallas kernels  53.2 us (26%)
  starting transfers between devices  45.7 us (22%)
  matrix products  13.4 us (7%)
  local copies, waits for them, and re-layouts  12.2 us (6%)
  other arithmetic  7.13 us (3%)
    all_to_all x5, waiting for transfers between devices, all_to_all(): lax.all_to_all(block, axis, split_axis=0, concat_axis=0, tiled=True, axis...  69.9 us
    pallas_call x2, Pallas kernels, span_step(): pl.pallas_call(functools.partial(span_kernel, part * spans), grid=(1,), o...  37.1 us
    all_to_all x5, starting transfers between devices, all_to_all(): lax.all_to_all(block, axis, split_axis=0, concat_axis=0, tiled=True, axis...  35.4 us
    dot_general x3, matrix products, dot(): return lax.dot_general(a, b, dims, preferred_element_type=F32)  13.4 us
    pallas_call x2, Pallas kernels, weight_half(): pl.pallas_call(weight_kernel, grid_spec=pltpu.PrefetchScalarGridSpec(num_...  7.53 us
    unnamed x25, local copies, waits for them, and re-layouts  6.51 us
    ppermute x1, starting transfers between devices, local(): received = lax.ppermute(theirs, 'dp', [(i, i ^ 1) for i in range(dp)])  5.37 us
    pallas_call x1, Pallas kernels, spread(): pl.pallas_call(spread_kernel, grid=(1,), out_shape=(jax.ShapeDtypeStruct(...  4.45 us
  transfers between devices with their start and end apart: 8, of which 5 were waited for; matrix products, arithmetic and copies ran while one was open for 11% of the time, Pallas kernels for 13%

profile of v2, /device:TPU:1, one launch (start us, length us, event | category | flops | bytes accessed | tf_op | source)
XLA Modules:
  0.0 203.4 jit_solution(14329984465904939598)
XLA Ops:
  0.6 1.3 copy.18.neighbours_ref
  2.0 4.5 %spread.1 = (bf16[16,85,8,128]{3,2,1,0:T(8,128)(2,1)}, bf16[2,64,1536]{2,1,0:T(8,128)(2,1)}) custom-call(s32[192]{0:T(256)} %home_ref.1, s32[4,2]{1,0:T(4,128)} %copy.18.neighbours_ref, bf16[12,128,896]{2,1,0:T(8,128)(2,1)} %bitcast.16, bf16[256,1536]{1,0:T(8,128)(2,1)} %hidden_ref.1, bf16[256,1536]{1,0:T(8,128)(2,1)} %cotangent_ref.1), custom_call_target="tpu_custom_call" | custom-call | flops 1048576 | bytes 6291456 | tf_op jit(solution)/shard_map/spread/pallas_call | solution.py:79
  6.4 8.6 %all-to-all-start = ((bf16[16,85,8,128]{3,2,1,0:T(8,128)(2,1)}), bf16[16,85,8,128]{3,2,1,0:T(8,128)(2,1)S(1)}, u32[]{:S(2)}, u32[]{:S(2)}) async-start(bf16[16,85,8,128]{3,2,1,0:T(8,128)(2,1)} %get-tuple-element.13), calls=%async_computation | async-start | bytes 5570560 | tf_op jit(solution)/shard_map/all_to_all | solution.py:382
  15.0 1.3 collective-permute-start
  16.3 0.0 copy-start.5
  16.4 1.3 slice.25
  17.6 0.0 copy-done.5
  17.7 1.0 slice.28
  18.7 32.8 %all-to-all-done.table_ref = bf16[16,85,8,128]{3,2,1,0:T(8,128)(2,1)S(1)} async-done(((bf16[16,85,8,128]{3,2,1,0:T(8,128)(2,1)}), bf16[16,85,8,128]{3,2,1,0:T(8,128)(2,1)S(1)}, u32[]{:S(2)}, u32[]{:S(2)}) %all-to-all-start) | async-done | bytes 2785312 | tf_op jit(solution)/shard_map/all_to_all | solution.py:382
  51.5 0.7 slice_convert_fusion
  52.2 0.9 copy-done.4
  53.1 4.1 %pick.1 = (bf16[16,28,8,128]{3,2,1,0:T(8,128)(2,1)}, bf16[16,28,8,128]{3,2,1,0:T(8,128)(2,1)}) custom-call(s32[16,8]{1,0:T(8,128)} %bitcast.17, bf16[16,85,8,128]{3,2,1,0:T(8,128)(2,1)} %copy-done.4), custom_call_target="tpu_custom_call" | custom-call | tf_op jit(solution)/shard_map/pick/pallas_call | solution.py:116
  57.2 6.5 %all-to-all-start.2 = ((bf16[16,28,8,128]{3,2,1,0:T(8,128)(2,1)}), bf16[16,28,8,128]{3,2,1,0:T(8,128)(2,1)S(1)}, u32[]{:S(2)}, u32[]{:S(2)}) async-start(bf16[16,28,8,128]{3,2,1,0:T(8,128)(2,1)} %get-tuple-element.16), calls=%async_computation.2 | async-start | bytes 1835008 | tf_op jit(solution)/shard_map/all_to_all | solution.py:382
  63.6 0.0 collective-permute-done
  63.7 1.0 slice_bitcast_fusion
  64.7 0.0 copy-start.9
  64.7 0.3 fusion.1
  65.0 4.6 %convolution_convert_fusion.1.queries_ref = bf16[256,1536]{1,0:T(8,128)(2,1)} fusion(bf16[1536,1536]{1,0:T(8,128)(2,1)} %param.22, f32[1536]{0:T(1024)S(1)} %copy-done.11, f32[256]{0:T(256)S(1)} %add_rsqrt_fusion, bf16[63,1536]{1,0:T(8,128)(2,1)S(1)} %get-tuple-element.23, bf16[193,1536]{1,0:T(8,128)(2,1)S(1)} %slice.25), kind=kOutput, calls=%fused_computation.4 | convolution fusion | flops 1211105280 | bytes 6298624 | tf_op jit(solution)/shard_map/dot_general | solution.py:24
  69.7 0.0 copy-done.9
  69.7 5.4 %all-to-all-done.2.pieces_ref = bf16[16,28,8,128]{3,2,1,0:T(8,128)(2,1)S(1)} async-done(((bf16[16,28,8,128]{3,2,1,0:T(8,128)(2,1)}), bf16[16,28,8,128]{3,2,1,0:T(8,128)(2,1)S(1)}, u32[]{:S(2)}, u32[]{:S(2)}) %all-to-all-start.2) | async-done | bytes 917536 | tf_op jit(solution)/shard_map/all_to_all | solution.py:382
  75.0 4.5 %all-to-all-start.1 = ((bf16[16,28,8,128]{3,2,1,0:T(8,128)(2,1)}), bf16[16,28,8,128]{3,2,1,0:T(8,128)(2,1)}, u32[]{:S(2)}, u32[]{:S(2)}) async-start(bf16[16,28,8,128]{3,2,1,0:T(8,128)(2,1)} %get-tuple-element.14), calls=%async_computation.1 | async-start | bytes 1835008 | tf_op jit(solution)/shard_map/all_to_all | solution.py:382
  79.5 4.6 %convolution_convert_fusion.grads_ref = bf16[256,1536]{1,0:T(8,128)(2,1)} fusion(bf16[1536,1536]{1,0:T(8,128)(2,1)} %param.24, bf16[63,1536]{1,0:T(8,128)(2,1)S(1)} %get-tuple-element.22, bf16[193,1536]{1,0:T(8,128)(2,1)S(1)} %copy-done.10), kind=kOutput, calls=%fused_computation.3 | convolution fusion | flops 1209925632 | bytes 6291456 | tf_op jit(solution)/shard_map/dot_general | solution.py:24
  84.2 18.4 %spans.3 = (bf16[512,896]{1,0:T(8,128)(2,1)}, bf16[2,1536,512]{2,1,0:T(8,128)(2,1)}, bf16[128,1536]{1,0:T(8,128)(2,1)}) custom-call(s32[4]{0:T(128)} %counts_ref.3, bf16[16,28,8,128]{3,2,1,0:T(8,128)(2,1)} %copy-done.8, f32[896]{0:T(1024)} %gain_ref.3, bf16[896,2688]{1,0:T(8,128)(2,1)} %projection_hbm.3, bf16[896,896]{1,0:T(8,128)(2,1)} %output_hbm.3, ...), custom_call_target="tpu_custom_call" | custom-call | flops 6106906624 | bytes 20971520 | tf_op jit(solution)/shard_map/spans/pallas_call | solution.py:306
  102.6 0.0 all-to-all-done.1.pieces_ref
  102.6 18.8 %spans.2 = (bf16[512,896]{1,0:T(8,128)(2,1)}, bf16[2,1536,512]{2,1,0:T(8,128)(2,1)}, bf16[128,1536]{1,0:T(8,128)(2,1)}) custom-call(s32[4]{0:T(128)} %counts_ref.3, bf16[16,28,8,128]{3,2,1,0:T(8,128)(2,1)} %all-to-all-done.1.pieces_ref, f32[896]{0:T(1024)} %gain_ref.3, bf16[896,2688]{1,0:T(8,128)(2,1)} %projection_hbm.3, bf16[896,896]{1,0:T(8,128)(2,1)} %output_hbm.3, ...), custom_call_target="tpu_custom_call" | custom-call | flops 6106906624 | bytes 20971520 | tf_op jit(solution)/shard_map/spans/pallas_call | solution.py:306
  121.4 1.9 copy-done.1
  123.2 1.2 copy-done.2
  124.4 1.2 copy-done.3
  125.6 3.8 %weight_half.3 = bf16[1536,896]{1,0:T(8,128)(2,1)S(1)} custom-call(s32[1]{0:T(128)} %bitcast.5.half_ref, bf16[2,1536,512]{2,1,0:T(8,128)(2,1)S(1)} %copy-done.1, bf16[2,1536,512]{2,1,0:T(8,128)(2,1)S(1)} %copy-done, bf16[512,896]{1,0:T(8,128)(2,1)S(1)} %copy-done.3, bf16[512,896]{1,0:T(8,128)(2,1)S(1)} %copy-done.2), custom_call_target="tpu_custom_call" | custom-call | flops 2818572288 | bytes 8388608 | tf_op jit(solution)/shard_map/weight_half/pallas_call | solution.py:364
  129.4 5.4 %collective-permute-start.2 = (bf16[1536,896]{1,0:T(8,128)(2,1)S(1)}, bf16[1536,896]{1,0:T(8,128)(2,1)S(1)}, u32[]{:S(2)}, u32[]{:S(2)}) collective-permute-start(bf16[1536,896]{1,0:T(8,128)(2,1)S(1)} %weight_half.3), channel_id=1, source_target_pairs={{0,16},{16,0},{32,48},{48,32},{64,80},{80,64},{96,112},{112,96},{1... | collective-permute-start | bytes 8257544 | tf_op jit(solution)/shard_map/ppermute | solution.py:448
  134.7 3.8 %weight_half.2 = bf16[1536,896]{1,0:T(8,128)(2,1)S(1)} custom-call(s32[1]{0:T(128)} %bitcast.4.half_ref, bf16[2,1536,512]{2,1,0:T(8,128)(2,1)S(1)} %copy-done.1, bf16[2,1536,512]{2,1,0:T(8,128)(2,1)S(1)} %copy-done, bf16[512,896]{1,0:T(8,128)(2,1)S(1)} %copy-done.3, bf16[512,896]{1,0:T(8,128)(2,1)S(1)} %copy-done.2), custom_call_target="tpu_custom_call" | custom-call | flops 2818572288 | bytes 8388608 | tf_op jit(solution)/shard_map/weight_half/pallas_call | solution.py:364
  138.5 1.0 collective-permute-done.2
  139.5 2.3 %add_convert_fusion = bf16[1536,896]{1,0:T(8,128)(2,1)} fusion(bf16[1536,896]{1,0:T(8,128)(2,1)S(1)} %collective-permute-done.2, bf16[1536,896]{1,0:T(8,128)(2,1)S(1)} %weight_half.2), kind=kLoop, calls=%fused_computation | loop fusion | flops 5505024 | bytes 8257536 | tf_op jit(solution)/shard_map/convert_element_type | solution.py:450
  141.7 10.0 %all-to-all-start.3 = ((bf16[64,24,896]{2,1,0:T(8,128)(2,1)}), bf16[64,24,896]{2,1,0:T(8,128)(2,1)S(1)}, u32[]{:S(2)}, u32[]{:S(2)}) async-start(bf16[64,24,896]{2,1,0:T(8,128)(2,1)} %bitcast.15), calls=%async_computation.3 | async-start | bytes 5505024 | tf_op jit(solution)/shard_map/all_to_all | solution.py:382
  151.7 4.1 %fusion = bf16[256,1536]{1,0:T(8,128)(2,1)S(1)} fusion(bf16[1536,1536]{1,0:T(8,128)(2,1)} %param.24, bf16[128,1536]{1,0:T(8,128)(2,1)} %get-tuple-element.17, bf16[128,1536]{1,0:T(8,128)(2,1)} %get-tuple-element.15, bf16[63,1536]{1,0:T(8,128)(2,1)} %copy-done.9, bf16[193,1536]{1,0:T(8,128)(2,1)} %copy-done.7), kind=kOutput, calls=%fused_computation.2 | convolution fusion | flops 1211891712 | bytes 7077888 | tf_op jit(solution)/shard_map/dot_general | solution.py:24
  155.9 0.0 copy-start.6
  155.9 0.8 slice.35
  156.7 3.6 %collective-permute-start.1 = (bf16[63,1536]{1,0:T(8,128)(2,1)}, bf16[63,1536]{1,0:T(8,128)(2,1)}, u32[]{:S(2)}, u32[]{:S(2)}) collective-permute-start(bf16[63,1536]{1,0:T(8,128)(2,1)} %slice.35), channel_id=1, source_target_pairs={{0,1},{1,2},{2,3},{3,4},{4,5},{5,6},{6,7},{7,8},{8,9},{9,10},{10,1... | collective-permute-start | bytes 580616 | tf_op jit(solution)/shard_map/ppermute | solution.py:463
  160.3 26.5 %all-to-all-done.3 = bf16[64,24,896]{2,1,0:T(8,128)(2,1)S(1)} async-done(((bf16[64,24,896]{2,1,0:T(8,128)(2,1)}), bf16[64,24,896]{2,1,0:T(8,128)(2,1)S(1)}, u32[]{:S(2)}, u32[]{:S(2)}) %all-to-all-start.3) | async-done | bytes 2752544 | tf_op jit(solution)/shard_map/all_to_all | solution.py:382
  186.8 1.0 reduce_sum.22
  187.8 1.5 broadcast_in_dim.2
  189.3 5.8 %all-to-all-start.4 = ((bf16[8,24,896]{2,1,0:T(8,128)(2,1)}), bf16[8,24,896]{2,1,0:T(8,128)(2,1)S(1)}, u32[]{:S(2)}, u32[]{:S(2)}) async-start(bf16[8,24,896]{2,1,0:T(8,128)(2,1)} %broadcast_in_dim.2), calls=%async_computation.4 | async-start | bytes 688128 | tf_op jit(solution)/shard_map/all_to_all | solution.py:382
  195.2 0.0 collective-permute-done.1
  195.2 1.0 slice_select_fusion
  196.1 0.0 slice-done
  196.1 1.0 pad_maximum_fusion.1
  197.2 5.3 %all-to-all-done.4 = bf16[8,24,896]{2,1,0:T(8,128)(2,1)S(1)} async-done(((bf16[8,24,896]{2,1,0:T(8,128)(2,1)}), bf16[8,24,896]{2,1,0:T(8,128)(2,1)S(1)}, u32[]{:S(2)}, u32[]{:S(2)}) %all-to-all-start.4) | async-done | bytes 344096 | tf_op jit(solution)/shard_map/all_to_all | solution.py:382
  202.4 0.9 bitcast_convert_fusion
  (17 shorter events, 0.0 us)
Async XLA Ops:
  6.4 45.1 %all-to-all-start = ((bf16[16,85,8,128]{3,2,1,0:T(8,128)(2,1)}), bf16[16,85,8,128]{3,2,1,0:T(8,128)(2,1)S(1)}, u32[]{:S(2)}, u32[]{:S(2)}) async-start(bf16[16,85,8,128]{3,2,1,0:T(8,128)(2,1)} %get-tuple-element.13), calls=%async_computation | async-start | bytes 5570560 | tf_op jit(solution)/shard_map/all_to_all | solution.py:382
  15.0 48.6 %collective-permute-start = (bf16[2,64,1536]{2,1,0:T(8,128)(2,1)}, bf16[2,64,1536]{2,1,0:T(8,128)(2,1)}, u32[]{:S(2)}, u32[]{:S(2)}) collective-permute-start(bf16[2,64,1536]{2,1,0:T(8,128)(2,1)} %get-tuple-element.12), channel_id=1, source_target_pairs={{1,0},{2,1},{3,2},{4,3},{5,4},{6,5},{7,6},{8,7},{9,8},{10,9},{11,1... | collective-permute-start | bytes 1179656 | tf_op jit(solution)/shard_map/ppermute | solution.py:415
  16.3 1.3 copy-start.5
  17.7 47.3 %copy-start.7 = (bf16[193,1536]{1,0:T(8,128)(2,1)}, bf16[193,1536]{1,0:T(8,128)(2,1)S(1)}, u32[]{:S(2)}) copy-start(bf16[193,1536]{1,0:T(8,128)(2,1)S(1)} %slice.25) | copy-start | bytes 1778692
  51.5 1.5 copy-start.4
  57.2 7.8 %copy-start.11 = (f32[1536]{0:T(1024)S(1)}, f32[1536]{0:T(1024)}, u32[]{:S(2)}) copy-start(f32[1536]{0:T(1024)} %param.21) | copy-start | bytes 18436
  57.2 17.9 %all-to-all-start.2 = ((bf16[16,28,8,128]{3,2,1,0:T(8,128)(2,1)}), bf16[16,28,8,128]{3,2,1,0:T(8,128)(2,1)S(1)}, u32[]{:S(2)}, u32[]{:S(2)}) async-start(bf16[16,28,8,128]{3,2,1,0:T(8,128)(2,1)} %get-tuple-element.16), calls=%async_computation.2 | async-start | bytes 1835008 | tf_op jit(solution)/shard_map/all_to_all | solution.py:382
  64.7 5.0 %copy-start.9 = (bf16[63,1536]{1,0:T(8,128)(2,1)}, bf16[63,1536]{1,0:T(8,128)(2,1)S(1)}, u32[]{:S(2)}) copy-start(bf16[63,1536]{1,0:T(8,128)(2,1)S(1)} %get-tuple-element.23) | copy-start | bytes 580612
  69.7 9.9 %copy-start.10 = (bf16[193,1536]{1,0:T(8,128)(2,1)S(1)}, bf16[193,1536]{1,0:T(8,128)(2,1)}, u32[]{:S(2)}) copy-start(bf16[193,1536]{1,0:T(8,128)(2,1)} %slice.28) | copy-start | bytes 1778692
  75.0 9.2 %copy-start.8 = (bf16[16,28,8,128]{3,2,1,0:T(8,128)(2,1)}, bf16[16,28,8,128]{3,2,1,0:T(8,128)(2,1)S(1)}, u32[]{:S(2)}) copy-start(bf16[16,28,8,128]{3,2,1,0:T(8,128)(2,1)S(1)} %all-to-all-done.2.pieces_ref) | copy-start | bytes 2752516
  75.0 27.5 %all-to-all-start.1 = ((bf16[16,28,8,128]{3,2,1,0:T(8,128)(2,1)}), bf16[16,28,8,128]{3,2,1,0:T(8,128)(2,1)}, u32[]{:S(2)}, u32[]{:S(2)}) async-start(bf16[16,28,8,128]{3,2,1,0:T(8,128)(2,1)} %get-tuple-element.14), calls=%async_computation.1 | async-start | bytes 1835008 | tf_op jit(solution)/shard_map/all_to_all | solution.py:382
  102.6 18.8 %copy-start = (bf16[2,1536,512]{2,1,0:T(8,128)(2,1)S(1)}, bf16[2,1536,512]{2,1,0:T(8,128)(2,1)}, u32[]{:S(2)}) copy-start(bf16[2,1536,512]{2,1,0:T(8,128)(2,1)} %get-tuple-element.19.grad_b) | copy-start | bytes 9437188
  121.3 1.9 copy-start.1
  123.2 1.2 copy-start.2
  124.4 1.2 copy-start.3
  129.4 10.1 %collective-permute-start.2 = (bf16[1536,896]{1,0:T(8,128)(2,1)S(1)}, bf16[1536,896]{1,0:T(8,128)(2,1)S(1)}, u32[]{:S(2)}, u32[]{:S(2)}) collective-permute-start(bf16[1536,896]{1,0:T(8,128)(2,1)S(1)} %weight_half.3), channel_id=1, source_target_pairs={{0,16},{16,0},{32,48},{48,32},{64,80},{80,64},{96,112},{112,96},{1... | collective-permute-start | bytes 8257544 | tf_op jit(solution)/shard_map/ppermute | solution.py:448
  141.7 45.0 %all-to-all-start.3 = ((bf16[64,24,896]{2,1,0:T(8,128)(2,1)}), bf16[64,24,896]{2,1,0:T(8,128)(2,1)S(1)}, u32[]{:S(2)}, u32[]{:S(2)}) async-start(bf16[64,24,896]{2,1,0:T(8,128)(2,1)} %bitcast.15), calls=%async_computation.3 | async-start | bytes 5505024 | tf_op jit(solution)/shard_map/all_to_all | solution.py:382
  155.9 31.9 %copy-start.6 = (bf16[256,1536]{1,0:T(8,128)(2,1)}, bf16[256,1536]{1,0:T(8,128)(2,1)S(1)}, u32[]{:S(2)}) copy-start(bf16[256,1536]{1,0:T(8,128)(2,1)S(1)} %fusion) | copy-start | bytes 2359300
  156.7 38.5 %collective-permute-start.1 = (bf16[63,1536]{1,0:T(8,128)(2,1)}, bf16[63,1536]{1,0:T(8,128)(2,1)}, u32[]{:S(2)}, u32[]{:S(2)}) collective-permute-start(bf16[63,1536]{1,0:T(8,128)(2,1)} %slice.35), channel_id=1, source_target_pairs={{0,1},{1,2},{2,3},{3,4},{4,5},{5,6},{6,7},{7,8},{8,9},{9,10},{10,1... | collective-permute-start | bytes 580616 | tf_op jit(solution)/shard_map/ppermute | solution.py:463
  189.3 6.8 %slice-start = ((bf16[256,1536]{1,0:T(8,128)(2,1)}), bf16[193,1536]{1,0:T(8,128)(2,1)S(1)}, s32[]{:S(2)}) async-start(bf16[256,1536]{1,0:T(8,128)(2,1)} %copy-done.6), calls=%async_computation.5 | async-start | bytes 1228800 | tf_op jit(solution)/shard_map/slice | solution.py:465
  189.3 13.1 %all-to-all-start.4 = ((bf16[8,24,896]{2,1,0:T(8,128)(2,1)}), bf16[8,24,896]{2,1,0:T(8,128)(2,1)S(1)}, u32[]{:S(2)}, u32[]{:S(2)}) async-start(bf16[8,24,896]{2,1,0:T(8,128)(2,1)} %broadcast_in_dim.2), calls=%async_computation.4 | async-start | bytes 688128 | tf_op jit(solution)/shard_map/all_to_all | solution.py:382

commit v3 on v2

--- a/solution.py
+++ b/solution.py
@@ -33,7 +33,19 @@
     )
 
 
-def spread_kernel(home_ref, neighbours_ref, blocks_hbm, hidden_ref, cotangent_ref, slices_ref, tails_ref, blocks_ref, sems):
+def spread_kernel(
+    home_ref,
+    neighbours_ref,
+    blocks_hbm,
+    hidden_ref,
+    cotangent_ref,
+    slices_hbm,
+    tails_ref,
+    blocks_ref,
+    slices_ref,
+    sems,
+    out_sems,
+):
     blocks, length, feature = blocks_ref.shape
     devices, units, rows, _ = slices_ref.shape
     tiles = feature // HEAD
@@ -44,6 +56,12 @@
         part_rows = pl.ds(part * size, size)
         return pltpu.make_async_copy(
             blocks_hbm.at[:, part_rows], blocks_ref.at[:, part_rows], sems.at[part]
+        )
+
+    def store(part):
+        several = pl.ds(part * (devices // parts), devices // parts)
+        return pltpu.make_async_copy(
+            slices_ref.at[several], slices_hbm.at[several], out_sems.at[part]
         )
 
     for part in range(parts):
@@ -66,6 +84,10 @@
                     b, d * rows : (d + 1) * rows, k * HEAD : (k + 1) * HEAD
                 ]
         slices_ref[d, units - 1] = notes
+        if (d + 1) % (devices // parts) == 0:
+            store(d // (devices // parts)).start()
+    for part in range(parts):
+        store(part).wait()
 
 
 def spread(block_home, neighbours, database, hidden, cotangent, devices):
@@ -84,48 +106,49 @@
             jax.ShapeDtypeStruct((2, SPAN, width), BF16),
         ),
         in_specs=[smem, smem, pl.BlockSpec(memory_space=pltpu.HBM), first, first],
-        out_specs=(whole, whole),
-        scratch_shapes=[VMEM(database.shape, BF16), pltpu.SemaphoreType.DMA((4,))],
+        out_specs=(pl.BlockSpec(memory_space=pltpu.HBM), whole),
+        scratch_shapes=[
+            VMEM(database.shape, BF16),
+            VMEM((devices, units, rows, HEAD), BF16),
+            pltpu.SemaphoreType.DMA((4,)),
+            pltpu.SemaphoreType.DMA((4,)),
+        ],
         cost_estimate=pl.CostEstimate(flops=1 << 20, bytes_accessed=6 << 20, transcendentals=0),
         compiler_params=pltpu.CompilerParams(vmem_limit_bytes=60 << 20),
         name="spread",
     )(block_home, neighbours, database, hidden, cotangent)
 
 
-def pick_kernel(tiles, where_ref, table_ref, *outs):
+def pick_kernel(tiles, where_ref, table_ref, out_ref):
     blocks = table_ref.shape[1] // tiles
 
-    @pl.loop(0, outs[0].shape[0])
+    @pl.loop(0, out_ref.shape[0])
     def _(r):
-        first = 0
-        for out in outs:
-            for i in range(out.shape[1] // tiles):
-                where = where_ref[r, first + i]
-                start = (where % blocks) * tiles
-                out[r, i * tiles : (i + 1) * tiles] = table_ref[
-                    where // blocks, pl.ds(start, tiles)
-                ]
-            first += out.shape[1] // tiles
-
-
-def pick(where, table, tiles, chunks):
+        for i in range(out_ref.shape[1] // tiles):
+            where = where_ref[r, i]
+            start = (where % blocks) * tiles
+            out_ref[r, i * tiles : (i + 1) * tiles] = table_ref[
+                where // blocks, pl.ds(start, tiles)
+            ]
+
+
+def pick(where, table, tiles):
     readers, requests = where.shape
     rows, width = table.shape[2:]
-    shape = jax.ShapeDtypeStruct((readers, requests // chunks * tiles, rows, width), BF16)
     whole = pl.BlockSpec(memory_space=VMEM)
     return pl.pallas_call(
         functools.partial(pick_kernel, tiles),
-        out_shape=(shape,) * chunks,
+        out_shape=jax.ShapeDtypeStruct((readers, requests * tiles, rows, width), BF16),
         in_specs=[pl.BlockSpec(memory_space=pltpu.SMEM), whole],
-        out_specs=(whole,) * chunks,
+        out_specs=whole,
         compiler_params=pltpu.CompilerParams(vmem_limit_bytes=60 << 20),
         name="pick",
     )(where, table)
 
 
 def span_kernel(
-    first_span,
     counts_ref,
+    theirs_ref,
     pieces_ref,
     gain_ref,
     projection_hbm,
@@ -133,8 +156,9 @@
     keyvalue_hbm,
     queries_ref,
     grads_ref,
-    encoded_ref,
-    grad_ref,
+    encoded_hbm,
+    own_hbm,
+    product_hbm,
     attended_ref,
     projection_ref,
     output_ref,
@@ -150,7 +174,11 @@
     changes_ref,
     chances_ref,
     grad_scores_ref,
+    encoded_ref,
+    grad_ref,
+    product_ref,
     sems,
+    out_sems,
 ):
     slices, _, rows, _ = pieces_ref.shape
     length = slices * rows
@@ -233,6 +261,8 @@
             plain_ref[:, columns] + dot(mixed_ref[...], output_ref[:, columns], NN)
         ).astype(BF16)
 
+    stores = [pltpu.make_async_copy(encoded_ref, encoded_hbm, out_sems.at[0])]
+    stores[0].start()
     for j in range(len(wide)):
         wide_load(j).wait()
         columns = slice(wide[j], wide[j] + tile)
@@ -242,7 +272,7 @@
 
     @pl.loop(0, spans)
     def _(u):
-        valid = key_block < counts_ref[first_span + u]
+        valid = key_block < counts_ref[u]
         query_rows = pl.ds(pl.multiple_of(u * SPAN, SPAN), SPAN)
         key_rows = pl.ds(pl.multiple_of(u * keys, keys), keys)
 
@@ -288,8 +318,23 @@
                         BF16
                     )
 
-
-def span_step(part, counts, pieces, gain, projection, output, keyvalue, queries, grads):
+    theirs = theirs_ref[0]
+    stores.append(pltpu.make_async_copy(grad_ref.at[1 - theirs], own_hbm, out_sems.at[1]))
+    stores[1].start()
+    for i in range(width // 512):
+        part = slice(i * 512, (i + 1) * 512)
+        product_ref[part] = dot(grad_ref[theirs, part], encoded_ref[...], NN).astype(BF16)
+        stores.append(
+            pltpu.make_async_copy(
+                product_ref.at[part], product_hbm.at[part], out_sems.at[2 + i]
+            )
+        )
+        stores[-1].start()
+    for store in stores:
+        store.wait()
+
+
+def span_step(counts, theirs, pieces, gain, projection, output, keyvalue, queries, grads):
     width = queries.shape[1]
     feature = keyvalue.shape[1]
     slices, units, rows, _ = pieces.shape
@@ -302,26 +347,26 @@
     heads = width // HEAD
     whole = pl.BlockSpec(memory_space=VMEM)
     hbm = pl.BlockSpec(memory_space=pltpu.HBM)
-    own = pl.BlockSpec((spans * SPAN, width), lambda i: (part, 0))
     return pl.pallas_call(
-        functools.partial(span_kernel, part * spans),
-        grid=(1,),
+        span_kernel,
         out_shape=(
             jax.ShapeDtypeStruct((total, feature), BF16),
-            jax.ShapeDtypeStruct((2, width, total), BF16),
+            jax.ShapeDtypeStruct((width, total), BF16),
+            jax.ShapeDtypeStruct((width, feature), BF16),
             jax.ShapeDtypeStruct((spans * SPAN, width), BF16),
         ),
         in_specs=[
+            pl.BlockSpec(memory_space=pltpu.SMEM),
             pl.BlockSpec(memory_space=pltpu.SMEM),
             whole,
             whole,
             hbm,
             hbm,
             hbm,
-            own,
-            own,
+            whole,
+            whole,
         ],
-        out_specs=(whole, whole, whole),
+        out_specs=(hbm, hbm, hbm, whole),
         scratch_shapes=[
             VMEM(projection.shape, BF16),
             VMEM(output.shape, BF16),
@@ -337,55 +382,69 @@
             VMEM((heads, SPAN, keys), F32),
             VMEM((heads, SPAN, keys), BF16),
             VMEM((heads, SPAN, keys), BF16),
+            VMEM((total, feature), BF16),
+            VMEM((2, width, total), BF16),
+            VMEM((width, feature), BF16),
             pltpu.SemaphoreType.DMA((pl.cdiv(3 * feature, 1024) + 1 + 2 * width // 1024,)),
+            pltpu.SemaphoreType.DMA((2 + width // 512,)),
         ],
         cost_estimate=pl.CostEstimate(
-            flops=total * feature * (8 * feature + 4 * width),
+            flops=total * feature * (8 * feature + 6 * width),
             bytes_accessed=20 << 20,
             transcendentals=1 << 20,
         ),
-        compiler_params=pltpu.CompilerParams(vmem_limit_bytes=(60, 54)[part] << 20),
+        compiler_params=pltpu.CompilerParams(vmem_limit_bytes=58 << 20),
         name="spans",
-    )(counts, pieces, gain, projection, output, keyvalue, queries, grads)
-
-
-def weight_kernel(half_ref, grad_a, grad_b, encoded_a, encoded_b, out_ref):
-    out_ref[...] = (
-        dot(grad_a[0], encoded_a[...], NN) + dot(grad_b[0], encoded_b[...], NN)
-    ).astype(BF16)
-
-
-def weight_half(half, grads, encodeds):
-    _, rows, keys = grads[0].shape
-    feature = encodeds[0].shape[1]
+    )(counts, theirs, pieces, gain, projection, output, keyvalue, queries, grads)
+
+
+def weight_kernel(grad_ref, encoded_ref, out_ref):
+    out_ref[...] = dot(grad_ref[...], encoded_ref[...], NN).astype(BF16)
+
+
+def weight_half(grad, encoded):
+    rows, keys = grad.shape
+    feature = encoded.shape[1]
     tile = 512
-    grad_spec = pl.BlockSpec((1, tile, keys), lambda i, half: (half[0], i, 0))
-    encoded_spec = pl.BlockSpec((keys, feature), lambda i, half: (0, 0))
     return pl.pallas_call(
         weight_kernel,
-        grid_spec=pltpu.PrefetchScalarGridSpec(
-            num_scalar_prefetch=1,
-            grid=(rows // tile,),
-            in_specs=[grad_spec, grad_spec, encoded_spec, encoded_spec],
-            out_specs=pl.BlockSpec((tile, feature), lambda i, half: (i, 0)),
-        ),
+        grid=(rows // tile,),
+        in_specs=[
+            pl.BlockSpec((tile, keys), lambda i: (i, 0)),
+            pl.BlockSpec((keys, feature), lambda i: (0, 0)),
+        ],
+        out_specs=pl.BlockSpec((tile, feature), lambda i: (i, 0)),
         out_shape=jax.ShapeDtypeStruct((rows, feature), BF16),
         cost_estimate=pl.CostEstimate(
-            flops=4 * rows * feature * keys, bytes_accessed=8 << 20, transcendentals=0
+            flops=2 * rows * feature * keys, bytes_accessed=8 << 20, transcendentals=0
         ),
         compiler_params=pltpu.CompilerParams(vmem_limit_bytes=24 << 20),
         name="weight_half",
-    )(half, *grads, *encodeds)
+    )(grad, encoded)
+
+
+def total_kernel(terms_ref, out_ref):
+    total = jnp.sum(terms_ref[...].astype(F32), axis=0).astype(BF16)
+    for i in range(out_ref.shape[0]):
+        out_ref[i] = total
+
+
+def total_copies(terms, copies):
+    whole = pl.BlockSpec(memory_space=VMEM)
+    return pl.pallas_call(
+        total_kernel,
+        out_shape=jax.ShapeDtypeStruct((copies, *terms.shape[1:]), BF16),
+        in_specs=[whole],
+        out_specs=whole,
+        compiler_params=pltpu.CompilerParams(vmem_limit_bytes=16 << 20),
+        name="total",
+    )(terms)
 
 
 def all_to_all(block, axis, groups=None):
     return lax.all_to_all(
         block, axis, split_axis=0, concat_axis=0, tiled=True, axis_index_groups=groups
     )
-
-
-def summed(copies):
-    return copies.astype(F32).sum(axis=0)
 
 
 def local(
@@ -423,41 +482,32 @@
     queries = dot(normed, cross_query, NN).astype(BF16)
     grads = dot(own_cotangent, cross_output, NT).astype(BF16)
 
-    chunks = 2
-    encoded, grad_rows, attended = [], [], []
-    picked = pick(readers_where, table, tiles, chunks)
-    for part in range(chunks):
-        pieces = all_to_all(picked[part], "seq")
-        out = span_step(
-            part,
-            neighbour_counts,
-            pieces,
-            encoder_gain,
-            encoder_projection,
-            encoder_output,
-            cross_keyvalue,
-            queries,
-            grads,
-        )
-        encoded.append(out[0])
-        grad_rows.append(out[1])
-        attended.append(out[2])
-
+    picked = pick(readers_where, table, tiles)
+    pieces = all_to_all(picked, "seq")
     core = lax.axis_index("dp") % 2
-    theirs = weight_half((1 - core).reshape(1), grad_rows, encoded)
+    encoded, own, theirs, attended = span_step(
+        neighbour_counts,
+        (1 - core).reshape(1),
+        pieces,
+        encoder_gain,
+        encoder_projection,
+        encoder_output,
+        cross_keyvalue,
+        queries,
+        grads,
+    )
     received = lax.ppermute(theirs, "dp", [(i, i ^ 1) for i in range(dp)])
-    mine = weight_half(core.reshape(1), grad_rows, encoded)
+    mine = weight_half(own, encoded)
     pair = (mine.astype(F32) + received.astype(F32)).astype(BF16)
 
     half = [
         [d * seq + s for d in range(c, dp, 2) for s in range(seq)] for c in range(2)
     ]
     sent = all_to_all(pair.reshape(dp // 2 * seq, -1, feature), ("dp", "seq"), half)
-    piece = summed(sent).astype(BF16)
-    keyvalue_grad = all_to_all(jnp.broadcast_to(piece, (dp, *piece.shape)), "dp")
+    keyvalue_grad = all_to_all(total_copies(sent, dp), "dp")
     keyvalue_grad = keyvalue_grad.reshape(-1, feature).astype(F32)
 
-    cross = dot(jnp.concatenate(attended, axis=0), cross_output, NN)
+    cross = dot(attended, cross_output, NN)
     rows = (own_hidden.astype(F32) + cross).astype(BF16)
     forth = [(i, i + 1) for i in range(seq - 1)]
     returned = lax.ppermute(rows[token_count - tail :], "seq", forth)

time: 205 us -> 194 us (0.946)
  starting transfers between devices: 45.7 us -> 37 us
  waiting for transfers between devices: 70.9 us -> 78.6 us
  Pallas kernels: 53.2 us -> 48.5 us
  matrix products: 13.4 us -> 11.3 us
    all_to_all x5 -> x4, starting transfers between devices: 35.4 us -> 26.6 us  [all_to_all(): lax.all_to_all(block, axis, split_axis=0, concat_axis=0, tiled=True, axis...]
    all_to_all x5 -> x4, waiting for transfers between devices: 69.9 us -> 78.6 us  [all_to_all(): lax.all_to_all(block, axis, split_axis=0, concat_axis=0, tiled=True, axis...]
    pallas_call x5 -> x4, Pallas kernels: 48.7 us -> 43.9 us  [the longest x1 35 us: span_step(): pl.pallas_call(span_kernel, out_shape=(jax.ShapeDtypeStruct((total, featu...]
    dot_general x3, matrix products: 13.4 us -> 11.3 us  [dot(): return lax.dot_general(a, b, dims, preferred_element_type=F32)]
    unnamed x25 -> x23, local copies, waits for them, and re-layouts: 6.51 us -> 6.53 us
  transfers between devices with their start and end apart: 8 -> 7, of which waited for: 5 -> 4; matrix products, arithmetic and copies ran while one was open for 11% -> 10% of each run, Pallas kernels for 13% -> 5%
where the time goes in v3:
time: 194 us; the launch traced here: 193 us
  waiting for transfers between devices  78.6 us (41%)
  Pallas kernels  48.5 us (25%)
  starting transfers between devices  37 us (19%)
  matrix products  11.3 us (6%)
  local copies, waits for them, and re-layouts  10.6 us (5%)
  other arithmetic  6.26 us (3%)
    all_to_all x4, waiting for transfers between devices, all_to_all(): lax.all_to_all(block, axis, split_axis=0, concat_axis=0, tiled=True, axis...  78.6 us
    pallas_call x1, Pallas kernels, span_step(): pl.pallas_call(span_kernel, out_shape=(jax.ShapeDtypeStruct((total, featu...  35 us
    all_to_all x4, starting transfers between devices, all_to_all(): lax.all_to_all(block, axis, split_axis=0, concat_axis=0, tiled=True, axis...  26.6 us
    dot_general x3, matrix products, dot(): return lax.dot_general(a, b, dims, preferred_element_type=F32)  11.3 us
    unnamed x23, local copies, waits for them, and re-layouts  6.53 us
    ppermute x1, starting transfers between devices, local(): received = lax.ppermute(theirs, 'dp', [(i, i ^ 1) for i in range(dp)])  5.49 us
    pallas_call x1, Pallas kernels, spread(): pl.pallas_call(spread_kernel, grid=(1,), out_shape=(jax.ShapeDtypeStruct(...  4.54 us
    pallas_call x1, Pallas kernels, pick(): pl.pallas_call(functools.partial(pick_kernel, tiles), out_shape=jax.Shape...  4.07 us
  transfers between devices with their start and end apart: 7, of which 4 were waited for; matrix products, arithmetic and copies ran while one was open for 10% of the time, Pallas kernels for 5%

profile of v3, /device:TPU:1, one launch (start us, length us, event | category | flops | bytes accessed | tf_op | source)
XLA Modules:
  0.0 193.0 jit_solution(10502317292523222649)
XLA Ops:
  0.6 1.3 copy.18.neighbours_ref
  2.0 4.5 %spread.1 = (bf16[16,85,8,128]{3,2,1,0:T(8,128)(2,1)}, bf16[2,64,1536]{2,1,0:T(8,128)(2,1)}) custom-call(s32[192]{0:T(256)} %home_ref.1, s32[4,2]{1,0:T(4,128)} %copy.18.neighbours_ref, bf16[12,128,896]{2,1,0:T(8,128)(2,1)} %bitcast.16, bf16[256,1536]{1,0:T(8,128)(2,1)} %hidden_ref.1, bf16[256,1536]{1,0:T(8,128)(2,1)} %cotangent_ref.1), custom_call_target="tpu_custom_call" | custom-call | flops 1048576 | bytes 6291456 | tf_op jit(solution)/shard_map/spread/pallas_call | solution.py:101
  6.5 8.6 %all-to-all-start = ((bf16[16,85,8,128]{3,2,1,0:T(8,128)(2,1)}), bf16[16,85,8,128]{3,2,1,0:T(8,128)(2,1)S(1)}, u32[]{:S(2)}, u32[]{:S(2)}) async-start(bf16[16,85,8,128]{3,2,1,0:T(8,128)(2,1)} %get-tuple-element.9), calls=%async_computation | async-start | bytes 5570560 | tf_op jit(solution)/shard_map/all_to_all | solution.py:445
  15.1 1.3 collective-permute-start
  16.4 35.2 %all-to-all-done.table_ref = bf16[16,85,8,128]{3,2,1,0:T(8,128)(2,1)S(1)} async-done(((bf16[16,85,8,128]{3,2,1,0:T(8,128)(2,1)}), bf16[16,85,8,128]{3,2,1,0:T(8,128)(2,1)S(1)}, u32[]{:S(2)}, u32[]{:S(2)}) %all-to-all-start) | async-done | bytes 2785312 | tf_op jit(solution)/shard_map/all_to_all | solution.py:445
  51.6 0.7 slice_convert_fusion
  52.3 0.9 copy-done.2
  53.2 4.1 %pick.1 = bf16[16,56,8,128]{3,2,1,0:T(8,128)(2,1)} custom-call(s32[16,8]{1,0:T(8,128)} %bitcast.17, bf16[16,85,8,128]{3,2,1,0:T(8,128)(2,1)} %copy-done.2), custom_call_target="tpu_custom_call" | custom-call | tf_op jit(solution)/shard_map/pick/pallas_call | solution.py:139
  57.2 6.5 %all-to-all-start.1 = ((bf16[16,56,8,128]{3,2,1,0:T(8,128)(2,1)}), bf16[16,56,8,128]{3,2,1,0:T(8,128)(2,1)}, u32[]{:S(2)}, u32[]{:S(2)}) async-start(bf16[16,56,8,128]{3,2,1,0:T(8,128)(2,1)} %pick.1), calls=%async_computation.1 | async-start | bytes 3670016 | tf_op jit(solution)/shard_map/all_to_all | solution.py:445
  63.8 0.0 copy-done.3
  63.8 0.1 slice.25
  63.9 0.0 copy-done.4
  63.9 0.0 copy-start.5
  64.0 0.1 slice.28
  64.1 0.0 collective-permute-done
  64.1 1.1 slice_bitcast_fusion
  65.2 0.0 copy-start.7
  65.2 0.0 slice-start
  65.2 0.3 fusion.1
  65.5 0.0 slice-start.1
  65.5 0.0 copy-start.8
  65.6 4.9 %convolution_convert_fusion.grads_ref = bf16[256,1536]{1,0:T(8,128)(2,1)} fusion(bf16[1536,1536]{1,0:T(8,128)(2,1)} %param.24, bf16[63,1536]{1,0:T(8,128)(2,1)S(1)} %get-tuple-element.14, bf16[193,1536]{1,0:T(8,128)(2,1)S(1)} %slice.28), kind=kOutput, calls=%fused_computation.3 | convolution fusion | flops 1209925632 | bytes 6291456 | tf_op jit(solution)/shard_map/dot_general | solution.py:24
  70.4 0.0 copy-done.5
  70.4 0.0 copy-done.7
  70.4 0.0 slice-done
  70.5 2.3 %convolution_convert_fusion.1.queries_ref = bf16[256,1536]{1,0:T(8,128)(2,1)} fusion(bf16[1536,1536]{1,0:T(8,128)(2,1)S(1)} %bitcast.19, f32[1536]{0:T(1024)S(1)} %copy-done.8, f32[256]{0:T(256)S(1)} %add_rsqrt_fusion, bf16[63,1536]{1,0:T(8,128)(2,1)S(1)} %get-tuple-element.15, bf16[193,1536]{1,0:T(8,128)(2,1)S(1)} %slice.25), kind=kOutput, calls=%fused_computation.4 | convolution fusion | flops 1211105280 | bytes 6298624 | tf_op jit(solution)/shard_map/dot_general | solution.py:24
  72.8 13.3 %all-to-all-done.1.pieces_ref = bf16[16,56,8,128]{3,2,1,0:T(8,128)(2,1)} async-done(((bf16[16,56,8,128]{3,2,1,0:T(8,128)(2,1)}), bf16[16,56,8,128]{3,2,1,0:T(8,128)(2,1)}, u32[]{:S(2)}, u32[]{:S(2)}) %all-to-all-start.1) | async-done | bytes 1835040 | tf_op jit(solution)/shard_map/all_to_all | solution.py:445
  86.0 35.0 %spans.1 = (bf16[1024,896]{1,0:T(8,128)(2,1)}, bf16[1536,1024]{1,0:T(8,128)(2,1)}, bf16[1536,896]{1,0:T(8,128)(2,1)}, bf16[256,1536]{1,0:T(8,128)(2,1)}) custom-call(s32[4]{0:T(128)} %counts_ref.1, s32[1]{0:T(128)} %bitcast.2.theirs_ref, bf16[16,56,8,128]{3,2,1,0:T(8,128)(2,1)} %all-to-all-done.1.pieces_ref, f32[896]{0:T(1024)} %gain_ref.1, ...), custom_call_target="tpu_custom_call" | custom-call | flops 15032385536 | bytes 20971520 | tf_op jit(solution)/shard_map/spans/pallas_call | solution.py:350
  121.0 5.5 %collective-permute-start.2 = (bf16[1536,896]{1,0:T(8,128)(2,1)}, bf16[1536,896]{1,0:T(8,128)(2,1)S(1)}, u32[]{:S(2)}, u32[]{:S(2)}) collective-permute-start(bf16[1536,896]{1,0:T(8,128)(2,1)} %get-tuple-element.13), channel_id=1, source_target_pairs={{0,16},{16,0},{32,48},{48,32},{64,80},{80,64},{96,112},{112,96},{1... | collective-permute-start | bytes 8257544 | tf_op jit(solution)/shard_map/ppermute | solution.py:499
  126.5 1.9 copy-done
  128.4 1.5 copy-done.1
  129.9 3.8 %weight_half.1 = bf16[1536,896]{1,0:T(8,128)(2,1)S(1)} custom-call(bf16[1536,1024]{1,0:T(8,128)(2,1)S(1)} %copy-done, bf16[1024,896]{1,0:T(8,128)(2,1)S(1)} %copy-done.1), custom_call_target="tpu_custom_call" | custom-call | flops 2818572288 | bytes 8388608 | tf_op jit(solution)/shard_map/weight_half/pallas_call | solution.py:409
  133.7 0.0 collective-permute-done.2
  133.7 2.3 %add_convert_fusion = bf16[1536,896]{1,0:T(8,128)(2,1)} fusion(bf16[1536,896]{1,0:T(8,128)(2,1)S(1)} %collective-permute-done.2, bf16[1536,896]{1,0:T(8,128)(2,1)S(1)} %weight_half.1), kind=kLoop, calls=%fused_computation | loop fusion | flops 5505024 | bytes 8257536 | tf_op jit(solution)/shard_map/convert_element_type | solution.py:501
  136.0 6.8 %all-to-all-start.2 = ((bf16[64,24,896]{2,1,0:T(8,128)(2,1)}), bf16[64,24,896]{2,1,0:T(8,128)(2,1)S(1)}, u32[]{:S(2)}, u32[]{:S(2)}) async-start(bf16[64,24,896]{2,1,0:T(8,128)(2,1)} %bitcast.15), calls=%async_computation.2 | async-start | bytes 5505024 | tf_op jit(solution)/shard_map/all_to_all | solution.py:445
  142.7 4.1 %fusion = bf16[256,1536]{1,0:T(8,128)(2,1)S(1)} fusion(bf16[256,1536]{1,0:T(8,128)(2,1)} %get-tuple-element.10, bf16[1536,1536]{1,0:T(8,128)(2,1)} %param.24, bf16[63,1536]{1,0:T(8,128)(2,1)} %copy-done.7, bf16[193,1536]{1,0:T(8,128)(2,1)} %copy-done.5), kind=kOutput, calls=%fused_computation.2 | convolution fusion | flops 1210318848 | bytes 7077888 | tf_op jit(solution)/shard_map/dot_general | solution.py:24
  146.9 0.0 copy-start.6
  146.9 0.9 copy-done.6
  147.8 0.7 slice.35
  148.5 3.6 %collective-permute-start.1 = (bf16[63,1536]{1,0:T(8,128)(2,1)}, bf16[63,1536]{1,0:T(8,128)(2,1)}, u32[]{:S(2)}, u32[]{:S(2)}) collective-permute-start(bf16[63,1536]{1,0:T(8,128)(2,1)} %slice.35), channel_id=1, source_target_pairs={{0,1},{1,2},{2,3},{3,4},{4,5},{5,6},{6,7},{7,8},{8,9},{9,10},{10,1... | collective-permute-start | bytes 580616 | tf_op jit(solution)/shard_map/ppermute | solution.py:513
  152.1 1.9 %slice.36 = bf16[193,1536]{1,0:T(8,128)(2,1)} slice(bf16[256,1536]{1,0:T(8,128)(2,1)} %copy-done.6), slice={[0:193], [0:1536]} | slice | bytes 1185792 | tf_op jit(solution)/shard_map/slice | solution.py:515
  154.1 25.0 %all-to-all-done.2.terms_ref = bf16[64,24,896]{2,1,0:T(8,128)(2,1)S(1)} async-done(((bf16[64,24,896]{2,1,0:T(8,128)(2,1)}), bf16[64,24,896]{2,1,0:T(8,128)(2,1)S(1)}, u32[]{:S(2)}, u32[]{:S(2)}) %all-to-all-start.2) | async-done | bytes 2752544 | tf_op jit(solution)/shard_map/all_to_all | solution.py:445
  179.1 1.1 total.1
  180.2 4.7 %all-to-all-start.3 = ((bf16[8,24,896]{2,1,0:T(8,128)(2,1)}), bf16[8,24,896]{2,1,0:T(8,128)(2,1)S(1)}, u32[]{:S(2)}, u32[]{:S(2)}) async-start(bf16[8,24,896]{2,1,0:T(8,128)(2,1)} %total.1), calls=%async_computation.3 | async-start | bytes 688128 | tf_op jit(solution)/shard_map/all_to_all | solution.py:445
  184.9 0.0 collective-permute-done.1
  184.9 2.1 %pad_maximum_fusion.1 = bf16[256,1536]{1,0:T(8,128)(2,1)} fusion(bf16[193,1536]{1,0:T(8,128)(2,1)} %slice.36, bf16[63,1536]{1,0:T(8,128)(2,1)S(1)} %slice_select_fusion), kind=kLoop, calls=%fused_computation.14 | loop fusion | flops 1572864 | bytes 1572864 | tf_op jit(solution)/shard_map/concatenate | solution.py:515
  187.0 5.1 %all-to-all-done.3 = bf16[8,24,896]{2,1,0:T(8,128)(2,1)S(1)} async-done(((bf16[8,24,896]{2,1,0:T(8,128)(2,1)}), bf16[8,24,896]{2,1,0:T(8,128)(2,1)S(1)}, u32[]{:S(2)}, u32[]{:S(2)}) %all-to-all-start.3) | async-done | bytes 344096 | tf_op jit(solution)/shard_map/all_to_all | solution.py:445
  192.1 0.9 bitcast_convert_fusion
  (10 shorter events, 0.0 us)
Async XLA Ops:
  6.5 45.1 %all-to-all-start = ((bf16[16,85,8,128]{3,2,1,0:T(8,128)(2,1)}), bf16[16,85,8,128]{3,2,1,0:T(8,128)(2,1)S(1)}, u32[]{:S(2)}, u32[]{:S(2)}) async-start(bf16[16,85,8,128]{3,2,1,0:T(8,128)(2,1)} %get-tuple-element.9), calls=%async_computation | async-start | bytes 5570560 | tf_op jit(solution)/shard_map/all_to_all | solution.py:445
  15.1 49.0 %collective-permute-start = (bf16[2,64,1536]{2,1,0:T(8,128)(2,1)}, bf16[2,64,1536]{2,1,0:T(8,128)(2,1)}, u32[]{:S(2)}, u32[]{:S(2)}) collective-permute-start(bf16[2,64,1536]{2,1,0:T(8,128)(2,1)} %get-tuple-element.8), channel_id=1, source_target_pairs={{1,0},{2,1},{3,2},{4,3},{5,4},{6,5},{7,6},{8,7},{9,8},{10,9},{11,1... | collective-permute-start | bytes 1179656 | tf_op jit(solution)/shard_map/ppermute | solution.py:474
  51.6 1.5 copy-start.2
  57.2 6.5 %copy-start.3 = (bf16[256,1536]{1,0:T(8,128)(2,1)S(1)}, bf16[256,1536]{1,0:T(8,128)(2,1)}, u32[]{:S(2)}) copy-start(bf16[256,1536]{1,0:T(8,128)(2,1)} %hidden_ref.1) | copy-start | bytes 2359300
  57.2 6.7 %copy-start.4 = (bf16[256,1536]{1,0:T(8,128)(2,1)S(1)}, bf16[256,1536]{1,0:T(8,128)(2,1)}, u32[]{:S(2)}) copy-start(bf16[256,1536]{1,0:T(8,128)(2,1)} %cotangent_ref.1) | copy-start | bytes 2359300
  57.2 28.8 %all-to-all-start.1 = ((bf16[16,56,8,128]{3,2,1,0:T(8,128)(2,1)}), bf16[16,56,8,128]{3,2,1,0:T(8,128)(2,1)}, u32[]{:S(2)}, u32[]{:S(2)}) async-start(bf16[16,56,8,128]{3,2,1,0:T(8,128)(2,1)} %pick.1), calls=%async_computation.1 | async-start | bytes 3670016 | tf_op jit(solution)/shard_map/all_to_all | solution.py:445
  63.9 6.5 %copy-start.5 = (bf16[193,1536]{1,0:T(8,128)(2,1)}, bf16[193,1536]{1,0:T(8,128)(2,1)S(1)}, u32[]{:S(2)}) copy-start(bf16[193,1536]{1,0:T(8,128)(2,1)S(1)} %slice.25) | copy-start | bytes 1778692
  65.2 5.2 %copy-start.7 = (bf16[63,1536]{1,0:T(8,128)(2,1)}, bf16[63,1536]{1,0:T(8,128)(2,1)S(1)}, u32[]{:S(2)}) copy-start(bf16[63,1536]{1,0:T(8,128)(2,1)S(1)} %get-tuple-element.15) | copy-start | bytes 580612
  65.2 5.2 %slice-start = ((s8[4718592]{0:T(1024)(128)(4,1)}), s8[4194304]{0:T(1024)(128)(4,1)S(1)}, s32[]{:S(2)}) async-start(s8[4718592]{0:T(1024)(128)(4,1)} %bitcast.18), calls=%async_computation.4 | async-start | bytes 8388608
  65.5 4.9 %slice-start.1 = ((s8[4718592]{0:T(1024)(128)(4,1)}), s8[524288]{0:T(1024)(128)(4,1)S(1)}, s32[]{:S(2)}) async-start(s8[4718592]{0:T(1024)(128)(4,1)} %bitcast.18), calls=%async_computation.5 | async-start | bytes 1048576
  65.5 4.9 %copy-start.8 = (f32[1536]{0:T(1024)S(1)}, f32[1536]{0:T(1024)}, u32[]{:S(2)}) copy-start(f32[1536]{0:T(1024)} %param.21) | copy-start | bytes 18436
  121.0 12.7 %collective-permute-start.2 = (bf16[1536,896]{1,0:T(8,128)(2,1)}, bf16[1536,896]{1,0:T(8,128)(2,1)S(1)}, u32[]{:S(2)}, u32[]{:S(2)}) collective-permute-start(bf16[1536,896]{1,0:T(8,128)(2,1)} %get-tuple-element.13), channel_id=1, source_target_pairs={{0,16},{16,0},{32,48},{48,32},{64,80},{80,64},{96,112},{112,96},{1... | collective-permute-start | bytes 8257544 | tf_op jit(solution)/shard_map/ppermute | solution.py:499
  126.5 1.9 copy-start
  128.4 1.5 copy-start.1
  136.0 43.1 %all-to-all-start.2 = ((bf16[64,24,896]{2,1,0:T(8,128)(2,1)}), bf16[64,24,896]{2,1,0:T(8,128)(2,1)S(1)}, u32[]{:S(2)}, u32[]{:S(2)}) async-start(bf16[64,24,896]{2,1,0:T(8,128)(2,1)} %bitcast.15), calls=%async_computation.2 | async-start | bytes 5505024 | tf_op jit(solution)/shard_map/all_to_all | solution.py:445
  146.9 0.9 copy-start.6
  148.5 36.4 %collective-permute-start.1 = (bf16[63,1536]{1,0:T(8,128)(2,1)}, bf16[63,1536]{1,0:T(8,128)(2,1)}, u32[]{:S(2)}, u32[]{:S(2)}) collective-permute-start(bf16[63,1536]{1,0:T(8,128)(2,1)} %slice.35), channel_id=1, source_target_pairs={{0,1},{1,2},{2,3},{3,4},{4,5},{5,6},{6,7},{7,8},{8,9},{9,10},{10,1... | collective-permute-start | bytes 580616 | tf_op jit(solution)/shard_map/ppermute | solution.py:513
  180.2 11.9 %all-to-all-start.3 = ((bf16[8,24,896]{2,1,0:T(8,128)(2,1)}), bf16[8,24,896]{2,1,0:T(8,128)(2,1)S(1)}, u32[]{:S(2)}, u32[]{:S(2)}) async-start(bf16[8,24,896]{2,1,0:T(8,128)(2,1)} %total.1), calls=%async_computation.3 | async-start | bytes 688128 | tf_op jit(solution)/shard_map/all_to_all | solution.py:445

commit v4 on v3

--- a/solution.py
+++ b/solution.py
@@ -37,14 +37,16 @@
     home_ref,
     neighbours_ref,
     blocks_hbm,
-    hidden_ref,
-    cotangent_ref,
+    hidden_hbm,
+    cotangent_hbm,
     slices_hbm,
-    tails_ref,
+    tails_hbm,
     blocks_ref,
     slices_ref,
+    tails_ref,
     sems,
     out_sems,
+    tail_sems,
 ):
     blocks, length, feature = blocks_ref.shape
     devices, units, rows, _ = slices_ref.shape
@@ -64,8 +66,17 @@
             slices_ref.at[several], slices_hbm.at[several], out_sems.at[part]
         )
 
+    span = tails_ref.shape[1]
+    tail_loads = [
+        pltpu.make_async_copy(rows_hbm.at[pl.ds(0, span)], tails_ref.at[i], tail_sems.at[i])
+        for i, rows_hbm in enumerate((hidden_hbm, cotangent_hbm))
+    ]
+    tail_store = pltpu.make_async_copy(tails_ref, tails_hbm, tail_sems.at[2])
     for part in range(parts):
         load(part).start()
+        if part == 0:
+            for tail_load in tail_loads:
+                tail_load.start()
     lane = lax.broadcasted_iota(jnp.int32, (rows, HEAD), 1)
     notes = jnp.zeros((rows, HEAD), jnp.int32)
     spans, each = neighbours_ref.shape
@@ -73,8 +84,6 @@
         for n in range(each):
             notes = jnp.where(lane == u * each + n, home_ref[neighbours_ref[u, n]], notes)
     notes = notes.astype(F32).astype(BF16)
-    tails_ref[0] = hidden_ref[...]
-    tails_ref[1] = cotangent_ref[...]
     for d in range(devices):
         if d % (devices // parts) == 0:
             load(d // (devices // parts)).wait()
@@ -86,8 +95,13 @@
         slices_ref[d, units - 1] = notes
         if (d + 1) % (devices // parts) == 0:
             store(d // (devices // parts)).start()
+            if d < devices // parts:
+                for tail_load in tail_loads:
+                    tail_load.wait()
+                tail_store.start()
     for part in range(parts):
         store(part).wait()
+    tail_store.wait()
 
 
 def spread(block_home, neighbours, database, hidden, cotangent, devices):
@@ -96,22 +110,22 @@
     units = blocks * (feature // HEAD) + 1
     rows = length // devices
     smem = pl.BlockSpec(memory_space=pltpu.SMEM)
-    first = pl.BlockSpec((SPAN, width), lambda i: (0, 0))
-    whole = pl.BlockSpec(memory_space=VMEM)
+    hbm = pl.BlockSpec(memory_space=pltpu.HBM)
     return pl.pallas_call(
         spread_kernel,
-        grid=(1,),
         out_shape=(
             jax.ShapeDtypeStruct((devices, units, rows, HEAD), BF16),
             jax.ShapeDtypeStruct((2, SPAN, width), BF16),
         ),
-        in_specs=[smem, smem, pl.BlockSpec(memory_space=pltpu.HBM), first, first],
-        out_specs=(pl.BlockSpec(memory_space=pltpu.HBM), whole),
+        in_specs=[smem, smem, hbm, hbm, hbm],
+        out_specs=(hbm, hbm),
         scratch_shapes=[
             VMEM(database.shape, BF16),
             VMEM((devices, units, rows, HEAD), BF16),
+            VMEM((2, SPAN, width), BF16),
             pltpu.SemaphoreType.DMA((4,)),
             pltpu.SemaphoreType.DMA((4,)),
+            pltpu.SemaphoreType.DMA((3,)),
         ],
         cost_estimate=pl.CostEstimate(flops=1 << 20, bytes_accessed=6 << 20, transcendentals=0),
         compiler_params=pltpu.CompilerParams(vmem_limit_bytes=60 << 20),
@@ -119,28 +133,42 @@
     )(block_home, neighbours, database, hidden, cotangent)
 
 
-def pick_kernel(tiles, where_ref, table_ref, out_ref):
+def pick_kernel(tiles, where_ref, table_ref, out_hbm, out_ref, sems):
     blocks = table_ref.shape[1] // tiles
-
-    @pl.loop(0, out_ref.shape[0])
-    def _(r):
-        for i in range(out_ref.shape[1] // tiles):
-            where = where_ref[r, i]
-            start = (where % blocks) * tiles
-            out_ref[r, i * tiles : (i + 1) * tiles] = table_ref[
-                where // blocks, pl.ds(start, tiles)
-            ]
+    parts = sems.shape[0]
+    size = out_ref.shape[0] // parts
+
+    def store(part):
+        readers = pl.ds(part * size, size)
+        return pltpu.make_async_copy(out_ref.at[readers], out_hbm.at[readers], sems.at[part])
+
+    for part in range(parts):
+
+        @pl.loop(part * size, (part + 1) * size)
+        def _(r):
+            for i in range(out_ref.shape[1] // tiles):
+                where = where_ref[r, i]
+                start = (where % blocks) * tiles
+                out_ref[r, i * tiles : (i + 1) * tiles] = table_ref[
+                    where // blocks, pl.ds(start, tiles)
+                ]
+
+        store(part).start()
+    for part in range(parts):
+        store(part).wait()
 
 
 def pick(where, table, tiles):
     readers, requests = where.shape
     rows, width = table.shape[2:]
+    shape = (readers, requests * tiles, rows, width)
     whole = pl.BlockSpec(memory_space=VMEM)
     return pl.pallas_call(
         functools.partial(pick_kernel, tiles),
-        out_shape=jax.ShapeDtypeStruct((readers, requests * tiles, rows, width), BF16),
+        out_shape=jax.ShapeDtypeStruct(shape, BF16),
         in_specs=[pl.BlockSpec(memory_space=pltpu.SMEM), whole],
-        out_specs=whole,
+        out_specs=pl.BlockSpec(memory_space=pltpu.HBM),
+        scratch_shapes=[VMEM(shape, BF16), pltpu.SemaphoreType.DMA((4,))],
         compiler_params=pltpu.CompilerParams(vmem_limit_bytes=60 << 20),
         name="pick",
     )(where, table)
@@ -149,13 +177,13 @@
 def span_kernel(
     counts_ref,
     theirs_ref,
-    pieces_ref,
+    pieces_hbm,
     gain_ref,
     projection_hbm,
     output_hbm,
     keyvalue_hbm,
-    queries_ref,
-    grads_ref,
+    queries_hbm,
+    grads_hbm,
     encoded_hbm,
     own_hbm,
     product_hbm,
@@ -177,8 +205,12 @@
     encoded_ref,
     grad_ref,
     product_ref,
+    pieces_ref,
+    queries_ref,
+    grads_ref,
     sems,
     out_sems,
+    in_sems,
 ):
     slices, _, rows, _ = pieces_ref.shape
     length = slices * rows
@@ -208,10 +240,26 @@
         )
 
     output_load = pltpu.make_async_copy(output_hbm, output_ref, sems.at[len(narrow)])
+
+    def piece_load(b):
+        units = pl.ds(b * tiles, 2 * tiles)
+        return pltpu.make_async_copy(
+            pieces_hbm.at[:, units], pieces_ref.at[:, units], in_sems.at[2 + b // 2]
+        )
+
+    row_loads = [
+        pltpu.make_async_copy(queries_hbm, queries_ref, in_sems.at[0]),
+        pltpu.make_async_copy(grads_hbm, grads_ref, in_sems.at[1]),
+    ]
+    piece_load(0).start()
     load(0).start()
+    for b in range(2, blocks, 2):
+        piece_load(b).start()
     gain = gain_ref[...].reshape(1, feature)
     for b in range(blocks):
         block_rows = slice(b * length, (b + 1) * length)
+        if b % 2 == 0:
+            piece_load(b).wait()
         for k in range(tiles):
             plain_ref[block_rows, k * HEAD : (k + 1) * HEAD] = (
                 pieces_ref[:, b * tiles + k].astype(F32).reshape(length, HEAD)
@@ -227,6 +275,8 @@
         if j == 1:
             for i in range(len(wide)):
                 wide_load(i).start()
+            for row_load in row_loads:
+                row_load.start()
         columns = slice(narrow[j], min(narrow[j] + tile, 3 * feature))
         qkv_ref[:, columns] = dot(normed_ref[...], projection_ref[:, columns], NN).astype(BF16)
 
@@ -268,6 +318,8 @@
         columns = slice(wide[j], wide[j] + tile)
         kv_ref[:, columns] = dot(encoded_ref[...], keyvalue_ref[columns, :], NT).astype(BF16)
 
+    for row_load in row_loads:
+        row_load.wait()
     key_block = lax.broadcasted_iota(jnp.int32, (1, keys), 1) // length
 
     @pl.loop(0, spans)
@@ -358,13 +410,13 @@
         in_specs=[
             pl.BlockSpec(memory_space=pltpu.SMEM),
             pl.BlockSpec(memory_space=pltpu.SMEM),
-            whole,
+            hbm,
             whole,
             hbm,
             hbm,
             hbm,
-            whole,
-            whole,
+            hbm,
+            hbm,
         ],
         out_specs=(hbm, hbm, hbm, whole),
         scratch_shapes=[
@@ -385,8 +437,12 @@
             VMEM((total, feature), BF16),
             VMEM((2, width, total), BF16),
             VMEM((width, feature), BF16),
+            VMEM(pieces.shape, BF16),
+            VMEM(queries.shape, BF16),
+            VMEM(queries.shape, BF16),
             pltpu.SemaphoreType.DMA((pl.cdiv(3 * feature, 1024) + 1 + 2 * width // 1024,)),
             pltpu.SemaphoreType.DMA((2 + width // 512,)),
+            pltpu.SemaphoreType.DMA((2 + blocks // 2,)),
         ],
         cost_estimate=pl.CostEstimate(
             flops=total * feature * (8 * feature + 6 * width),

time: 194 us -> 192 us (0.990)
  transfers between devices with their start and end apart: 7 -> 7, of which waited for: 4 -> 4; matrix products, arithmetic and copies ran while one was open for 10% -> 10% of each run, Pallas kernels for 5% -> 4%
where the time goes in v4:
time: 192 us; the launch traced here: 191 us
  waiting for transfers between devices  78.6 us (41%)
  Pallas kernels  46.7 us (24%)
  starting transfers between devices  37 us (19%)
  matrix products  11.3 us (6%)
  local copies, waits for them, and re-layouts  10.6 us (6%)
  other arithmetic  6.26 us (3%)
    all_to_all x4, waiting for transfers between devices, all_to_all(): lax.all_to_all(block, axis, split_axis=0, concat_axis=0, tiled=True, axis...  78.6 us
    pallas_call x1, Pallas kernels, span_step(): pl.pallas_call(span_kernel, out_shape=(jax.ShapeDtypeStruct((total, featu...  34.4 us
    all_to_all x4, starting transfers between devices, all_to_all(): lax.all_to_all(block, axis, split_axis=0, concat_axis=0, tiled=True, axis...  26.6 us
    dot_general x3, matrix products, dot(): return lax.dot_general(a, b, dims, preferred_element_type=F32)  11.3 us
    unnamed x23, local copies, waits for them, and re-layouts  6.53 us
    ppermute x1, starting transfers between devices, local(): received = lax.ppermute(theirs, 'dp', [(i, i ^ 1) for i in range(dp)])  5.49 us
    pallas_call x1, Pallas kernels, spread(): pl.pallas_call(spread_kernel, out_shape=(jax.ShapeDtypeStruct((devices, u...  3.85 us
  transfers between devices with their start and end apart: 7, of which 4 were waited for; matrix products, arithmetic and copies ran while one was open for 10% of the time, Pallas kernels for 4%

profile of v4, /device:TPU:1, one launch (start us, length us, event | category | flops | bytes accessed | tf_op | source)
XLA Modules:
  0.0 191.4 jit_solution(4670671401174994597)
XLA Ops:
  0.6 1.3 copy.18.neighbours_ref
  2.0 3.9 %spread.1 = (bf16[16,85,8,128]{3,2,1,0:T(8,128)(2,1)}, bf16[2,64,1536]{2,1,0:T(8,128)(2,1)}) custom-call(s32[192]{0:T(256)} %home_ref.1, s32[4,2]{1,0:T(4,128)} %copy.18.neighbours_ref, bf16[12,128,896]{2,1,0:T(8,128)(2,1)} %bitcast.16, bf16[256,1536]{1,0:T(8,128)(2,1)} %hidden_hbm.1, bf16[256,1536]{1,0:T(8,128)(2,1)} %cotangent_hbm.1), custom_call_target="tpu_custom_call" | custom-call | flops 1048576 | bytes 6291456 | tf_op jit(solution)/shard_map/spread/pallas_call | solution.py:114
  5.8 8.6 %all-to-all-start = ((bf16[16,85,8,128]{3,2,1,0:T(8,128)(2,1)}), bf16[16,85,8,128]{3,2,1,0:T(8,128)(2,1)S(1)}, u32[]{:S(2)}, u32[]{:S(2)}) async-start(bf16[16,85,8,128]{3,2,1,0:T(8,128)(2,1)} %get-tuple-element.9), calls=%async_computation | async-start | bytes 5570560 | tf_op jit(solution)/shard_map/all_to_all | solution.py:501
  14.4 1.3 collective-permute-start
  15.7 35.2 %all-to-all-done.table_ref = bf16[16,85,8,128]{3,2,1,0:T(8,128)(2,1)S(1)} async-done(((bf16[16,85,8,128]{3,2,1,0:T(8,128)(2,1)}), bf16[16,85,8,128]{3,2,1,0:T(8,128)(2,1)S(1)}, u32[]{:S(2)}, u32[]{:S(2)}) %all-to-all-start) | async-done | bytes 2785312 | tf_op jit(solution)/shard_map/all_to_all | solution.py:501
  50.9 0.7 slice_convert_fusion
  51.6 0.9 copy-done.2
  52.5 3.6 %pick.1 = bf16[16,56,8,128]{3,2,1,0:T(8,128)(2,1)} custom-call(s32[16,8]{1,0:T(8,128)} %bitcast.17, bf16[16,85,8,128]{3,2,1,0:T(8,128)(2,1)} %copy-done.2), custom_call_target="tpu_custom_call" | custom-call | tf_op jit(solution)/shard_map/pick/pallas_call | solution.py:166
  56.1 0.0 copy-start.3
  56.1 0.0 copy-start.4
  56.2 6.5 %all-to-all-start.1 = ((bf16[16,56,8,128]{3,2,1,0:T(8,128)(2,1)}), bf16[16,56,8,128]{3,2,1,0:T(8,128)(2,1)}, u32[]{:S(2)}, u32[]{:S(2)}) async-start(bf16[16,56,8,128]{3,2,1,0:T(8,128)(2,1)} %pick.1), calls=%async_computation.1 | async-start | bytes 3670016 | tf_op jit(solution)/shard_map/all_to_all | solution.py:501
  62.7 0.0 copy-done.3
  62.7 0.1 slice.25
  62.9 0.0 copy-done.4
  62.9 0.0 copy-start.5
  62.9 0.1 slice.28
  63.0 0.0 collective-permute-done
  63.1 1.1 slice_bitcast_fusion
  64.2 0.0 copy-start.7
  64.2 0.0 slice-start
  64.2 0.3 fusion.1
  64.5 0.0 slice-start.1
  64.5 0.0 copy-start.8
  64.5 4.9 %convolution_convert_fusion.grads_hbm = bf16[256,1536]{1,0:T(8,128)(2,1)} fusion(bf16[1536,1536]{1,0:T(8,128)(2,1)} %param.24, bf16[63,1536]{1,0:T(8,128)(2,1)S(1)} %get-tuple-element.14, bf16[193,1536]{1,0:T(8,128)(2,1)S(1)} %slice.28), kind=kOutput, calls=%fused_computation.3 | convolution fusion | flops 1209925632 | bytes 6291456 | tf_op jit(solution)/shard_map/dot_general | solution.py:24
  69.3 0.0 copy-done.7
  69.4 2.3 %convolution_convert_fusion.1.queries_hbm = bf16[256,1536]{1,0:T(8,128)(2,1)} fusion(bf16[1536,1536]{1,0:T(8,128)(2,1)S(1)} %bitcast.19, f32[1536]{0:T(1024)S(1)} %copy-done.8, f32[256]{0:T(256)S(1)} %add_rsqrt_fusion, bf16[63,1536]{1,0:T(8,128)(2,1)S(1)} %get-tuple-element.15, bf16[193,1536]{1,0:T(8,128)(2,1)S(1)} %slice.25), kind=kOutput, calls=%fused_computation.4 | convolution fusion | flops 1211105280 | bytes 6298624 | tf_op jit(solution)/shard_map/dot_general | solution.py:24
  71.7 13.3 %all-to-all-done.1.pieces_hbm = bf16[16,56,8,128]{3,2,1,0:T(8,128)(2,1)} async-done(((bf16[16,56,8,128]{3,2,1,0:T(8,128)(2,1)}), bf16[16,56,8,128]{3,2,1,0:T(8,128)(2,1)}, u32[]{:S(2)}, u32[]{:S(2)}) %all-to-all-start.1) | async-done | bytes 1835040 | tf_op jit(solution)/shard_map/all_to_all | solution.py:501
  85.0 34.4 %spans.1 = (bf16[1024,896]{1,0:T(8,128)(2,1)}, bf16[1536,1024]{1,0:T(8,128)(2,1)}, bf16[1536,896]{1,0:T(8,128)(2,1)}, bf16[256,1536]{1,0:T(8,128)(2,1)}) custom-call(s32[4]{0:T(128)} %counts_ref.1, s32[1]{0:T(128)} %bitcast.2.theirs_ref, bf16[16,56,8,128]{3,2,1,0:T(8,128)(2,1)} %all-to-all-done.1.pieces_hbm, f32[896]{0:T(1024)} %gain_ref.1, ...), custom_call_target="tpu_custom_call" | custom-call | flops 15032385536 | bytes 20971520 | tf_op jit(solution)/shard_map/spans/pallas_call | solution.py:402
  119.3 5.5 %collective-permute-start.2 = (bf16[1536,896]{1,0:T(8,128)(2,1)}, bf16[1536,896]{1,0:T(8,128)(2,1)S(1)}, u32[]{:S(2)}, u32[]{:S(2)}) collective-permute-start(bf16[1536,896]{1,0:T(8,128)(2,1)} %get-tuple-element.13), channel_id=1, source_target_pairs={{0,16},{16,0},{32,48},{48,32},{64,80},{80,64},{96,112},{112,96},{1... | collective-permute-start | bytes 8257544 | tf_op jit(solution)/shard_map/ppermute | solution.py:555
  124.8 1.9 copy-done
  126.7 1.5 copy-done.1
  128.2 3.8 %weight_half.1 = bf16[1536,896]{1,0:T(8,128)(2,1)S(1)} custom-call(bf16[1536,1024]{1,0:T(8,128)(2,1)S(1)} %copy-done, bf16[1024,896]{1,0:T(8,128)(2,1)S(1)} %copy-done.1), custom_call_target="tpu_custom_call" | custom-call | flops 2818572288 | bytes 8388608 | tf_op jit(solution)/shard_map/weight_half/pallas_call | solution.py:465
  132.0 0.0 collective-permute-done.2
  132.0 2.3 %add_convert_fusion = bf16[1536,896]{1,0:T(8,128)(2,1)} fusion(bf16[1536,896]{1,0:T(8,128)(2,1)S(1)} %collective-permute-done.2, bf16[1536,896]{1,0:T(8,128)(2,1)S(1)} %weight_half.1), kind=kLoop, calls=%fused_computation | loop fusion | flops 5505024 | bytes 8257536 | tf_op jit(solution)/shard_map/convert_element_type | solution.py:557
  134.3 6.8 %all-to-all-start.2 = ((bf16[64,24,896]{2,1,0:T(8,128)(2,1)}), bf16[64,24,896]{2,1,0:T(8,128)(2,1)S(1)}, u32[]{:S(2)}, u32[]{:S(2)}) async-start(bf16[64,24,896]{2,1,0:T(8,128)(2,1)} %bitcast.15), calls=%async_computation.2 | async-start | bytes 5505024 | tf_op jit(solution)/shard_map/all_to_all | solution.py:501
  141.1 4.1 %fusion = bf16[256,1536]{1,0:T(8,128)(2,1)S(1)} fusion(bf16[256,1536]{1,0:T(8,128)(2,1)} %get-tuple-element.10, bf16[1536,1536]{1,0:T(8,128)(2,1)} %param.24, bf16[63,1536]{1,0:T(8,128)(2,1)} %copy-done.7, bf16[193,1536]{1,0:T(8,128)(2,1)} %copy-done.5), kind=kOutput, calls=%fused_computation.2 | convolution fusion | flops 1210318848 | bytes 7077888 | tf_op jit(solution)/shard_map/dot_general | solution.py:24
  145.2 0.0 copy-start.6
  145.2 0.9 copy-done.6
  146.1 0.7 slice.35
  146.8 3.6 %collective-permute-start.1 = (bf16[63,1536]{1,0:T(8,128)(2,1)}, bf16[63,1536]{1,0:T(8,128)(2,1)}, u32[]{:S(2)}, u32[]{:S(2)}) collective-permute-start(bf16[63,1536]{1,0:T(8,128)(2,1)} %slice.35), channel_id=1, source_target_pairs={{0,1},{1,2},{2,3},{3,4},{4,5},{5,6},{6,7},{7,8},{8,9},{9,10},{10,1... | collective-permute-start | bytes 580616 | tf_op jit(solution)/shard_map/ppermute | solution.py:569
  150.4 1.9 %slice.36 = bf16[193,1536]{1,0:T(8,128)(2,1)} slice(bf16[256,1536]{1,0:T(8,128)(2,1)} %copy-done.6), slice={[0:193], [0:1536]} | slice | bytes 1185792 | tf_op jit(solution)/shard_map/slice | solution.py:571
  152.4 25.0 %all-to-all-done.2.terms_ref = bf16[64,24,896]{2,1,0:T(8,128)(2,1)S(1)} async-done(((bf16[64,24,896]{2,1,0:T(8,128)(2,1)}), bf16[64,24,896]{2,1,0:T(8,128)(2,1)S(1)}, u32[]{:S(2)}, u32[]{:S(2)}) %all-to-all-start.2) | async-done | bytes 2752544 | tf_op jit(solution)/shard_map/all_to_all | solution.py:501
  177.4 1.1 total.1
  178.5 4.7 %all-to-all-start.3 = ((bf16[8,24,896]{2,1,0:T(8,128)(2,1)}), bf16[8,24,896]{2,1,0:T(8,128)(2,1)S(1)}, u32[]{:S(2)}, u32[]{:S(2)}) async-start(bf16[8,24,896]{2,1,0:T(8,128)(2,1)} %total.1), calls=%async_computation.3 | async-start | bytes 688128 | tf_op jit(solution)/shard_map/all_to_all | solution.py:501
  183.2 0.0 collective-permute-done.1
  183.2 2.1 %pad_maximum_fusion.1 = bf16[256,1536]{1,0:T(8,128)(2,1)} fusion(bf16[193,1536]{1,0:T(8,128)(2,1)} %slice.36, bf16[63,1536]{1,0:T(8,128)(2,1)S(1)} %slice_select_fusion), kind=kLoop, calls=%fused_computation.14 | loop fusion | flops 1572864 | bytes 1572864 | tf_op jit(solution)/shard_map/concatenate | solution.py:571
  185.3 5.1 %all-to-all-done.3 = bf16[8,24,896]{2,1,0:T(8,128)(2,1)S(1)} async-done(((bf16[8,24,896]{2,1,0:T(8,128)(2,1)}), bf16[8,24,896]{2,1,0:T(8,128)(2,1)S(1)}, u32[]{:S(2)}, u32[]{:S(2)}) %all-to-all-start.3) | async-done | bytes 344096 | tf_op jit(solution)/shard_map/all_to_all | solution.py:501
  190.4 0.9 bitcast_convert_fusion
  (10 shorter events, 0.0 us)
Async XLA Ops:
  5.8 45.1 %all-to-all-start = ((bf16[16,85,8,128]{3,2,1,0:T(8,128)(2,1)}), bf16[16,85,8,128]{3,2,1,0:T(8,128)(2,1)S(1)}, u32[]{:S(2)}, u32[]{:S(2)}) async-start(bf16[16,85,8,128]{3,2,1,0:T(8,128)(2,1)} %get-tuple-element.9), calls=%async_computation | async-start | bytes 5570560 | tf_op jit(solution)/shard_map/all_to_all | solution.py:501
  14.4 48.6 %collective-permute-start = (bf16[2,64,1536]{2,1,0:T(8,128)(2,1)}, bf16[2,64,1536]{2,1,0:T(8,128)(2,1)}, u32[]{:S(2)}, u32[]{:S(2)}) collective-permute-start(bf16[2,64,1536]{2,1,0:T(8,128)(2,1)} %get-tuple-element.8), channel_id=1, source_target_pairs={{1,0},{2,1},{3,2},{4,3},{5,4},{6,5},{7,6},{8,7},{9,8},{10,9},{11,1... | collective-permute-start | bytes 1179656 | tf_op jit(solution)/shard_map/ppermute | solution.py:530
  50.9 1.5 copy-start.2
  56.1 6.6 %copy-start.3 = (bf16[256,1536]{1,0:T(8,128)(2,1)S(1)}, bf16[256,1536]{1,0:T(8,128)(2,1)}, u32[]{:S(2)}) copy-start(bf16[256,1536]{1,0:T(8,128)(2,1)} %hidden_hbm.1) | copy-start | bytes 2359300
  56.1 6.7 %copy-start.4 = (bf16[256,1536]{1,0:T(8,128)(2,1)S(1)}, bf16[256,1536]{1,0:T(8,128)(2,1)}, u32[]{:S(2)}) copy-start(bf16[256,1536]{1,0:T(8,128)(2,1)} %cotangent_hbm.1) | copy-start | bytes 2359300
  56.2 28.8 %all-to-all-start.1 = ((bf16[16,56,8,128]{3,2,1,0:T(8,128)(2,1)}), bf16[16,56,8,128]{3,2,1,0:T(8,128)(2,1)}, u32[]{:S(2)}, u32[]{:S(2)}) async-start(bf16[16,56,8,128]{3,2,1,0:T(8,128)(2,1)} %pick.1), calls=%async_computation.1 | async-start | bytes 3670016 | tf_op jit(solution)/shard_map/all_to_all | solution.py:501
  62.9 6.5 %copy-start.5 = (bf16[193,1536]{1,0:T(8,128)(2,1)}, bf16[193,1536]{1,0:T(8,128)(2,1)S(1)}, u32[]{:S(2)}) copy-start(bf16[193,1536]{1,0:T(8,128)(2,1)S(1)} %slice.25) | copy-start | bytes 1778692
  64.2 5.2 %copy-start.7 = (bf16[63,1536]{1,0:T(8,128)(2,1)}, bf16[63,1536]{1,0:T(8,128)(2,1)S(1)}, u32[]{:S(2)}) copy-start(bf16[63,1536]{1,0:T(8,128)(2,1)S(1)} %get-tuple-element.15) | copy-start | bytes 580612
  64.2 5.2 %slice-start = ((s8[4718592]{0:T(1024)(128)(4,1)}), s8[4194304]{0:T(1024)(128)(4,1)S(1)}, s32[]{:S(2)}) async-start(s8[4718592]{0:T(1024)(128)(4,1)} %bitcast.18), calls=%async_computation.4 | async-start | bytes 8388608
  64.5 4.9 %slice-start.1 = ((s8[4718592]{0:T(1024)(128)(4,1)}), s8[524288]{0:T(1024)(128)(4,1)S(1)}, s32[]{:S(2)}) async-start(s8[4718592]{0:T(1024)(128)(4,1)} %bitcast.18), calls=%async_computation.5 | async-start | bytes 1048576
  64.5 4.9 %copy-start.8 = (f32[1536]{0:T(1024)S(1)}, f32[1536]{0:T(1024)}, u32[]{:S(2)}) copy-start(f32[1536]{0:T(1024)} %param.21) | copy-start | bytes 18436
  119.3 12.7 %collective-permute-start.2 = (bf16[1536,896]{1,0:T(8,128)(2,1)}, bf16[1536,896]{1,0:T(8,128)(2,1)S(1)}, u32[]{:S(2)}, u32[]{:S(2)}) collective-permute-start(bf16[1536,896]{1,0:T(8,128)(2,1)} %get-tuple-element.13), channel_id=1, source_target_pairs={{0,16},{16,0},{32,48},{48,32},{64,80},{80,64},{96,112},{112,96},{1... | collective-permute-start | bytes 8257544 | tf_op jit(solution)/shard_map/ppermute | solution.py:555
  124.8 1.9 copy-start
  126.7 1.5 copy-start.1
  134.3 43.1 %all-to-all-start.2 = ((bf16[64,24,896]{2,1,0:T(8,128)(2,1)}), bf16[64,24,896]{2,1,0:T(8,128)(2,1)S(1)}, u32[]{:S(2)}, u32[]{:S(2)}) async-start(bf16[64,24,896]{2,1,0:T(8,128)(2,1)} %bitcast.15), calls=%async_computation.2 | async-start | bytes 5505024 | tf_op jit(solution)/shard_map/all_to_all | solution.py:501
  145.2 0.9 copy-start.6
  146.8 36.4 %collective-permute-start.1 = (bf16[63,1536]{1,0:T(8,128)(2,1)}, bf16[63,1536]{1,0:T(8,128)(2,1)}, u32[]{:S(2)}, u32[]{:S(2)}) collective-permute-start(bf16[63,1536]{1,0:T(8,128)(2,1)} %slice.35), channel_id=1, source_target_pairs={{0,1},{1,2},{2,3},{3,4},{4,5},{5,6},{6,7},{7,8},{8,9},{9,10},{10,1... | collective-permute-start | bytes 580616 | tf_op jit(solution)/shard_map/ppermute | solution.py:569
  178.5 11.9 %all-to-all-start.3 = ((bf16[8,24,896]{2,1,0:T(8,128)(2,1)}), bf16[8,24,896]{2,1,0:T(8,128)(2,1)S(1)}, u32[]{:S(2)}, u32[]{:S(2)}) async-start(bf16[8,24,896]{2,1,0:T(8,128)(2,1)} %total.1), calls=%async_computation.3 | async-start | bytes 688128 | tf_op jit(solution)/shard_map/all_to_all | solution.py:501

commit v5 on v4

--- a/solution.py
+++ b/solution.py
@@ -133,7 +133,18 @@
     )(block_home, neighbours, database, hidden, cotangent)
 
 
-def pick_kernel(tiles, where_ref, table_ref, out_hbm, out_ref, sems):
+def pick_kernel(
+    tiles,
+    table_hbm,
+    out_hbm,
+    table_ref,
+    notes_ref,
+    found_ref,
+    where_ref,
+    out_ref,
+    sems,
+    in_sems,
+):
     blocks = table_ref.shape[1] // tiles
     parts = sems.shape[0]
     size = out_ref.shape[0] // parts
@@ -142,6 +153,18 @@
         readers = pl.ds(part * size, size)
         return pltpu.make_async_copy(out_ref.at[readers], out_hbm.at[readers], sems.at[part])
 
+    notes_load = pltpu.make_async_copy(
+        table_hbm.at[:, table_ref.shape[1] - 1], notes_ref, in_sems.at[0]
+    )
+    table_load = pltpu.make_async_copy(table_hbm, table_ref, in_sems.at[1])
+    notes_load.start()
+    table_load.start()
+    notes_load.wait()
+    found_ref[...] = jnp.max(notes_ref[...].astype(F32), axis=1).astype(jnp.int32)
+    where_load = pltpu.make_async_copy(found_ref, where_ref, in_sems.at[2])
+    where_load.start()
+    where_load.wait()
+    table_load.wait()
     for part in range(parts):
 
         @pl.loop(part * size, (part + 1) * size)
@@ -158,20 +181,27 @@
         store(part).wait()
 
 
-def pick(where, table, tiles):
-    readers, requests = where.shape
-    rows, width = table.shape[2:]
+def pick(table, requests, tiles):
+    readers, _, rows, width = table.shape
     shape = (readers, requests * tiles, rows, width)
-    whole = pl.BlockSpec(memory_space=VMEM)
+    hbm = pl.BlockSpec(memory_space=pltpu.HBM)
     return pl.pallas_call(
         functools.partial(pick_kernel, tiles),
         out_shape=jax.ShapeDtypeStruct(shape, BF16),
-        in_specs=[pl.BlockSpec(memory_space=pltpu.SMEM), whole],
-        out_specs=pl.BlockSpec(memory_space=pltpu.HBM),
-        scratch_shapes=[VMEM(shape, BF16), pltpu.SemaphoreType.DMA((4,))],
+        in_specs=[hbm],
+        out_specs=hbm,
+        scratch_shapes=[
+            VMEM(table.shape, BF16),
+            VMEM((readers, rows, width), BF16),
+            VMEM((readers, width), jnp.int32),
+            pltpu.SMEM((readers, width), jnp.int32),
+            VMEM(shape, BF16),
+            pltpu.SemaphoreType.DMA((4,)),
+            pltpu.SemaphoreType.DMA((3,)),
+        ],
         compiler_params=pltpu.CompilerParams(vmem_limit_bytes=60 << 20),
         name="pick",
-    )(where, table)
+    )(table)
 
 
 def span_kernel(
@@ -530,7 +560,6 @@
     late = lax.ppermute(tails, "seq", [(i, i - 1) for i in range(1, seq)])
     late_hidden, late_cotangent = late[0, :tail], late[1, :tail]
     table = all_to_all(slices, "seq")
-    readers_where = table[:, -1, 0, :requests].astype(jnp.int32)
 
     own_hidden = jnp.concatenate([hidden[tail:], late_hidden], axis=0)
     own_cotangent = jnp.concatenate([cotangent[tail:], late_cotangent], axis=0)
@@ -538,7 +567,7 @@
     queries = dot(normed, cross_query, NN).astype(BF16)
     grads = dot(own_cotangent, cross_output, NT).astype(BF16)
 
-    picked = pick(readers_where, table, tiles)
+    picked = pick(table, requests, tiles)
     pieces = all_to_all(picked, "seq")
     core = lax.axis_index("dp") % 2
     encoded, own, theirs, attended = span_step(

time: 192 us -> 192 us (level)
  transfers between devices with their start and end apart: 7 -> 7, of which waited for: 4 -> 4; matrix products, arithmetic and copies ran while one was open for 10% -> 9% of each run, Pallas kernels for 4% -> 4%
where the time goes in v5:
time: 192 us; the launch traced here: 191 us
  waiting for transfers between devices  78.6 us (41%)
  Pallas kernels  46.8 us (24%)
  starting transfers between devices  37 us (19%)
  matrix products  11.3 us (6%)
  local copies, waits for them, and re-layouts  11.2 us (6%)
  other arithmetic  5.6 us (3%)
    all_to_all x4, waiting for transfers between devices, all_to_all(): lax.all_to_all(block, axis, split_axis=0, concat_axis=0, tiled=True, axis...  78.6 us
    pallas_call x1, Pallas kernels, span_step(): pl.pallas_call(span_kernel, out_shape=(jax.ShapeDtypeStruct((total, featu...  34.4 us
    all_to_all x4, starting transfers between devices, all_to_all(): lax.all_to_all(block, axis, split_axis=0, concat_axis=0, tiled=True, axis...  26.6 us
    dot_general x3, matrix products, dot(): return lax.dot_general(a, b, dims, preferred_element_type=F32)  11.3 us
    unnamed x23, local copies, waits for them, and re-layouts  7.19 us
    ppermute x1, starting transfers between devices, local(): received = lax.ppermute(theirs, 'dp', [(i, i ^ 1) for i in range(dp)])  5.49 us
    pallas_call x1, Pallas kernels, spread(): pl.pallas_call(spread_kernel, out_shape=(jax.ShapeDtypeStruct((devices, u...  3.85 us
  transfers between devices with their start and end apart: 7, of which 4 were waited for; matrix products, arithmetic and copies ran while one was open for 9% of the time, Pallas kernels for 4%

profile of v5, /device:TPU:1, one launch (start us, length us, event | category | flops | bytes accessed | tf_op | source)
XLA Modules:
  0.0 191.4 jit_solution(7161750106889097699)
XLA Ops:
  0.6 1.3 copy.15.neighbours_ref
  2.0 3.9 %spread.1 = (bf16[16,85,8,128]{3,2,1,0:T(8,128)(2,1)}, bf16[2,64,1536]{2,1,0:T(8,128)(2,1)}) custom-call(s32[192]{0:T(256)} %home_ref.1, s32[4,2]{1,0:T(4,128)} %copy.15.neighbours_ref, bf16[12,128,896]{2,1,0:T(8,128)(2,1)} %bitcast.15, bf16[256,1536]{1,0:T(8,128)(2,1)} %hidden_hbm.1, bf16[256,1536]{1,0:T(8,128)(2,1)} %cotangent_hbm.1), custom_call_target="tpu_custom_call" | custom-call | flops 1048576 | bytes 6291456 | tf_op jit(solution)/shard_map/spread/pallas_call | solution.py:114
  5.8 8.6 %all-to-all-start = ((bf16[16,85,8,128]{3,2,1,0:T(8,128)(2,1)}), bf16[16,85,8,128]{3,2,1,0:T(8,128)(2,1)S(1)}, u32[]{:S(2)}, u32[]{:S(2)}) async-start(bf16[16,85,8,128]{3,2,1,0:T(8,128)(2,1)} %get-tuple-element.9), calls=%async_computation | async-start | bytes 5570560 | tf_op jit(solution)/shard_map/all_to_all | solution.py:531
  14.4 1.3 collective-permute-start
  15.7 35.2 %all-to-all-done.table_hbm = bf16[16,85,8,128]{3,2,1,0:T(8,128)(2,1)S(1)} async-done(((bf16[16,85,8,128]{3,2,1,0:T(8,128)(2,1)}), bf16[16,85,8,128]{3,2,1,0:T(8,128)(2,1)S(1)}, u32[]{:S(2)}, u32[]{:S(2)}) %all-to-all-start) | async-done | bytes 2785312 | tf_op jit(solution)/shard_map/all_to_all | solution.py:531
  50.9 1.5 copy-done.2
  52.5 3.7 %pick.1 = bf16[16,56,8,128]{3,2,1,0:T(8,128)(2,1)} custom-call(bf16[16,85,8,128]{3,2,1,0:T(8,128)(2,1)} %copy-done.2), custom_call_target="tpu_custom_call" | custom-call | tf_op jit(solution)/shard_map/pick/pallas_call | solution.py:188
  56.2 0.0 copy-start.3
  56.2 0.0 copy-start.4
  56.2 6.5 %all-to-all-start.1 = ((bf16[16,56,8,128]{3,2,1,0:T(8,128)(2,1)}), bf16[16,56,8,128]{3,2,1,0:T(8,128)(2,1)}, u32[]{:S(2)}, u32[]{:S(2)}) async-start(bf16[16,56,8,128]{3,2,1,0:T(8,128)(2,1)} %pick.1), calls=%async_computation.1 | async-start | bytes 3670016 | tf_op jit(solution)/shard_map/all_to_all | solution.py:531
  62.8 0.0 copy-done.3
  62.8 0.1 slice.22
  62.9 0.0 copy-done.4
  62.9 0.0 copy-start.5
  62.9 0.1 slice.24
  63.1 0.0 collective-permute-done
  63.1 1.1 slice_bitcast_fusion
  64.2 0.0 copy-start.7
  64.2 0.0 slice-start
  64.2 0.3 fusion.1
  64.5 0.0 slice-start.1
  64.5 0.0 copy-start.8
  64.5 4.9 %convolution_convert_fusion.grads_hbm = bf16[256,1536]{1,0:T(8,128)(2,1)} fusion(bf16[1536,1536]{1,0:T(8,128)(2,1)} %param.24, bf16[63,1536]{1,0:T(8,128)(2,1)S(1)} %get-tuple-element.14, bf16[193,1536]{1,0:T(8,128)(2,1)S(1)} %slice.24), kind=kOutput, calls=%fused_computation.3 | convolution fusion | flops 1209925632 | bytes 6291456 | tf_op jit(solution)/shard_map/dot_general | solution.py:24
  69.4 0.0 copy-done.5
  69.4 0.0 slice-done
  69.4 2.3 %convolution_convert_fusion.1.queries_hbm = bf16[256,1536]{1,0:T(8,128)(2,1)} fusion(bf16[1536,1536]{1,0:T(8,128)(2,1)S(1)} %bitcast.17, f32[1536]{0:T(1024)S(1)} %copy-done.8, f32[256]{0:T(256)S(1)} %add_rsqrt_fusion, bf16[63,1536]{1,0:T(8,128)(2,1)S(1)} %get-tuple-element.15, bf16[193,1536]{1,0:T(8,128)(2,1)S(1)} %slice.22), kind=kOutput, calls=%fused_computation.4 | convolution fusion | flops 1211105280 | bytes 6298624 | tf_op jit(solution)/shard_map/dot_general | solution.py:24
  71.7 13.3 %all-to-all-done.1.pieces_hbm = bf16[16,56,8,128]{3,2,1,0:T(8,128)(2,1)} async-done(((bf16[16,56,8,128]{3,2,1,0:T(8,128)(2,1)}), bf16[16,56,8,128]{3,2,1,0:T(8,128)(2,1)}, u32[]{:S(2)}, u32[]{:S(2)}) %all-to-all-start.1) | async-done | bytes 1835040 | tf_op jit(solution)/shard_map/all_to_all | solution.py:531
  85.0 34.4 %spans.1 = (bf16[1024,896]{1,0:T(8,128)(2,1)}, bf16[1536,1024]{1,0:T(8,128)(2,1)}, bf16[1536,896]{1,0:T(8,128)(2,1)}, bf16[256,1536]{1,0:T(8,128)(2,1)}) custom-call(s32[4]{0:T(128)} %counts_ref.1, s32[1]{0:T(128)} %bitcast.2.theirs_ref, bf16[16,56,8,128]{3,2,1,0:T(8,128)(2,1)} %all-to-all-done.1.pieces_hbm, f32[896]{0:T(1024)} %gain_ref.1, ...), custom_call_target="tpu_custom_call" | custom-call | flops 15032385536 | bytes 20971520 | tf_op jit(solution)/shard_map/spans/pallas_call | solution.py:432
  119.4 5.5 %collective-permute-start.2 = (bf16[1536,896]{1,0:T(8,128)(2,1)}, bf16[1536,896]{1,0:T(8,128)(2,1)S(1)}, u32[]{:S(2)}, u32[]{:S(2)}) collective-permute-start(bf16[1536,896]{1,0:T(8,128)(2,1)} %get-tuple-element.13), channel_id=1, source_target_pairs={{0,16},{16,0},{32,48},{48,32},{64,80},{80,64},{96,112},{112,96},{1... | collective-permute-start | bytes 8257544 | tf_op jit(solution)/shard_map/ppermute | solution.py:584
  124.9 1.9 copy-done
  126.8 1.5 copy-done.1
  128.3 3.8 %weight_half.1 = bf16[1536,896]{1,0:T(8,128)(2,1)S(1)} custom-call(bf16[1536,1024]{1,0:T(8,128)(2,1)S(1)} %copy-done, bf16[1024,896]{1,0:T(8,128)(2,1)S(1)} %copy-done.1), custom_call_target="tpu_custom_call" | custom-call | flops 2818572288 | bytes 8388608 | tf_op jit(solution)/shard_map/weight_half/pallas_call | solution.py:495
  132.1 0.0 collective-permute-done.2
  132.1 2.3 %add_convert_fusion = bf16[1536,896]{1,0:T(8,128)(2,1)} fusion(bf16[1536,896]{1,0:T(8,128)(2,1)S(1)} %collective-permute-done.2, bf16[1536,896]{1,0:T(8,128)(2,1)S(1)} %weight_half.1), kind=kLoop, calls=%fused_computation | loop fusion | flops 5505024 | bytes 8257536 | tf_op jit(solution)/shard_map/convert_element_type | solution.py:586
  134.3 6.7 %all-to-all-start.2 = ((bf16[64,24,896]{2,1,0:T(8,128)(2,1)}), bf16[64,24,896]{2,1,0:T(8,128)(2,1)S(1)}, u32[]{:S(2)}, u32[]{:S(2)}) async-start(bf16[64,24,896]{2,1,0:T(8,128)(2,1)} %bitcast.14), calls=%async_computation.2 | async-start | bytes 5505024 | tf_op jit(solution)/shard_map/all_to_all | solution.py:531
  141.1 4.1 %fusion = bf16[256,1536]{1,0:T(8,128)(2,1)S(1)} fusion(bf16[256,1536]{1,0:T(8,128)(2,1)} %get-tuple-element.10, bf16[1536,1536]{1,0:T(8,128)(2,1)} %param.24, bf16[63,1536]{1,0:T(8,128)(2,1)} %copy-done.7, bf16[193,1536]{1,0:T(8,128)(2,1)} %copy-done.5), kind=kOutput, calls=%fused_computation.2 | convolution fusion | flops 1210318848 | bytes 7077888 | tf_op jit(solution)/shard_map/dot_general | solution.py:24
  145.2 0.0 copy-start.6
  145.3 0.9 copy-done.6
  146.1 0.7 slice.30
  146.9 3.6 %collective-permute-start.1 = (bf16[63,1536]{1,0:T(8,128)(2,1)}, bf16[63,1536]{1,0:T(8,128)(2,1)}, u32[]{:S(2)}, u32[]{:S(2)}) collective-permute-start(bf16[63,1536]{1,0:T(8,128)(2,1)} %slice.30), channel_id=1, source_target_pairs={{0,1},{1,2},{2,3},{3,4},{4,5},{5,6},{6,7},{7,8},{8,9},{9,10},{10,1... | collective-permute-start | bytes 580616 | tf_op jit(solution)/shard_map/ppermute | solution.py:598
  150.5 1.9 %slice.31 = bf16[193,1536]{1,0:T(8,128)(2,1)} slice(bf16[256,1536]{1,0:T(8,128)(2,1)} %copy-done.6), slice={[0:193], [0:1536]} | slice | bytes 1185792 | tf_op jit(solution)/shard_map/slice | solution.py:600
  152.4 25.0 %all-to-all-done.2.terms_ref = bf16[64,24,896]{2,1,0:T(8,128)(2,1)S(1)} async-done(((bf16[64,24,896]{2,1,0:T(8,128)(2,1)}), bf16[64,24,896]{2,1,0:T(8,128)(2,1)S(1)}, u32[]{:S(2)}, u32[]{:S(2)}) %all-to-all-start.2) | async-done | bytes 2752544 | tf_op jit(solution)/shard_map/all_to_all | solution.py:531
  177.4 1.1 total.1
  178.5 4.7 %all-to-all-start.3 = ((bf16[8,24,896]{2,1,0:T(8,128)(2,1)}), bf16[8,24,896]{2,1,0:T(8,128)(2,1)S(1)}, u32[]{:S(2)}, u32[]{:S(2)}) async-start(bf16[8,24,896]{2,1,0:T(8,128)(2,1)} %total.1), calls=%async_computation.3 | async-start | bytes 688128 | tf_op jit(solution)/shard_map/all_to_all | solution.py:531
  183.2 0.0 collective-permute-done.1
  183.3 2.1 %pad_maximum_fusion.1 = bf16[256,1536]{1,0:T(8,128)(2,1)} fusion(bf16[193,1536]{1,0:T(8,128)(2,1)} %slice.31, bf16[63,1536]{1,0:T(8,128)(2,1)S(1)} %slice_select_fusion), kind=kLoop, calls=%fused_computation.14 | loop fusion | flops 1572864 | bytes 1572864 | tf_op jit(solution)/shard_map/concatenate | solution.py:600
  185.4 5.1 %all-to-all-done.3 = bf16[8,24,896]{2,1,0:T(8,128)(2,1)S(1)} async-done(((bf16[8,24,896]{2,1,0:T(8,128)(2,1)}), bf16[8,24,896]{2,1,0:T(8,128)(2,1)S(1)}, u32[]{:S(2)}, u32[]{:S(2)}) %all-to-all-start.3) | async-done | bytes 344096 | tf_op jit(solution)/shard_map/all_to_all | solution.py:531
  190.5 0.9 bitcast_convert_fusion
  (9 shorter events, 0.0 us)
Async XLA Ops:
  5.8 45.1 %all-to-all-start = ((bf16[16,85,8,128]{3,2,1,0:T(8,128)(2,1)}), bf16[16,85,8,128]{3,2,1,0:T(8,128)(2,1)S(1)}, u32[]{:S(2)}, u32[]{:S(2)}) async-start(bf16[16,85,8,128]{3,2,1,0:T(8,128)(2,1)} %get-tuple-element.9), calls=%async_computation | async-start | bytes 5570560 | tf_op jit(solution)/shard_map/all_to_all | solution.py:531
  14.4 48.7 %collective-permute-start = (bf16[2,64,1536]{2,1,0:T(8,128)(2,1)}, bf16[2,64,1536]{2,1,0:T(8,128)(2,1)}, u32[]{:S(2)}, u32[]{:S(2)}) collective-permute-start(bf16[2,64,1536]{2,1,0:T(8,128)(2,1)} %get-tuple-element.8), channel_id=1, source_target_pairs={{1,0},{2,1},{3,2},{4,3},{5,4},{6,5},{7,6},{8,7},{9,8},{10,9},{11,1... | collective-permute-start | bytes 1179656 | tf_op jit(solution)/shard_map/ppermute | solution.py:560
  50.9 1.5 copy-start.2
  56.2 6.6 %copy-start.3 = (bf16[256,1536]{1,0:T(8,128)(2,1)S(1)}, bf16[256,1536]{1,0:T(8,128)(2,1)}, u32[]{:S(2)}) copy-start(bf16[256,1536]{1,0:T(8,128)(2,1)} %hidden_hbm.1) | copy-start | bytes 2359300
  56.2 6.7 %copy-start.4 = (bf16[256,1536]{1,0:T(8,128)(2,1)S(1)}, bf16[256,1536]{1,0:T(8,128)(2,1)}, u32[]{:S(2)}) copy-start(bf16[256,1536]{1,0:T(8,128)(2,1)} %cotangent_hbm.1) | copy-start | bytes 2359300
  56.2 28.8 %all-to-all-start.1 = ((bf16[16,56,8,128]{3,2,1,0:T(8,128)(2,1)}), bf16[16,56,8,128]{3,2,1,0:T(8,128)(2,1)}, u32[]{:S(2)}, u32[]{:S(2)}) async-start(bf16[16,56,8,128]{3,2,1,0:T(8,128)(2,1)} %pick.1), calls=%async_computation.1 | async-start | bytes 3670016 | tf_op jit(solution)/shard_map/all_to_all | solution.py:531
  62.9 6.5 %copy-start.5 = (bf16[193,1536]{1,0:T(8,128)(2,1)}, bf16[193,1536]{1,0:T(8,128)(2,1)S(1)}, u32[]{:S(2)}) copy-start(bf16[193,1536]{1,0:T(8,128)(2,1)S(1)} %slice.22) | copy-start | bytes 1778692
  64.2 5.2 %copy-start.7 = (bf16[63,1536]{1,0:T(8,128)(2,1)}, bf16[63,1536]{1,0:T(8,128)(2,1)S(1)}, u32[]{:S(2)}) copy-start(bf16[63,1536]{1,0:T(8,128)(2,1)S(1)} %get-tuple-element.15) | copy-start | bytes 580612
  64.2 5.2 %slice-start = ((s8[4718592]{0:T(1024)(128)(4,1)}), s8[4194304]{0:T(1024)(128)(4,1)S(1)}, s32[]{:S(2)}) async-start(s8[4718592]{0:T(1024)(128)(4,1)} %bitcast.16), calls=%async_computation.4 | async-start | bytes 8388608
  64.5 4.9 %slice-start.1 = ((s8[4718592]{0:T(1024)(128)(4,1)}), s8[524288]{0:T(1024)(128)(4,1)S(1)}, s32[]{:S(2)}) async-start(s8[4718592]{0:T(1024)(128)(4,1)} %bitcast.16), calls=%async_computation.5 | async-start | bytes 1048576
  64.5 4.9 %copy-start.8 = (f32[1536]{0:T(1024)S(1)}, f32[1536]{0:T(1024)}, u32[]{:S(2)}) copy-start(f32[1536]{0:T(1024)} %param.21) | copy-start | bytes 18436
  119.4 12.7 %collective-permute-start.2 = (bf16[1536,896]{1,0:T(8,128)(2,1)}, bf16[1536,896]{1,0:T(8,128)(2,1)S(1)}, u32[]{:S(2)}, u32[]{:S(2)}) collective-permute-start(bf16[1536,896]{1,0:T(8,128)(2,1)} %get-tuple-element.13), channel_id=1, source_target_pairs={{0,16},{16,0},{32,48},{48,32},{64,80},{80,64},{96,112},{112,96},{1... | collective-permute-start | bytes 8257544 | tf_op jit(solution)/shard_map/ppermute | solution.py:584
  124.9 1.9 copy-start
  126.8 1.5 copy-start.1
  134.3 43.1 %all-to-all-start.2 = ((bf16[64,24,896]{2,1,0:T(8,128)(2,1)}), bf16[64,24,896]{2,1,0:T(8,128)(2,1)S(1)}, u32[]{:S(2)}, u32[]{:S(2)}) async-start(bf16[64,24,896]{2,1,0:T(8,128)(2,1)} %bitcast.14), calls=%async_computation.2 | async-start | bytes 5505024 | tf_op jit(solution)/shard_map/all_to_all | solution.py:531
  145.2 0.9 copy-start.6
  146.9 36.4 %collective-permute-start.1 = (bf16[63,1536]{1,0:T(8,128)(2,1)}, bf16[63,1536]{1,0:T(8,128)(2,1)}, u32[]{:S(2)}, u32[]{:S(2)}) collective-permute-start(bf16[63,1536]{1,0:T(8,128)(2,1)} %slice.30), channel_id=1, source_target_pairs={{0,1},{1,2},{2,3},{3,4},{4,5},{5,6},{6,7},{7,8},{8,9},{9,10},{10,1... | collective-permute-start | bytes 580616 | tf_op jit(solution)/shard_map/ppermute | solution.py:598
  178.5 11.9 %all-to-all-start.3 = ((bf16[8,24,896]{2,1,0:T(8,128)(2,1)}), bf16[8,24,896]{2,1,0:T(8,128)(2,1)S(1)}, u32[]{:S(2)}, u32[]{:S(2)}) async-start(bf16[8,24,896]{2,1,0:T(8,128)(2,1)} %total.1), calls=%async_computation.3 | async-start | bytes 688128 | tf_op jit(solution)/shard_map/all_to_all | solution.py:531
